TPU v7x, 128 devices: a whole 4x4x4 slice. The times are simulated.
128 devices in a mesh: days: 8 (over x, y_hi), assets: 16 (over z, y_lo, core).
Axes of the slice: x: 4, y: 4 (y_hi: 2, y_lo: 2; y = y_hi * 2 + y_lo), z: 4, core: 2. Of those that a mesh axis runs over, the one named last changes fastest.
Arguments:
- factors: bfloat16 [1536, 256], P('days'), may hold values from -6 to 6
- returns: bfloat16 [1536, 16384], P('days', 'assets'), may hold values from -6 to 6
Outputs:
- loadings: float32 [256, 16384], P(None, 'assets')
- covariance: float32 [16384, 16384], P('assets', 'days')
All inputs are finite; a program needn't handle non-finite values.
Results may differ from a plain program's by a relative error of at most 0.0036.
Values may be sent and summed in bfloat16 or wider, within the bound.
A program may use at most 64 MiB of HBM per device.

v0:
```python
import jax
import jax.numpy as jnp
from jax import lax
from jax.sharding import PartitionSpec as P


def in_one(arrays, axis):
    ends = [0]
    for a in arrays:
        ends.append(ends[-1] + a.size)
    total = lax.psum(jnp.concatenate([a.ravel() for a in arrays]), axis)
    return tuple((total[b:e].reshape(a.shape) for a, b, e in zip(arrays, ends, ends[1:])))


def per_device(factors, returns):
    gram = lax.dot_general(
        factors, factors, (((0,), (0,)), ((), ())), preferred_element_type=jnp.float32
    )
    cross = lax.dot_general(
        factors, returns, (((0,), (0,)), ((), ())), preferred_element_type=jnp.float32
    )
    gram, cross = in_one((gram, cross), "days")
    lower = jnp.linalg.cholesky(gram)
    middle = lax.linalg.triangular_solve(lower, cross, left_side=True, lower=True)
    loadings = lax.linalg.triangular_solve(
        lower, middle, left_side=True, lower=True, transpose_a=True
    )
    fitted = jnp.dot(factors, loadings.astype(jnp.bfloat16), preferred_element_type=jnp.float32)
    residual = (returns.astype(jnp.float32) - fitted).astype(jnp.bfloat16)
    mine = lax.all_gather(residual, "days", axis=0, tiled=True)
    day_block = lax.all_gather(residual, "assets", axis=1, tiled=True)
    columns = lax.all_to_all(day_block, "days", split_axis=1, concat_axis=0, tiled=True)
    covariance = lax.dot_general(
        mine, columns, (((0,), (0,)), ((), ())), preferred_element_type=jnp.float32
    )
    covariance = covariance / mine.shape[0]
    return (loadings, covariance)


def solution(mesh):
    in_specs = (P("days", None), P("days", "assets"))
    out_specs = (P(None, "assets"), P("assets", "days"))
    return jax.shard_map(
        per_device, mesh=mesh, in_specs=in_specs, out_specs=out_specs, check_vma=False
    )
```

profile of v0, /device:TPU:5, one launch (start us, length us, event | category | flops | bytes accessed | tf_op | source)
XLA Modules:
  0.0 346.3 jit_solution(16355281017859403252)
XLA Ops:
  7.2 0.8 copy-done
  8.4 1.3 convolution_bitcast_fusion
  10.0 1.1 pad_maximum_fusion
  11.2 87.5 %all-reduce.3.cloned.1.call-done = f32[327680]{0:T(1024)} async-done(((f32[327680]{0:T(1024)}), f32[327680]{0:T(1024)}) %all-reduce.3.cloned.1.call-update) | async-done | bytes 1310736 | tf_op jit(solution)/shard_map/psum | solution.py:11
  98.7 1.0 slice.103
  99.7 1.3 fusion.14
  101.3 11.7 %cholesky.50 = f32[128,128]{1,0:T(8,128)S(1)} custom-call(f32[128,128]{1,0:T(8,128)S(1)} %cholesky.118), custom_call_target="Cholesky" | custom-call | tf_op jit(solution)/shard_map/jit(cholesky)/cholesky | solution.py:23
  113.0 9.8 %custom-call.16 = f32[1,128,128]{1,2,0:T(8,128)S(1)} custom-call(f32[1,128,128]{2,1,0:T(8,128)S(1)} %get-tuple-element.25), custom_call_target="InvertDiagBlocksLowerTriangular" | custom-call | tf_op jit(solution)/shard_map/jit(cholesky)/cholesky | solution.py:23
  123.4 11.7 %cholesky.105 = f32[128,128]{1,0:T(8,128)S(1)} custom-call(f32[128,128]{1,0:T(8,128)S(1)} %convolution_subtract_fusion.2), custom_call_target="Cholesky" | custom-call | tf_op jit(solution)/shard_map/jit(cholesky)/cholesky | solution.py:23
  135.1 0.7 compare_reduce_fusion
  137.3 4.2 %while.1 = (s32[]{:T(128)}, f32[256,256]{1,0:T(8,128)S(1)}, s32[2,2]{1,0:T(2,128)S(1)}, f32[2,128,128]{2,1,0:T(8,128)S(1)}, s32[]{:T(128)}) while((s32[]{:T(128)}, f32[256,256]{1,0:T(8,128)S(1)}, s32[2,2]{1,0:T(2,128)S(1)}, f32[2,128,128]{2,1,0:T(8,128)S(1)}, s32[]{:T(128)}) %tuple.28), condition=%wide.while_cond, body=%wide.while_body.sunk | while | flops 2 | bytes 131189 | solution.py:25
  138.1 1.4 bitcast_dynamic-update-slice_fusion.2
  140.1 1.4 bitcast_dynamic-update-slice_fusion.2
  141.6 19.7 %custom-call.17 = f32[2,128,128]{1,2,0:T(8,128)S(1)} custom-call(f32[2,128,128]{2,1,0:T(8,128)S(1)} %get-tuple-element.9), custom_call_target="InvertDiagBlocksLowerTriangular" | custom-call | tf_op jit(solution)/shard_map/triangular_solve | solution.py:25
  161.3 0.6 fusion.8
  162.5 0.6 fusion.10
  163.8 0.6 convolution_subtract_fusion
  165.1 1.1 fusion.1
  166.3 0.7 all-gather.3.cloned.1.call-update
  166.9 47.5 %all-gather.5.cloned.1.call-done = bf16[192,16384]{1,0:T(8,128)(2,1)} async-done(((bf16[192,1024]{1,0:T(8,128)(2,1)}), bf16[192,16384]{1,0:T(8,128)(2,1)}) %all-gather.5.cloned.1.call-update) | async-done | bytes 6291472 | tf_op jit(solution)/shard_map/all_gather | solution.py:31
  214.5 6.6 %copy.11 = bf16[24,8,8,2048]{3,2,0,1:T(8,128)(2,1)} copy(bf16[24,8,8,2048]{3,2,1,0:T(8,128)(2,1)} %bitcast.64) | data formatting | bytes 12582912 | tf_op jit(solution)/shard_map/all_to_all | solution.py:32
  221.1 6.5 %all-to-all-start = ((bf16[192,8,2048]{2,0,1:T(8,128)(2,1)}), bf16[192,8,2048]{2,0,1:T(8,128)(2,1)}, u32[]{:S(2)}, u32[]{:S(2)}) async-start(bf16[192,8,2048]{2,0,1:T(8,128)(2,1)} %bitcast.63), calls=%async_computation | async-start | bytes 12582912 | tf_op jit(solution)/shard_map/all_to_all | solution.py:32
  227.6 100.4 %all-gather.3.cloned.1.call-done = bf16[1536,1024]{1,0:T(8,128)(2,1)} async-done(((bf16[192,1024]{1,0:T(8,128)(2,1)}), bf16[1536,1024]{1,0:T(8,128)(2,1)}) %all-gather.3.cloned.1.call-update) | async-done | bytes 3145744 | tf_op jit(solution)/shard_map/all_gather | solution.py:30
  327.9 11.8 %convolution_multiply_fusion = f32[1024,2048]{1,0:T(8,128)} fusion(bf16[1536,1024]{1,0:T(8,128)(2,1)} %all-gather.3.cloned.1.call-done, bf16[1536,2048]{1,0:T(8,128)(2,1)} %bitcast.7), kind=kOutput, calls=%fused_computation.3 | convolution fusion | flops 6444548096 | bytes 17825792 | tf_op jit(solution)/shard_map/dot_general | solution.py:33
  (37 shorter events, 4.8 us)
Async XLA Ops:
  7.2 0.9 copy-start
  7.2 91.5 %all-reduce.3.cloned.1.call-start = ((), (), s32[]{:S(2)}) async-start(), calls=%async_computation.1 | async-start | bytes 2621440 | tf_op jit(solution)/shard_map/psum | solution.py:11
  11.1 203.4 %all-gather.5.cloned.1.call-start = ((), (), s32[]{:S(2)}) async-start(), calls=%async_computation.3 | async-start | bytes 6684672 | tf_op jit(solution)/shard_map/all_gather | solution.py:31
  123.1 42.0 %copy-start.2 = (bf16[192,1024]{1,0:T(8,128)(2,1)S(1)}, bf16[192,1024]{1,0:T(8,128)(2,1)}, u32[]{:S(2)}) copy-start(bf16[192,1024]{1,0:T(8,128)(2,1)} %param.3) | copy-start | bytes 1179652
  165.1 56.0 %copy-start.1 = (f32[256,1024]{1,0:T(8,128)}, f32[256,1024]{1,0:T(8,128)S(1)}, u32[]{:S(2)}) copy-start(f32[256,1024]{1,0:T(8,128)S(1)} %pad_maximum_fusion.1) | copy-start | bytes 3145732
  166.2 161.7 %all-gather.3.cloned.1.call-start = ((), (), s32[]{:S(2)}) async-start(), calls=%async_computation.2 | async-start | bytes 3538944 | tf_op jit(solution)/shard_map/all_gather | solution.py:30
  221.1 106.8 %all-to-all-start = ((bf16[192,8,2048]{2,0,1:T(8,128)(2,1)}), bf16[192,8,2048]{2,0,1:T(8,128)(2,1)}, u32[]{:S(2)}, u32[]{:S(2)}) async-start(bf16[192,8,2048]{2,0,1:T(8,128)(2,1)} %bitcast.63), calls=%async_computation | async-start | bytes 12582912 | tf_op jit(solution)/shard_map/all_to_all | solution.py:32
Sparse Core Ops, SparseCore 0:
  11.2 87.3 all-reduce.2
  166.3 48.1 all-gather.4
  216.8 111.0 all-gather.2
where the time goes:
time: 350 us; the launch traced here: 346 us
  waiting for transfers between devices  236 us (67%)
  other arithmetic  55 us (16%)
  matrix products  18.5 us (5%)
  between operations  15.3 us (4%)
  local copies, waits for them, and re-layouts  14.6 us (4%)
  starting transfers between devices  6.58 us (2%)
    all_gather x1, waiting for transfers between devices, per_device(): mine = lax.all_gather(residual, 'days', axis=0, tiled=True)  100 us
    psum x1, waiting for transfers between devices, in_one(): total = lax.psum(jnp.concatenate([a.ravel() for a in arrays]), axis)  87.5 us
    all_gather x1, waiting for transfers between devices, per_device(): day_block = lax.all_gather(residual, 'assets', axis=1, tiled=True)  47.5 us
    another operation x6, other arithmetic, per_device(): lower = jnp.linalg.cholesky(gram)  34 us
    another operation x4, other arithmetic, per_device(): lax.linalg.triangular_solve(lower, middle, left_side=True, lower=True, tr...  19.8 us
    dot_general x1, matrix products, per_device(): lax.dot_general(mine, columns, (((0,), (0,)), ((), ())), preferred_elemen...  11.8 us
  transfers between devices with their start and end apart: 4, of which 3 were waited for; matrix products, arithmetic and copies ran while one was open for 2% of the time, Pallas kernels for 0%

commit v1 on v0

v1 whole, which is shorter than its diff:
```python
import functools

import jax
import jax.numpy as jnp
from jax import lax
from jax.experimental import pallas as pl
from jax.experimental.pallas import tpu as pltpu
from jax.sharding import PartitionSpec as P

MESH = pl.DeviceIdType.MESH
DAY_BLOCK = 192
ASSET_BLOCK = 1024
PART = 64
HALF = 96

TREES = (
    (("z+", ((0, 0), (0, 1), (0, 2), (1, 2))), ("y", ((0, 1), (0, 2))), ("z-", ((1, 1),))),
    (("z-", ((0, 0), (0, 3), (0, 2), (1, 3), (1, 2))), ("y", ((0, 3),)), ("z+", ((1, 3),))),
    (("y", ((0, 0), (1, 1), (1, 2), (1, 3))), ("z+", ((1, 0), (1, 1))), ("z-", ((1, 0),))),
)


def events():
    mine = {}
    for dx in (1, -1):
        for p in range(3):
            mine[dx, 0, p] = 5.0 + 2.7 * p
            mine[dx, 1, p] = 17.0 + 2.8 * p
    for p in range(3):
        mine[0, 1, p] = 5.5 + 3.5 * p
        mine[2, 0, p] = (14.0, 17.0, 14.1)[p]
        mine[2, 1, p] = (27.0, 26.0, 27.1)[p]
    order = [(t, "mine", key) for key, t in mine.items()]
    mine.update({(0, 0, p): 0.0 for p in range(3)})
    order += [(t + 7.0, "cols", key) for key, t in mine.items()]
    return sorted(order)


def gather_kernel(f_hbm, x_hbm, mine, cols, fall, load_sem, f_send, f_recv, f_pair, m_send, m_recv,
                  c_send, c_recv, c_pair, fp_send, cp_send):
    day, asset = lax.axis_index("days"), lax.axis_index("assets")
    x, h = day // 2, day % 2
    z, l, c = asset // 4, (asset // 2) % 2, asset % 2
    dl, dz = (l + h) % 2, (z - x + 4) % 4
    is_root = jnp.logical_and(dl == 0, dz == 0)

    def day_of(dx, dh):
        return lax.rem(x + dx + 4, 4) * 2 + lax.rem(h + dh, 2)

    def asset_of(link):
        if link == "z+":
            return lax.rem(z + 1, 4) * 4 + l * 2 + c
        if link == "z-":
            return lax.rem(z + 3, 4) * 4 + l * 2 + c
        return z * 4 + (1 - l) * 2 + c

    sibling = z * 4 + l * 2 + 1 - c

    load_x = pltpu.make_async_copy(
        x_hbm, mine.at[pl.ds(pl.multiple_of(day * DAY_BLOCK, DAY_BLOCK), DAY_BLOCK)], load_sem.at[0])
    load_f = pltpu.make_async_copy(
        f_hbm, fall.at[pl.ds(pl.multiple_of(day * DAY_BLOCK, DAY_BLOCK), DAY_BLOCK)], load_sem.at[1])
    load_f.start()
    load_x.start()

    barrier = pltpu.get_barrier_semaphore()
    greeted = [(day_of(dx, dh), asset) for dx in (0, 1, -1) for dh in (0, 1) if (dx, dh) != (0, 0) and (dh == 0 or dx == 0)]
    greeted += [(day, asset_of("z+")), (day, asset_of("z-")), (day, asset_of("y")), (day, sibling)]
    for d, a in greeted:
        pl.semaphore_signal(barrier, inc=1, device_id={"days": d, "assets": a}, device_id_type=MESH)
    pl.semaphore_wait(barrier, len(greeted))
    load_f.wait()
    load_x.wait()

    pending = []

    def send(src, dst, ssem, rsem, d, a, when=None):
        copy = pltpu.make_async_remote_copy(
            src_ref=src, dst_ref=dst, send_sem=ssem, recv_sem=rsem,
            device_id={"days": d, "assets": a}, device_id_type=MESH)
        if when is None:
            copy.start()
        else:
            pl.when(when)(copy.start)
        pending.append((when, copy))

    def arrived(ref, rsem, when=None):
        copy = pltpu.make_async_remote_copy(
            src_ref=ref, dst_ref=ref, send_sem=load_sem.at[0], recv_sem=rsem,
            device_id={"days": day, "assets": sibling}, device_id_type=MESH)
        if when is None:
            copy.wait_recv()
        else:
            pl.when(when)(copy.wait_recv)

    def f_rows(dx, dh, core):
        return fall.at[pl.ds(pl.multiple_of(day_of(dx, dh) * DAY_BLOCK + core * HALF, 32), HALF)]

    def part_rows(dx, dh, p):
        return pl.ds(pl.multiple_of(day_of(dx, dh) * DAY_BLOCK + p * PART, PART), PART)

    def m_part(dx, dh, p):
        return mine.at[part_rows(dx, dh, p)]

    def c_part(dx, dh, p, core):
        return cols.at[part_rows(dx, dh, p), pl.ds(pl.multiple_of(core * ASSET_BLOCK, ASSET_BLOCK), ASSET_BLOCK)]

    n_f, n_m, n_c = [0], [0], [0]

    def send_f(dx, dh, to):
        ref = f_rows(dx, dh, c)
        send(ref, ref, f_send.at[n_f[0]], f_recv.at[day_of(dx, dh)], day_of(*to), asset)
        n_f[0] += 1

    def send_m(dx, dh, p, to):
        ref = m_part(dx, dh, p)
        send(ref, ref, m_send.at[n_m[0]], m_recv.at[day_of(dx, dh), p], day_of(*to), asset)
        n_m[0] += 1

    def pair_f(dx, dh):
        ref = f_rows(dx, dh, c)
        arrived(ref, f_recv.at[day_of(dx, dh)])
        send(ref, ref, fp_send.at[day_of(dx, dh)], f_pair.at[day_of(dx, dh)], day, sibling)

    def root_sends(dx, dh, p):
        link = TREES[p][0][0]
        src, dst = m_part(dx, dh, p), c_part(dx, dh, p, c)
        send(src, dst, c_send.at[n_c[0]], c_recv.at[day_of(dx, dh), p], day, asset_of(link), is_root)
        n_c[0] += 1
        send(src, dst, cp_send.at[day_of(dx, dh), p], c_pair.at[day_of(dx, dh), p], day, sibling, is_root)

    def cols_relay(dx, dh, p):
        ref = c_part(dx, dh, p, c)
        other = jnp.logical_not(is_root)
        arrived(ref, c_recv.at[day_of(dx, dh), p], other)
        for link, roles in TREES[p]:
            roles = [role for role in roles if role != (0, 0)]
            if not roles:
                continue
            here = functools.reduce(jnp.logical_or, [jnp.logical_and(dl == i, dz == j) for i, j in roles])
            send(ref, ref, c_send.at[n_c[0]], c_recv.at[day_of(dx, dh), p], day, asset_of(link), here)
            n_c[0] += 1
        send(ref, ref, cp_send.at[day_of(dx, dh), p], c_pair.at[day_of(dx, dh), p], day, sibling, other)

    send_f(0, 0, (0, 1))
    send_f(0, 0, (1, 0))
    send_f(0, 0, (-1, 0))
    for p in range(3):
        send_m(0, 0, p, (0, 1))
        if p == 0:
            send_m(0, 0, p, (1, 0))
            send_m(0, 0, p, (-1, 0))
        root_sends(0, 0, p)
    pair_f(0, 1)
    send_f(0, 1, (1, 0))
    send_f(0, 1, (-1, 0))
    pair_f(1, 0)
    pair_f(-1, 0)
    send_f(-1, 0, (1, 0))
    for p in (1, 2):
        send_m(0, 0, p, (1, 0))
        send_m(0, 0, p, (-1, 0))
    pair_f(1, 1)
    send_f(1, 1, (-1, 0))
    pair_f(-1, 1)
    pair_f(2, 0)
    pair_f(2, 1)

    for _, kind, (dx, dh, p) in events():
        if kind == "mine":
            arrived(m_part(dx, dh, p), m_recv.at[day_of(dx, dh), p])
            if (dx, dh) == (0, 1):
                send_m(dx, dh, p, (1, 0))
                send_m(dx, dh, p, (-1, 0))
            if (dx, dh, p) in ((-1, 0, 0), (-1, 0, 1), (-1, 1, 0)):
                send_m(dx, dh, p, (1, 0))
            if (dx, dh, p) in ((1, 0, 2), (1, 1, 1), (1, 1, 2)):
                send_m(dx, dh, p, (-1, 0))
            root_sends(dx, dh, p)
        else:
            cols_relay(dx, dh, p)

    @pl.when(is_root)
    def _():
        @pl.loop(0, 8 * DAY_BLOCK // PART)
        def _(i):
            rows = pl.ds(pl.multiple_of(i * PART, PART), PART)
            cols[rows, pl.ds(pl.multiple_of(c * ASSET_BLOCK, ASSET_BLOCK), ASSET_BLOCK)] = mine[rows, :]

    keys = [(dx, dh) for dx in (0, 1, -1, 2) for dh in (0, 1)]
    for dx, dh in keys:
        if (dx, dh) != (0, 0):
            arrived(f_rows(dx, dh, 1 - c), f_pair.at[day_of(dx, dh)])
        for p in range(3):
            arrived(c_part(dx, dh, p, 1 - c), c_pair.at[day_of(dx, dh), p])
    for when, copy in pending:
        if when is None:
            copy.wait_send()
        else:
            pl.when(when)(copy.wait_send)


def gather(factors, returns):
    dma = pltpu.SemaphoreType.DMA
    days = 8 * DAY_BLOCK
    return pl.pallas_call(
        gather_kernel,
        out_shape=(
            jax.ShapeDtypeStruct((days, ASSET_BLOCK), jnp.bfloat16),
            jax.ShapeDtypeStruct((days, 2 * ASSET_BLOCK), jnp.bfloat16),
            jax.ShapeDtypeStruct((days, factors.shape[1]), jnp.bfloat16),
        ),
        in_specs=[pl.BlockSpec(memory_space=pl.ANY)] * 2,
        out_specs=(pl.BlockSpec(memory_space=pltpu.VMEM),) * 3,
        scratch_shapes=[
            dma((2,)), dma((7,)), dma((8,)), dma((8,)), dma((21,)), dma((8, 3)),
            dma((12 * 8,)), dma((8, 3)), dma((8, 3)), dma((8,)), dma((8, 3)),
        ],
        compiler_params=pltpu.CompilerParams(collective_id=0, has_side_effects=True),
    )(factors, returns)


def per_device(factors, returns):
    mine, columns, factors = gather(factors, returns)
    gram = lax.dot_general(
        factors, factors, (((0,), (0,)), ((), ())), preferred_element_type=jnp.float32
    )
    both = jnp.concatenate((mine, columns), axis=1)
    cross = lax.dot_general(
        factors, both, (((0,), (0,)), ((), ())), preferred_element_type=jnp.float32
    )
    lower = jnp.linalg.cholesky(gram)
    middle = lax.linalg.triangular_solve(lower, cross, left_side=True, lower=True)
    loadings = lax.linalg.triangular_solve(
        lower, middle, left_side=True, lower=True, transpose_a=True
    )
    fitted = jnp.dot(factors, loadings.astype(jnp.bfloat16), preferred_element_type=jnp.float32)
    residual = (both.astype(jnp.float32) - fitted).astype(jnp.bfloat16)
    covariance = lax.dot_general(
        residual[:, :ASSET_BLOCK], residual[:, ASSET_BLOCK:], (((0,), (0,)), ((), ())),
        preferred_element_type=jnp.float32
    )
    covariance = covariance / mine.shape[0]
    return (loadings[:, :ASSET_BLOCK], covariance)


def solution(mesh):
    in_specs = (P("days", None), P("days", "assets"))
    out_specs = (P(None, "assets"), P("assets", "days"))
    return jax.shard_map(
        per_device, mesh=mesh, in_specs=in_specs, out_specs=out_specs, check_vma=False
    )
```

time: 350 us -> 280 us (0.80); the launches traced: 346 us -> 280 us
  waiting for transfers between devices: 236 us -> 0 us
  Pallas kernels: 0 us -> 167 us
  matrix products: 18.5 us -> 36.1 us
  between operations: 15.3 us -> 2.05 us
  starting transfers between devices: 6.58 us -> 0 us
    pallas_call x0 -> x1, Pallas kernels: none -> 167 us  [gather(): pl.pallas_call(gather_kernel, out_shape=(jax.ShapeDtypeStruct((days, ASSE...]
    all_gather x2 -> x0, waiting for transfers between devices: 148 us -> none  [the longest x1 100 us: per_device(): mine = lax.all_gather(residual, 'days', axis=0, tiled=True)]
    psum x1 -> x0, waiting for transfers between devices: 87.5 us -> none  [in_one(): total = lax.psum(jnp.concatenate([a.ravel() for a in arrays]), axis)]
    unnamed x8 -> x19, local copies, waits for them, and re-layouts: 1.19 us -> 9.83 us
    dot_general x1, matrix products: 1.08 us -> 8.03 us  [per_device(): jnp.dot(factors, loadings.astype(jnp.bfloat16), preferred_element_type=jn...]
    all_to_all x1 -> x0, local copies, waits for them, and re-layouts: 6.61 us -> none  [per_device(): lax.all_to_all(day_block, 'days', split_axis=1, concat_axis=0, tiled=True)]
    all_to_all x1 -> x0, starting transfers between devices: 6.46 us -> none  [per_device(): lax.all_to_all(day_block, 'days', split_axis=1, concat_axis=0, tiled=True)]
  transfers between devices with their start and end apart: 4 -> 0, of which waited for: 3 -> 0; matrix products, arithmetic and copies ran while one was open for 2% -> 0% of each run, Pallas kernels for 0% -> 0%
where the time goes in v1:
time: 280 us
  Pallas kernels  167 us (60%)
  other arithmetic  58.2 us (21%)
  matrix products  36.1 us (13%)
  local copies, waits for them, and re-layouts  16.3 us (6%)
    pallas_call x1, Pallas kernels, gather(): pl.pallas_call(gather_kernel, out_shape=(jax.ShapeDtypeStruct((days, ASSE...  167 us
    another operation x6, other arithmetic, per_device(): lower = jnp.linalg.cholesky(gram)  34.7 us
    another operation x4, other arithmetic, per_device(): lax.linalg.triangular_solve(lower, middle, left_side=True, lower=True, tr...  22.5 us
    dot_general x1, matrix products, per_device(): lax.dot_general(residual[:, :ASSET_BLOCK], residual[:, ASSET_BLOCK:], (((...  11.8 us
    unnamed x19, local copies, waits for them, and re-layouts  9.83 us
    dot_general x1, matrix products, per_device(): jnp.dot(factors, loadings.astype(jnp.bfloat16), preferred_element_type=jn...  8.03 us

profile of v1, /device:TPU:5, one launch (start us, length us, event | category | flops | bytes accessed | tf_op | source)
XLA Modules:
  0.0 279.8 jit_solution(1852630152858207315)
XLA Ops:
  0.6 167.2 %shard_map.41 = (bf16[1536,1024]{1,0:T(8,128)(2,1)}, bf16[1536,2048]{1,0:T(8,128)(2,1)}, bf16[1536,256]{1,0:T(8,128)(2,1)}) custom-call(bf16[192,256]{1,0:T(8,128)(2,1)} %f_hbm.1, bf16[192,1024]{1,0:T(8,128)(2,1)} %x_hbm.1), custom_call_target="tpu_custom_call" | custom-call | tf_op jit(solution)/shard_map/pallas_call | solution.py:206
  167.8 2.4 constant_dynamic-update-slice_fusion.1
  170.2 1.4 copy-done.3
  172.4 3.6 %copy-done = bf16[1536,3072]{1,0:T(8,128)(2,1)} copy-done((bf16[1536,3072]{1,0:T(8,128)(2,1)}, bf16[1536,3072]{1,0:T(8,128)(2,1)S(1)}, u32[]{:S(2)}) %copy-start) | copy-done | bytes 9437208
  176.0 2.8 fusion.23
  178.8 1.8 fusion.22
  183.1 11.7 %cholesky.50 = f32[128,128]{1,0:T(8,128)S(1)} custom-call(f32[128,128]{1,0:T(8,128)S(1)} %cholesky.118), custom_call_target="Cholesky" | custom-call | tf_op jit(solution)/shard_map/jit(cholesky)/cholesky | solution.py:232
  195.6 9.8 %custom-call.16 = f32[1,128,128]{1,2,0:T(8,128)S(1)} custom-call(f32[1,128,128]{2,1,0:T(8,128)S(1)} %get-tuple-element.29), custom_call_target="InvertDiagBlocksLowerTriangular" | custom-call | tf_op jit(solution)/shard_map/jit(cholesky)/cholesky | solution.py:232
  205.4 1.7 constant_dynamic-update-slice_fusion.3
  207.1 1.1 convolution_subtract_fusion.2
  208.2 11.9 %cholesky.105 = f32[128,128]{1,0:T(8,128)S(1)} custom-call(f32[128,128]{1,0:T(8,128)S(1)} %convolution_subtract_fusion.2), custom_call_target="Cholesky" | custom-call | tf_op jit(solution)/shard_map/jit(cholesky)/cholesky | solution.py:232
  223.6 4.0 %while.1 = (s32[]{:T(128)}, f32[256,256]{1,0:T(8,128)S(1)}, s32[2,2]{1,0:T(2,128)S(1)}, f32[2,128,128]{2,1,0:T(8,128)S(1)}, s32[]{:T(128)}) while((s32[]{:T(128)}, f32[256,256]{1,0:T(8,128)S(1)}, s32[2,2]{1,0:T(2,128)S(1)}, f32[2,128,128]{2,1,0:T(8,128)S(1)}, s32[]{:T(128)}) %tuple.27), condition=%wide.while_cond, body=%wide.while_body.sunk | while | flops 2 | bytes 131189 | solution.py:234
  224.2 1.4 bitcast_dynamic-update-slice_fusion.2
  226.2 1.4 bitcast_dynamic-update-slice_fusion.2
  228.3 20.5 %custom-call.17 = f32[2,128,128]{1,2,0:T(8,128)S(1)} custom-call(f32[2,128,128]{2,1,0:T(8,128)} %copy-done.5), custom_call_target="InvertDiagBlocksLowerTriangular" | custom-call | tf_op jit(solution)/shard_map/triangular_solve | solution.py:234
  248.8 1.5 fusion.8
  250.3 1.5 convolution_subtract_fusion.1
  251.8 1.5 fusion.17
  253.3 1.5 fusion.16
  254.7 1.5 convolution_subtract_fusion
  256.2 1.5 fusion.15
  257.7 1.1 copy-done.1
  259.9 8.0 %subtract_convert_fusion = bf16[1536,3072]{1,0:T(8,128)(2,1)} fusion(bf16[1536,3072]{1,0:T(8,128)(2,1)S(1)} %bitcast.42, bf16[1536,256]{1,0:T(8,128)(2,1)} %get-tuple-element.5, f32[128,3072]{1,0:T(8,128)S(1)} %fusion.16, f32[128,3072]{1,0:T(8,128)} %copy-done.1), kind=kOutput, calls=%fused_computation.2 | convolution fusion | flops 2433220608 | bytes 22806528 | tf_op jit(solution)/shard_map/dot_general | solution.py:237
  268.0 11.8 %fusion.2 = f32[1024,2048]{1,0:T(8,128)} fusion(bf16[1536,3072]{1,0:T(8,128)(2,1)} %subtract_convert_fusion), kind=kOutput, calls=%fused_computation.5 | convolution fusion | flops 6444548096 | bytes 17825792 | tf_op jit(solution)/shard_map/dot_general | solution.py:239
  (33 shorter events, 9.4 us)
Async XLA Ops:
  167.8 3.7 %copy-start.3 = (bf16[1536,2048]{1,0:T(8,128)(2,1)S(1)}, bf16[1536,2048]{1,0:T(8,128)(2,1)}, u32[]{:S(2)}) copy-start(bf16[1536,2048]{1,0:T(8,128)(2,1)} %get-tuple-element.7) | copy-start | bytes 18874372
  171.5 4.5 %copy-start.2 = (bf16[1536,256]{1,0:T(8,128)(2,1)S(1)}, bf16[1536,256]{1,0:T(8,128)(2,1)}, u32[]{:S(2)}) copy-start(bf16[1536,256]{1,0:T(8,128)(2,1)} %get-tuple-element.5) | copy-start | bytes 2359300
  172.4 3.6 %copy-start = (bf16[1536,3072]{1,0:T(8,128)(2,1)}, bf16[1536,3072]{1,0:T(8,128)(2,1)S(1)}, u32[]{:S(2)}) copy-start(bf16[1536,3072]{1,0:T(8,128)(2,1)S(1)} %constant_dynamic-update-slice_fusion) | copy-start | bytes 28311556
  182.4 0.7 copy-start.4
  227.6 0.7 copy-start.5
  250.3 9.7 %slice-start = ((s8[9437184]{0:T(1024)(128)(4,1)}), s8[4194304]{0:T(1024)(128)(4,1)S(1)}, s32[]{:S(2)}) async-start(s8[9437184]{0:T(1024)(128)(4,1)} %bitcast.41), calls=%async_computation | async-start | bytes 8388608
  251.8 8.1 %slice-start.1 = ((s8[9437184]{0:T(1024)(128)(4,1)}), s8[4194304]{0:T(1024)(128)(4,1)S(1)}, s32[]{:S(2)}) async-start(s8[9437184]{0:T(1024)(128)(4,1)} %bitcast.41), calls=%async_computation.1 | async-start | bytes 8388608
  254.7 5.2 %slice-start.2 = ((s8[9437184]{0:T(1024)(128)(4,1)}), s8[1048576]{0:T(1024)(128)(4,1)S(1)}, s32[]{:S(2)}) async-start(s8[9437184]{0:T(1024)(128)(4,1)} %bitcast.41), calls=%async_computation.2 | async-start | bytes 2097152
  257.7 1.1 copy-start.1

commit v2 on v1

v2 whole, which is shorter than its diff:
```python
import functools

import jax
import jax.numpy as jnp
from jax import lax
from jax.experimental import pallas as pl
from jax.experimental.pallas import tpu as pltpu
from jax.sharding import PartitionSpec as P

MESH = pl.DeviceIdType.MESH
DAY_BLOCK = 192
DAYS = 8 * DAY_BLOCK
ASSET_BLOCK = 1024
FACTORS = 256
HALF = 96
PARTS = 3
PART = DAY_BLOCK // PARTS
PIVOTS = 4
TILE = 256

TREES = (
    (("z+", ((0, 0), (0, 1), (0, 2), (1, 2))), ("y", ((0, 1), (0, 2))), ("z-", ((1, 1),))),
    (("z-", ((0, 0), (0, 3), (0, 2), (1, 3), (1, 2))), ("y", ((0, 3),)), ("z+", ((1, 3),))),
    (("y", ((0, 0), (1, 1), (1, 2), (1, 3))), ("z+", ((1, 0), (1, 1))), ("z-", ((1, 0),))),
)
DEPTHS = (
    (((0, 1),), ((0, 2), (1, 1)), ((0, 3), (1, 2), (1, 0)), ((1, 3),)),
    (((0, 3),), ((0, 2), (1, 3)), ((0, 1), (1, 2), (1, 0)), ((1, 1),)),
    (((1, 0),), ((1, 1), (1, 3)), ((0, 1), (1, 2), (0, 3)), ((0, 2),)),
)
CHUNKS = ((0, 0), (0, 1), (1, 0), (1, 1), (-1, 0), (-1, 1), (2, 0), (2, 1))

LINKS = ("h", "x+", "x-", "root")
ORDER = (
    (0, 2, 2), (0, 2, 0), (0, 1, 1), (0, 0, 1), (0, 0, 0), (0, 3, 1), (0, 2, 1), (0, 1, 2),
    (0, 1, 0), (0, 3, 2), (2, 0, 2, 1), (2, 0, 0, 1), (2, 4, 1, 1), (0, 3, 0), (1, 4, 1), (2, 2, 0, 1),
    (1, 2, 0), (2, 0, 1, 1), (0, 0, 2), (1, 2, 2), (1, 4, 0), (1, 1, 1), (2, 2, 2, 1), (2, 4, 1, 2),
    (1, 1, 0), (2, 6, 1, 1), (2, 0, 1, 2), (2, 0, 2, 2), (1, 6, 1), (2, 0, 0, 2), (1, 3, 1), (2, 4, 2, 1),
    (1, 2, 1), (1, 6, 0), (2, 2, 0, 2), (1, 4, 2), (1, 1, 2), (2, 2, 2, 2), (2, 2, 1, 1), (1, 6, 2),
    (2, 6, 1, 2), (1, 3, 0), (2, 3, 1, 1), (2, 1, 2, 1), (2, 6, 0, 2), (2, 4, 1, 3), (2, 6, 0, 1), (2, 0, 0, 3),
    (1, 5, 0), (2, 6, 2, 1), (2, 2, 1, 2), (2, 0, 2, 3), (2, 4, 0, 1), (2, 4, 2, 2), (2, 4, 0, 2), (2, 3, 1, 2),
    (2, 1, 0, 2), (2, 1, 2, 2), (2, 4, 1, 4), (1, 5, 1), (2, 6, 1, 3), (1, 3, 2), (2, 7, 1, 1), (2, 7, 1, 2),
    (2, 1, 0, 1), (2, 5, 0, 2), (2, 5, 1, 1), (2, 6, 0, 3), (2, 3, 2, 2), (2, 6, 2, 2), (2, 0, 1, 3), (2, 1, 1, 1),
    (2, 5, 0, 1), (2, 3, 2, 1), (2, 5, 2, 2), (2, 5, 2, 1), (2, 2, 2, 3), (2, 3, 0, 1), (2, 4, 0, 3), (1, 5, 2),
    (2, 7, 0, 1), (2, 7, 2, 1), (2, 3, 0, 2), (2, 5, 1, 2), (2, 1, 2, 4), (2, 4, 2, 3), (2, 7, 2, 2), (2, 2, 1, 3),
    (2, 7, 0, 2), (2, 3, 1, 3), (2, 1, 2, 3), (2, 4, 2, 4), (2, 1, 0, 3), (2, 7, 1, 3), (2, 1, 1, 2), (2, 0, 1, 4),
    (2, 6, 2, 4), (2, 2, 0, 3), (2, 6, 1, 4), (2, 3, 2, 3), (2, 4, 0, 4), (2, 3, 0, 4), (2, 5, 1, 4), (2, 0, 2, 4),
    (2, 5, 0, 3), (2, 6, 2, 3), (2, 7, 2, 4), (2, 3, 0, 3), (2, 5, 1, 3), (1, 7, 1), (2, 2, 2, 4), (2, 7, 1, 4),
    (2, 5, 2, 4), (2, 1, 0, 4), (1, 7, 2), (2, 5, 2, 3), (2, 7, 0, 3), (1, 7, 0), (2, 3, 1, 4), (2, 1, 1, 3),
    (2, 2, 0, 4), (2, 7, 0, 4), (2, 0, 0, 4), (2, 1, 1, 4), (2, 7, 2, 3), (2, 6, 0, 4), (2, 3, 2, 4), (2, 5, 0, 4),
    (2, 2, 1, 4),
)


def forward_right(dh, p):
    return p < (PARTS + 1 - dh) // 2


def invert(a):
    n = a.shape[0]
    lane = lax.broadcasted_iota(jnp.int32, (n, n), 1)
    lane_one = lax.broadcasted_iota(jnp.int32, (1, n), 1)
    sub = lax.broadcasted_iota(jnp.int32, (8, n), 0)
    for k in range(n):
        row, col = a[k:k + 1, :], a[:, k:k + 1]
        scale = 1.0 / a[k:k + 1, k:k + 1]
        scaled = jnp.where(lane_one == k, scale, row * scale)
        a = jnp.where(lane == k, 0.0, a) - col * scaled
        g = k // 8 * 8
        middle = jnp.where(sub == k - g, jnp.broadcast_to(scaled, (8, n)), a[g:g + 8])
        a = jnp.concatenate([part for part in (a[:g], middle, a[g + 8:]) if part.shape[0]], axis=0)
        if k % PIVOTS == PIVOTS - 1:
            yield None
    yield a


def exact_dot(a, b):
    return jnp.dot(a, b, precision=lax.Precision.HIGHEST, preferred_element_type=jnp.float32)


def inverse_of_gram(fall, fall_t, gram, inverse):
    fall_t[...] = fall[...].T
    yield
    gram[...] = jnp.dot(fall_t[...], fall[...], preferred_element_type=jnp.float32)
    yield
    n = FACTORS // 2
    first = None
    for first in invert(gram[:n, :n]):
        yield
    upper, lower = gram[:n, n:], gram[n:, :n]
    right, left = exact_dot(first, upper), exact_dot(lower, first)
    schur = gram[n:, n:] - exact_dot(lower, right)
    yield
    second = None
    for second in invert(schur):
        yield
    off = -exact_dot(right, second)
    inverse[:n, :n] = first - exact_dot(off, left)
    inverse[:n, n:] = off
    inverse[n:, :n] = -exact_dot(second, left)
    inverse[n:, n:] = second
    yield


def gather_kernel(f_hbm, x_hbm, mine, cols, fall, fall_t, inverse, gram, load_sem, f_send, f_recv, f_pair,
                  m_send, m_recv, c_send, c_recv, c_pair, fp_send, cp_send):
    day, asset = lax.axis_index("days"), lax.axis_index("assets")
    x, h = day // 2, day % 2
    z, l, c = asset // 4, (asset // 2) % 2, asset % 2
    dl, dz = (l + h) % 2, (z - x + 4) % 4
    is_root = jnp.logical_and(dl == 0, dz == 0)

    def among(roles):
        return functools.reduce(jnp.logical_or, [jnp.logical_and(dl == i, dz == j) for i, j in roles])

    def day_of(dx, dh):
        return lax.rem(x + dx + 4, 4) * 2 + lax.rem(h + dh, 2)

    def asset_of(link):
        if link == "z+":
            return lax.rem(z + 1, 4) * 4 + l * 2 + c
        if link == "z-":
            return lax.rem(z + 3, 4) * 4 + l * 2 + c
        return z * 4 + (1 - l) * 2 + c

    sibling = z * 4 + l * 2 + 1 - c
    own_rows = pl.ds(pl.multiple_of(day * DAY_BLOCK, DAY_BLOCK), DAY_BLOCK)
    load_x = pltpu.make_async_copy(x_hbm, mine.at[own_rows], load_sem.at[0])
    load_f = pltpu.make_async_copy(f_hbm, fall.at[own_rows], load_sem.at[1])
    load_f.start()
    load_x.start()

    barrier = pltpu.get_barrier_semaphore()
    greeted = [(day_of(0, 1), asset), (day_of(1, 0), asset), (day_of(-1, 0), asset)]
    greeted += [(day, asset_of("z+")), (day, asset_of("z-")), (day, asset_of("y")), (day, sibling)]
    for d, a in greeted:
        pl.semaphore_signal(barrier, inc=1, device_id={"days": d, "assets": a}, device_id_type=MESH)
    pl.semaphore_wait(barrier, len(greeted))
    load_f.wait()
    load_x.wait()

    pending = []

    def send(src, dst, ssem, rsem, d, a, when=None):
        copy = pltpu.make_async_remote_copy(
            src_ref=src, dst_ref=dst, send_sem=ssem, recv_sem=rsem,
            device_id={"days": d, "assets": a}, device_id_type=MESH)
        if when is None:
            copy.start()
        else:
            pl.when(when)(copy.start)
        pending.append((when, copy))

    def arrived(ref, rsem):
        pltpu.make_async_remote_copy(
            src_ref=ref, dst_ref=ref, send_sem=load_sem.at[0], recv_sem=rsem,
            device_id={"days": day, "assets": sibling}, device_id_type=MESH).wait_recv()

    def f_rows(dx, dh, core):
        return fall.at[pl.ds(pl.multiple_of(day_of(dx, dh) * DAY_BLOCK + core * HALF, 32), HALF)]

    def part_rows(dx, dh, p):
        return pl.ds(pl.multiple_of(day_of(dx, dh) * DAY_BLOCK + p * PART, PART), PART)

    def m_part(dx, dh, p):
        return mine.at[part_rows(dx, dh, p)]

    def c_part(dx, dh, p, core):
        return cols.at[part_rows(dx, dh, p), pl.ds(pl.multiple_of(core * ASSET_BLOCK, ASSET_BLOCK), ASSET_BLOCK)]

    n_f, n_m, n_c = [0], [0], [0]

    def send_f(dx, dh, to):
        ref = f_rows(dx, dh, c)
        send(ref, ref, f_send.at[n_f[0]], f_recv.at[day_of(dx, dh)], day_of(*to), asset)
        n_f[0] += 1

    def send_m(dx, dh, p, to):
        ref = m_part(dx, dh, p)
        send(ref, ref, m_send.at[n_m[0]], m_recv.at[day_of(dx, dh), p], day_of(*to), asset)
        n_m[0] += 1

    def pair_f(dx, dh):
        ref = f_rows(dx, dh, c)
        arrived(ref, f_recv.at[day_of(dx, dh)])
        send(ref, ref, fp_send.at[day_of(dx, dh)], f_pair.at[day_of(dx, dh)], day, sibling)

    def root_sends(dx, dh, p):
        link = TREES[p * 3 // PARTS][0][0]
        src, dst = m_part(dx, dh, p), c_part(dx, dh, p, c)
        send(src, dst, c_send.at[n_c[0]], c_recv.at[day_of(dx, dh), p], day, asset_of(link), is_root)
        n_c[0] += 1
        send(src, dst, cp_send.at[day_of(dx, dh), p], c_pair.at[day_of(dx, dh), p], day, sibling, is_root)

    def relay_mine(dx, dh, p):
        arrived(m_part(dx, dh, p), m_recv.at[day_of(dx, dh), p])
        if (dx, dh) == (0, 1):
            send_m(dx, dh, p, (1, 0))
            send_m(dx, dh, p, (-1, 0))
        if dx == -1 and forward_right(dh, p):
            send_m(dx, dh, p, (1, 0))
        if dx == 1 and not forward_right(dh, p):
            send_m(dx, dh, p, (-1, 0))
        root_sends(dx, dh, p)

    def relay_cols(dx, dh, p, depth):
        ref = c_part(dx, dh, p, c)
        tree = p * 3 // PARTS
        here = DEPTHS[tree][depth - 1]
        pl.when(among(here))(lambda: arrived(ref, c_recv.at[day_of(dx, dh), p]))
        for link, roles in TREES[tree]:
            roles = [role for role in roles if role in here]
            if roles:
                send(ref, ref, c_send.at[n_c[0]], c_recv.at[day_of(dx, dh), p], day, asset_of(link), among(roles))
                n_c[0] += 1
        send(ref, ref, cp_send.at[day_of(dx, dh), p], c_pair.at[day_of(dx, dh), p], day, sibling, among(here))

    send_f(0, 0, (0, 1))
    send_f(0, 0, (1, 0))
    send_f(0, 0, (-1, 0))
    factor_steps = [
        lambda: (pair_f(0, 1), send_f(0, 1, (1, 0)), send_f(0, 1, (-1, 0))),
        lambda: (pair_f(1, 0), pair_f(-1, 0), send_f(-1, 0, (1, 0))),
        lambda: (pair_f(1, 1), send_f(1, 1, (-1, 0)), pair_f(-1, 1)),
        lambda: (pair_f(2, 0), pair_f(2, 1)),
        lambda: [arrived(f_rows(dx, dh, 1 - c), f_pair.at[day_of(dx, dh)]) for dx, dh in CHUNKS[1:]],
    ]
    solve = inverse_of_gram(fall, fall_t, gram, inverse)

    for i, (kind, a, p, *depth) in enumerate(ORDER):
        if kind == 0 and LINKS[a] == "root":
            root_sends(0, 0, p)
        elif kind == 0:
            send_m(0, 0, p, {"h": (0, 1), "x+": (1, 0), "x-": (-1, 0)}[LINKS[a]])
        elif kind == 1:
            relay_mine(*CHUNKS[a], p)
        else:
            relay_cols(*CHUNKS[a], p, *depth)
        if i in (10, 11, 12, 22, 23):
            factor_steps.pop(0)()
        if not factor_steps:
            for _ in range(1):
                next(solve, None)
    for step in factor_steps:
        step()
    for _ in solve:
        pass

    @pl.when(is_root)
    def _():
        @pl.loop(0, DAYS // 64)
        def _(i):
            rows = pl.ds(pl.multiple_of(i * 64, 64), 64)
            cols[rows, pl.ds(pl.multiple_of(c * ASSET_BLOCK, ASSET_BLOCK), ASSET_BLOCK)] = mine[rows, :]

    for dx, dh in CHUNKS:
        for p in range(PARTS):
            arrived(c_part(dx, dh, p, 1 - c), c_pair.at[day_of(dx, dh), p])
    for when, copy in pending:
        if when is None:
            copy.wait_send()
        else:
            pl.when(when)(copy.wait_send)


def gather(factors, returns):
    dma = pltpu.SemaphoreType.DMA
    return pl.pallas_call(
        gather_kernel,
        out_shape=(
            jax.ShapeDtypeStruct((DAYS, ASSET_BLOCK), jnp.bfloat16),
            jax.ShapeDtypeStruct((DAYS, 2 * ASSET_BLOCK), jnp.bfloat16),
            jax.ShapeDtypeStruct((DAYS, FACTORS), jnp.bfloat16),
            jax.ShapeDtypeStruct((FACTORS, DAYS), jnp.bfloat16),
            jax.ShapeDtypeStruct((FACTORS, FACTORS), jnp.float32),
        ),
        in_specs=[pl.BlockSpec(memory_space=pltpu.HBM)] * 2,
        out_specs=(pl.BlockSpec(memory_space=pltpu.VMEM),) * 5,
        scratch_shapes=[
            pltpu.VMEM((FACTORS, FACTORS), jnp.float32),
            dma((2,)), dma((7,)), dma((8,)), dma((8,)), dma((7 * PARTS,)), dma((8, PARTS)),
            dma((8 * PARTS * 7,)), dma((8, PARTS)), dma((8, PARTS)), dma((8,)), dma((8, PARTS)),
        ],
        compiler_params=pltpu.CompilerParams(
            collective_id=0, has_side_effects=True, vmem_limit_bytes=32 * 2**20),
        name="gather",
    )(factors, returns)


def covariance_kernel(mine, cols, fall, fall_t, inverse, loadings, covariance, mine_t):
    def residual_of(block):
        cross = jnp.dot(fall_t[...], block, preferred_element_type=jnp.float32)
        exposure = exact_dot(inverse[...], cross)
        fitted = jnp.dot(fall[...], exposure.astype(jnp.bfloat16), preferred_element_type=jnp.float32)
        return exposure, (block.astype(jnp.float32) - fitted).astype(jnp.bfloat16)

    @pl.when(pl.program_id(0) == 0)
    def _():
        @pl.loop(0, ASSET_BLOCK // TILE)
        def _(i):
            part = pl.ds(pl.multiple_of(i * TILE, TILE), TILE)
            exposure, residual = residual_of(mine[:, part])
            loadings[:, part] = exposure
            mine_t[part, :] = residual.T

    _, residual = residual_of(cols[...])
    covariance[...] = jnp.dot(mine_t[...], residual, preferred_element_type=jnp.float32) * (1.0 / DAYS)


def covariances(mine, cols, fall, fall_t, inverse):
    def whole(a):
        return pl.BlockSpec(a.shape, lambda i: (0, 0), pipeline_mode=pl.Buffered(1))

    return pl.pallas_call(
        covariance_kernel,
        out_shape=(
            jax.ShapeDtypeStruct((FACTORS, ASSET_BLOCK), jnp.float32),
            jax.ShapeDtypeStruct((ASSET_BLOCK, 2 * ASSET_BLOCK), jnp.float32),
        ),
        grid=(2 * ASSET_BLOCK // TILE,),
        in_specs=[whole(mine), pl.BlockSpec((DAYS, TILE), lambda i: (0, i)), whole(fall), whole(fall_t), whole(inverse)],
        out_specs=(
            pl.BlockSpec((FACTORS, ASSET_BLOCK), lambda i: (0, 0)),
            pl.BlockSpec((ASSET_BLOCK, TILE), lambda i: (0, i)),
        ),
        scratch_shapes=[pltpu.VMEM((ASSET_BLOCK, DAYS), jnp.bfloat16)],
        compiler_params=pltpu.CompilerParams(
            dimension_semantics=("arbitrary",), vmem_limit_bytes=32 * 2**20),
        name="covariances",
    )(mine, cols, fall, fall_t, inverse)


def per_device(factors, returns):
    factors = pltpu.with_memory_space_constraint(factors, pltpu.HBM)
    returns = pltpu.with_memory_space_constraint(returns, pltpu.HBM)
    return covariances(*gather(factors, returns))


def solution(mesh):
    in_specs = (P("days", None), P("days", "assets"))
    out_specs = (P(None, "assets"), P("assets", "days"))
    return jax.shard_map(
        per_device, mesh=mesh, in_specs=in_specs, out_specs=out_specs, check_vma=False
    )
```

time: 280 us -> 117 us (0.42)
  other arithmetic: 58.2 us -> 0 us
  Pallas kernels: 167 us -> 114 us
  matrix products: 36.1 us -> 0 us
  local copies, waits for them, and re-layouts: 16.3 us -> 0 us
    another operation x10 -> x0, other arithmetic: 57.2 us -> none  [the longest x6 34.7 us: per_device(): lower = jnp.linalg.cholesky(gram)]
    pallas_call x1 -> x2, Pallas kernels: 167 us -> 114 us  [the longest x1 85.9 us: gather(): pl.pallas_call(gather_kernel, out_shape=(jax.ShapeDtypeStruct((DAYS, ASSE...]
    dot_general x4 -> x0, matrix products: 24.4 us -> none  [the longest x1 11.8 us: per_device(): lax.dot_general(residual[:, :ASSET_BLOCK], residual[:, ASSET_BLOCK:], (((...]
    another operation x8 -> x0, matrix products: 11.6 us -> none  [the longest x3 4.45 us: per_device(): lax.linalg.triangular_solve(lower, cross, left_side=True, lower=True)]
    unnamed x19 -> x0, local copies, waits for them, and re-layouts: 9.83 us -> none
    another operation x9 -> x0, local copies, waits for them, and re-layouts: 4.75 us -> none
where the time goes in v2:
time: 117 us; the launch traced here: 115 us
  Pallas kernels  114 us (97%)
    pallas_call x1, Pallas kernels, gather(): pl.pallas_call(gather_kernel, out_shape=(jax.ShapeDtypeStruct((DAYS, ASSE...  85.9 us
    pallas_call x1, Pallas kernels, covariances(): pl.pallas_call(covariance_kernel, out_shape=(jax.ShapeDtypeStruct((FACTOR...  28.3 us

profile of v2, /device:TPU:5, one launch (start us, length us, event | category | flops | bytes accessed | tf_op | source)
XLA Modules:
  0.0 114.9 jit_solution(4658415285972359496)
XLA Ops:
  0.6 85.9 %gather.1 = (bf16[1536,1024]{1,0:T(8,128)(2,1)S(1)}, bf16[1536,2048]{1,0:T(8,128)(2,1)S(1)}, bf16[1536,256]{1,0:T(8,128)(2,1)S(1)}, bf16[256,1536]{1,0:T(8,128)(2,1)S(1)}, f32[256,256]{1,0:T(8,128)S(1)}) custom-call(bf16[192,256]{1,0:T(8,128)(2,1)} %f_hbm.1, bf16[192,1024]{1,0:T(8,128)(2,1)} %x_hbm.1), custom_call_target="tpu_custom_call" | custom-call | tf_op jit(solution)/shard_map/gather/pallas_call | solution.py:268
  86.5 28.3 %covariances.1 = (f32[256,1024]{1,0:T(8,128)}, f32[1024,2048]{1,0:T(8,128)}) custom-call(bf16[1536,1024]{1,0:T(8,128)(2,1)S(1)} %get-tuple-element.7.mine, bf16[1536,2048]{1,0:T(8,128)(2,1)S(1)} %get-tuple-element.8.cols, bf16[1536,256]{1,0:T(8,128)(2,1)S(1)} %get-tuple-element.9.fall, bf16[256,1536]{1,0:T(8,128)(2,1)S(1)} %get-tuple-element.10.fall_t, ...), custom_call_target="tpu_custom_call" | custom-call | tf_op jit(solution)/shard_map/covariances/pallas_call | solution.py:314

commit v3 on v2

v3 whole, which is shorter than its diff:
```python
import functools
import itertools

import jax
import jax.numpy as jnp
from jax import lax
from jax.experimental import pallas as pl
from jax.experimental.pallas import tpu as pltpu
from jax.sharding import PartitionSpec as P

MESH = pl.DeviceIdType.MESH
DAY_BLOCK = 192
DAYS = 8 * DAY_BLOCK
ASSET_BLOCK = 1024
FACTORS = 256
HALF = 96
THIRDS, SIDES = 3, 2
PARTS = THIRDS * SIDES
PART = DAY_BLOCK // THIRDS
SIDE = ASSET_BLOCK // SIDES
PIVOTS = 8

TREES = (
    (("z+", ((0, 0), (0, 1), (0, 2), (1, 2))), ("y", ((0, 1), (0, 2))), ("z-", ((1, 1),))),
    (("z-", ((0, 0), (0, 3), (0, 2), (1, 3), (1, 2))), ("y", ((0, 3),)), ("z+", ((1, 3),))),
    (("y", ((0, 0), (1, 1), (1, 2), (1, 3))), ("z+", ((1, 0), (1, 1))), ("z-", ((1, 0),))),
)
DEPTHS = (
    (((0, 1),), ((0, 2), (1, 1)), ((0, 3), (1, 2), (1, 0)), ((1, 3),)),
    (((0, 3),), ((0, 2), (1, 3)), ((0, 1), (1, 2), (1, 0)), ((1, 1),)),
    (((1, 0),), ((1, 1), (1, 3)), ((0, 1), (1, 2), (0, 3)), ((0, 2),)),
)
CHUNKS = ((0, 0), (0, 1), (1, 0), (1, 1), (-1, 0), (-1, 1), (2, 0), (2, 1))

LINKS = ("h", "x+", "x-", "root")
ORDER = (
    (3, 0), (0, 1, 0), (0, 2, 0), (0, 3, 0), (0, 0, 0), (0, 1, 1), (0, 2, 1), (0, 3, 1),
    (0, 0, 1), (0, 1, 2), (0, 2, 2), (0, 3, 2), (0, 0, 2), (2, 0, 0, 1), (2, 0, 1, 1), (3, 1),
    (0, 1, 3), (0, 2, 3), (0, 3, 3), (0, 0, 3), (0, 1, 4), (0, 2, 4), (0, 3, 4), (0, 0, 4),
    (0, 1, 5), (0, 2, 5), (0, 3, 5), (0, 0, 5), (1, 2, 0), (1, 4, 0), (1, 2, 1), (1, 4, 1),
    (2, 0, 2, 1), (1, 2, 2), (1, 4, 2), (3, 2), (1, 1, 0), (2, 0, 0, 2), (2, 0, 1, 2), (2, 0, 3, 1),
    (2, 0, 4, 1), (1, 2, 3), (1, 4, 3), (1, 1, 1), (1, 1, 2), (2, 0, 2, 2), (2, 4, 0, 1), (2, 2, 0, 1),
    (2, 4, 1, 1), (1, 2, 4), (2, 2, 1, 1), (1, 4, 4), (2, 0, 5, 1), (1, 1, 3), (2, 0, 0, 3), (2, 1, 0, 1),
    (2, 0, 1, 3), (2, 0, 3, 2), (2, 1, 1, 1), (2, 0, 4, 2), (1, 2, 5), (1, 4, 5), (1, 1, 4), (2, 0, 2, 3),
    (1, 1, 5), (1, 6, 2), (1, 6, 0), (2, 4, 0, 2), (2, 4, 1, 2), (2, 0, 5, 2), (2, 4, 3, 1), (2, 2, 3, 1),
    (2, 4, 4, 1), (2, 2, 4, 1), (1, 3, 0), (1, 6, 1), (3, 3), (2, 0, 3, 3), (2, 0, 4, 3), (2, 0, 2, 4),
    (2, 2, 0, 2), (2, 2, 1, 2), (2, 1, 4, 1), (2, 0, 0, 4), (1, 3, 1), (2, 4, 2, 1), (2, 1, 0, 2), (2, 1, 1, 2),
    (1, 5, 0), (2, 6, 1, 1), (2, 0, 5, 3), (2, 0, 1, 4), (2, 4, 0, 3), (1, 3, 2), (2, 2, 2, 1), (2, 0, 3, 4),
    (2, 1, 3, 1), (2, 6, 0, 1), (2, 4, 1, 3), (2, 4, 3, 2), (2, 4, 4, 2), (1, 6, 3), (2, 3, 0, 1), (1, 3, 3),
    (2, 2, 0, 3), (2, 3, 1, 1), (2, 2, 1, 3), (2, 1, 2, 1), (2, 4, 2, 2), (2, 0, 4, 4), (2, 1, 0, 3), (1, 5, 1),
    (2, 1, 1, 3), (2, 2, 3, 2), (2, 4, 5, 1), (1, 6, 5), (2, 0, 5, 4), (2, 4, 0, 4), (2, 2, 4, 2), (2, 1, 3, 2),
    (2, 1, 4, 2), (1, 3, 4), (1, 5, 2), (2, 4, 3, 3), (2, 2, 5, 1), (2, 1, 5, 1), (2, 2, 2, 2), (2, 2, 0, 4),
    (1, 6, 4), (2, 6, 0, 2), (2, 6, 1, 2), (2, 4, 1, 4), (2, 1, 2, 2), (1, 3, 5), (2, 6, 2, 1), (2, 1, 0, 4),
    (2, 2, 3, 3), (1, 5, 3), (2, 3, 0, 2), (2, 3, 1, 2), (2, 2, 1, 4), (2, 1, 1, 4), (2, 4, 5, 2), (2, 4, 3, 4),
    (2, 2, 5, 2), (2, 1, 3, 3), (1, 7, 1), (3, 4), (4, 0), (2, 2, 3, 4), (4, 1), (2, 4, 4, 3),
    (2, 6, 0, 3), (4, 2), (2, 2, 4, 3), (2, 7, 1, 1), (2, 5, 1, 1), (2, 3, 4, 1), (4, 3), (2, 1, 4, 3),
    (4, 4), (2, 4, 2, 3), (4, 5), (2, 2, 2, 3), (4, 6), (2, 1, 2, 3), (4, 7), (4, 8),
    (4, 9), (2, 4, 2, 4), (4, 10), (4, 11), (4, 12), (4, 13), (4, 14), (4, 15),
    (2, 1, 3, 4), (4, 16), (2, 6, 0, 4), (1, 7, 2), (1, 5, 4), (4, 17), (4, 18), (4, 19),
    (2, 3, 0, 3), (1, 7, 0), (1, 5, 5), (4, 20), (2, 6, 4, 1), (2, 1, 5, 2), (2, 7, 2, 1), (2, 3, 2, 1),
    (1, 7, 4), (4, 21), (2, 4, 5, 3), (2, 2, 5, 3), (2, 6, 2, 2), (1, 7, 3), (2, 6, 1, 3), (1, 7, 5),
    (2, 7, 1, 2), (2, 3, 1, 3), (2, 5, 1, 2), (2, 7, 0, 1), (2, 3, 4, 2), (2, 5, 0, 1), (2, 6, 3, 1), (4, 22),
    (2, 3, 3, 1), (4, 23), (2, 3, 0, 4), (2, 5, 2, 1), (2, 4, 4, 4), (4, 24), (2, 7, 3, 1), (2, 5, 3, 1),
    (2, 7, 2, 2), (4, 25), (2, 7, 1, 3), (2, 7, 0, 2), (4, 26), (2, 3, 2, 2), (2, 6, 4, 2), (2, 1, 5, 3),
    (4, 27), (2, 5, 0, 2), (2, 2, 2, 4), (2, 2, 4, 4), (2, 1, 2, 4), (4, 28), (2, 6, 2, 3), (2, 6, 3, 2),
    (4, 29), (2, 7, 0, 3), (2, 6, 5, 1), (2, 5, 1, 3), (2, 7, 2, 3), (2, 1, 4, 4), (2, 4, 5, 4), (4, 30),
    (2, 3, 4, 3), (2, 3, 3, 2), (2, 5, 0, 3), (2, 7, 5, 1), (4, 31), (2, 6, 1, 4), (2, 2, 5, 4), (2, 5, 2, 2),
    (2, 5, 4, 1), (4, 32), (2, 6, 3, 3), (2, 3, 5, 1), (2, 7, 4, 1), (4, 33), (2, 7, 3, 2), (2, 7, 0, 4),
    (2, 3, 2, 3), (4, 34), (2, 3, 1, 4), (2, 1, 5, 4), (2, 7, 1, 4), (4, 35), (2, 5, 0, 4), (2, 6, 4, 3),
    (2, 3, 3, 3), (2, 5, 3, 2), (4, 36), (4, 37), (2, 6, 5, 2), (2, 5, 4, 2), (2, 5, 1, 4), (2, 7, 5, 2),
    (2, 6, 3, 4), (4, 38), (2, 3, 4, 4), (2, 5, 2, 3), (2, 6, 2, 4), (2, 5, 5, 1), (2, 7, 4, 2), (2, 7, 3, 3),
    (2, 3, 3, 4), (4, 39), (2, 6, 4, 4), (2, 7, 2, 4), (2, 5, 4, 3), (2, 3, 2, 4), (2, 6, 5, 3), (2, 5, 2, 4),
    (4, 40), (2, 7, 5, 3), (2, 7, 4, 3), (2, 5, 3, 3), (2, 3, 5, 2), (2, 5, 5, 2), (2, 7, 3, 4), (2, 5, 4, 4),
    (4, 41), (4, 42), (2, 6, 5, 4), (2, 3, 5, 3), (2, 5, 3, 4), (2, 7, 4, 4), (4, 43), (2, 7, 5, 4),
    (4, 44), (4, 45), (2, 3, 5, 4), (2, 5, 5, 3), (2, 5, 5, 4),
)


def forward_right(dh, p):
    return p % THIRDS < (THIRDS + 1 - dh) // 2


def invert(a):
    n = a.shape[0]
    lane = lax.broadcasted_iota(jnp.int32, (n, n), 1)
    lane_one = lax.broadcasted_iota(jnp.int32, (1, n), 1)
    sub = lax.broadcasted_iota(jnp.int32, (8, n), 0)
    for k in range(n):
        row, col = a[k:k + 1, :], a[:, k:k + 1]
        scale = 1.0 / a[k:k + 1, k:k + 1]
        scaled = jnp.where(lane_one == k, scale, row * scale)
        a = jnp.where(lane == k, 0.0, a) - col * scaled
        g = k // 8 * 8
        middle = jnp.where(sub == k - g, jnp.broadcast_to(scaled, (8, n)), a[g:g + 8])
        a = jnp.concatenate([part for part in (a[:g], middle, a[g + 8:]) if part.shape[0]], axis=0)
        if k % PIVOTS == PIVOTS - 1:
            yield None
    yield a


def exact_dot(a, b):
    return jnp.dot(a, b, precision=lax.Precision.HIGHEST, preferred_element_type=jnp.float32)


def inverse_of_gram(fall, fall_t, gram, inverse):
    fall_t[...] = fall[...].T
    yield
    gram[...] = jnp.dot(fall_t[...], fall[...], preferred_element_type=jnp.float32)
    yield
    n = FACTORS // 2
    first = None
    for first in invert(gram[:n, :n]):
        yield
    upper, lower = gram[:n, n:], gram[n:, :n]
    right, left = exact_dot(first, upper), exact_dot(lower, first)
    schur = gram[n:, n:] - exact_dot(lower, right)
    yield
    second = None
    for second in invert(schur):
        yield
    off = -exact_dot(right, second)
    inverse[:n, :n] = first - exact_dot(off, left)
    inverse[:n, n:] = off
    inverse[n:, :n] = -exact_dot(second, left)
    inverse[n:, n:] = second
    yield


def residual_of(block, fall, fall_t, inverse):
    cross = jnp.dot(fall_t[...], block, preferred_element_type=jnp.float32)
    exposure = exact_dot(inverse[...], cross)
    fitted = jnp.dot(fall[...], exposure.astype(jnp.bfloat16), preferred_element_type=jnp.float32)
    return exposure, (block.astype(jnp.float32) - fitted).astype(jnp.bfloat16)


def own_residuals(mine, fall, fall_t, inverse, loadings, mine_t):
    for side in range(SIDES):
        part = pl.ds(side * SIDE, SIDE)
        exposure, residual = residual_of(mine[:, part], fall, fall_t, inverse)
        loadings[:, part] = exposure
        mine_t[part, :] = residual.T
        yield


def early_columns(prepare, cols, fall, fall_t, inverse, mine_t, first_side, residuals):
    for core in range(2):
        if core == 0:
            prepare()
        part = pl.ds(core * ASSET_BLOCK, SIDE)
        residuals[core] = residual_of(cols[:, part], fall, fall_t, inverse)[1]
        yield
    for core in range(2):
        for block in range(2):
            rows = pl.ds(block * SIDE, SIDE)
            first_side[core, rows, :] = jnp.dot(
                mine_t[rows, :], residuals[core], preferred_element_type=jnp.float32) * (1.0 / DAYS)
            yield


def gather_kernel(f_hbm, x_hbm, cols, fall, fall_t, inverse, loadings, mine_t, first_side,
                  mine, residuals, gram, load_sem, f_send, f_recv, f_pair,
                  m_send, m_recv, c_send, c_recv, c_pair, fp_send, cp_send):
    day, asset = lax.axis_index("days"), lax.axis_index("assets")
    x, h = day // 2, day % 2
    z, l, c = asset // 4, (asset // 2) % 2, asset % 2
    dl, dz = (l + h) % 2, (z - x + 4) % 4
    is_root = jnp.logical_and(dl == 0, dz == 0)
    right_is_root = jnp.logical_and(dl == 0, dz == 1)
    left_is_root = jnp.logical_and(dl == 0, dz == 3)
    partner_is_root = jnp.logical_and(dl == 1, dz == 0)

    def among(roles):
        return functools.reduce(jnp.logical_or, [jnp.logical_and(dl == i, dz == j) for i, j in roles])

    def day_of(dx, dh):
        return lax.rem(x + dx + 4, 4) * 2 + lax.rem(h + dh, 2)

    def asset_of(link):
        if link == "z+":
            return lax.rem(z + 1, 4) * 4 + l * 2 + c
        if link == "z-":
            return lax.rem(z + 3, 4) * 4 + l * 2 + c
        return z * 4 + (1 - l) * 2 + c

    sibling = z * 4 + l * 2 + 1 - c
    own_rows = pl.ds(pl.multiple_of(day * DAY_BLOCK, DAY_BLOCK), DAY_BLOCK)
    load_x = pltpu.make_async_copy(x_hbm, mine.at[own_rows], load_sem.at[0])
    load_f = pltpu.make_async_copy(f_hbm, fall.at[own_rows], load_sem.at[1])
    load_f.start()
    load_x.start()

    barrier = pltpu.get_barrier_semaphore()
    greeted = [(day_of(0, 1), asset), (day_of(1, 0), asset), (day_of(-1, 0), asset)]
    greeted += [(day, asset_of("z+")), (day, asset_of("z-")), (day, asset_of("y")), (day, sibling)]
    for d, a in greeted:
        pl.semaphore_signal(barrier, inc=1, device_id={"days": d, "assets": a}, device_id_type=MESH)
    pl.semaphore_wait(barrier, len(greeted))
    load_f.wait()
    load_x.wait()

    pending = []

    def send(src, dst, ssem, rsem, d, a, when=None):
        copy = pltpu.make_async_remote_copy(
            src_ref=src, dst_ref=dst, send_sem=ssem, recv_sem=rsem,
            device_id={"days": d, "assets": a}, device_id_type=MESH)
        if when is None:
            copy.start()
        else:
            pl.when(when)(copy.start)
        pending.append((when, copy))

    def arrived(ref, rsem):
        pltpu.make_async_remote_copy(
            src_ref=ref, dst_ref=ref, send_sem=load_sem.at[0], recv_sem=rsem,
            device_id={"days": day, "assets": sibling}, device_id_type=MESH).wait_recv()

    def f_rows(dx, dh, core):
        return fall.at[pl.ds(pl.multiple_of(day_of(dx, dh) * DAY_BLOCK + core * HALF, 32), HALF)]

    def part_rows(dx, dh, p):
        return pl.ds(pl.multiple_of(day_of(dx, dh) * DAY_BLOCK + p % THIRDS * PART, PART), PART)

    def m_part(dx, dh, p):
        return mine.at[part_rows(dx, dh, p), pl.ds(p // THIRDS * SIDE, SIDE)]

    def c_part(dx, dh, p, core):
        lanes = pl.ds(pl.multiple_of(core * ASSET_BLOCK + p // THIRDS * SIDE, SIDE), SIDE)
        return cols.at[part_rows(dx, dh, p), lanes]

    n_f, n_m, n_c = [0], [0], [0]

    def send_f(dx, dh, to):
        ref = f_rows(dx, dh, c)
        send(ref, ref, f_send.at[n_f[0]], f_recv.at[day_of(dx, dh)], day_of(*to), asset)
        n_f[0] += 1

    def send_m(dx, dh, p, to, when=None):
        ref = m_part(dx, dh, p)
        send(ref, ref, m_send.at[n_m[0]], m_recv.at[day_of(dx, dh), p], day_of(*to), asset, when)
        n_m[0] += 1

    def pair_f(dx, dh):
        ref = f_rows(dx, dh, c)
        arrived(ref, f_recv.at[day_of(dx, dh)])
        send(ref, ref, fp_send.at[day_of(dx, dh)], f_pair.at[day_of(dx, dh)], day, sibling)

    def root_sends(dx, dh, p):
        link = TREES[p % THIRDS][0][0]
        src, dst = m_part(dx, dh, p), c_part(dx, dh, p, c)
        send(src, dst, c_send.at[n_c[0]], c_recv.at[day_of(dx, dh), p], day, asset_of(link), is_root)
        n_c[0] += 1
        send(src, dst, cp_send.at[day_of(dx, dh), p], c_pair.at[day_of(dx, dh), p], day, sibling, is_root)

    def relay_mine(dx, dh, p):
        arrived(m_part(dx, dh, p), m_recv.at[day_of(dx, dh), p])
        right, left = (None, None) if dh == 0 else (jnp.logical_not(right_is_root), jnp.logical_not(left_is_root))
        if (dx, dh) == (0, 1):
            send_m(dx, dh, p, (1, 0))
            send_m(dx, dh, p, (-1, 0))
        if dx == -1 and forward_right(dh, p):
            send_m(dx, dh, p, (1, 0), right)
        if dx == 1 and not forward_right(dh, p):
            send_m(dx, dh, p, (-1, 0), left)
        if (dx, dh) == (2, 0):
            send_m(dx, dh, p, (0, 1), partner_is_root)
        root_sends(dx, dh, p)

    def relay_cols(dx, dh, p, depth):
        ref = c_part(dx, dh, p, c)
        tree = p % THIRDS
        here = DEPTHS[tree][depth - 1]
        pl.when(among(here))(lambda: arrived(ref, c_recv.at[day_of(dx, dh), p]))
        for link, roles in TREES[tree]:
            roles = [role for role in roles if role in here]
            if roles:
                send(ref, ref, c_send.at[n_c[0]], c_recv.at[day_of(dx, dh), p], day, asset_of(link), among(roles))
                n_c[0] += 1
        send(ref, ref, cp_send.at[day_of(dx, dh), p], c_pair.at[day_of(dx, dh), p], day, sibling, among(here))

    def fill(side):
        @pl.when(is_root)
        def _():
            lanes = pl.ds(pl.multiple_of(c * ASSET_BLOCK + side * SIDE, SIDE), SIDE)

            @pl.loop(0, DAYS // 64)
            def _(i):
                rows = pl.ds(pl.multiple_of(i * 64, 64), 64)
                cols[rows, lanes] = mine[rows, pl.ds(side * SIDE, SIDE)]

        for dx, dh in CHUNKS:
            for p in range(side * THIRDS, (side + 1) * THIRDS):
                arrived(c_part(dx, dh, p, 1 - c), c_pair.at[day_of(dx, dh), p])

    factor_steps = iter((
        lambda: (send_f(0, 0, (0, 1)), send_f(0, 0, (1, 0)), send_f(0, 0, (-1, 0))),
        lambda: (pair_f(0, 1), send_f(0, 1, (1, 0)), send_f(0, 1, (-1, 0))),
        lambda: (pair_f(1, 0), pair_f(-1, 0), send_f(-1, 0, (1, 0))),
        lambda: (pair_f(1, 1), send_f(1, 1, (-1, 0)), pair_f(-1, 1)),
        lambda: (pair_f(2, 0), pair_f(2, 1),
                 [arrived(f_rows(dx, dh, 1 - c), f_pair.at[day_of(dx, dh)]) for dx, dh in CHUNKS[1:]]),
    ))
    compute = itertools.chain(
        inverse_of_gram(fall, fall_t, gram, inverse),
        own_residuals(mine, fall, fall_t, inverse, loadings, mine_t),
        early_columns(lambda: fill(0), cols, fall, fall_t, inverse, mine_t, first_side, residuals),
    )
    for kind, a, *rest in ORDER:
        if kind == 0 and LINKS[a] == "root":
            root_sends(0, 0, *rest)
        elif kind == 0:
            send_m(0, 0, *rest, {"h": (0, 1), "x+": (1, 0), "x-": (-1, 0)}[LINKS[a]])
        elif kind == 1:
            relay_mine(*CHUNKS[a], *rest)
        elif kind == 2:
            relay_cols(*CHUNKS[a], *rest)
        elif kind == 3:
            next(factor_steps)()
        else:
            next(compute)
    fill(1)
    for _ in compute:
        pass

    for when, copy in pending:
        if when is None:
            copy.wait_send()
        else:
            pl.when(when)(copy.wait_send)


def gather(factors, returns):
    dma = pltpu.SemaphoreType.DMA
    shape = jax.ShapeDtypeStruct
    return pl.pallas_call(
        gather_kernel,
        out_shape=(
            shape((DAYS, 2 * ASSET_BLOCK), jnp.bfloat16),
            shape((DAYS, FACTORS), jnp.bfloat16),
            shape((FACTORS, DAYS), jnp.bfloat16),
            shape((FACTORS, FACTORS), jnp.float32),
            shape((FACTORS, ASSET_BLOCK), jnp.float32),
            shape((ASSET_BLOCK, DAYS), jnp.bfloat16),
            shape((2, ASSET_BLOCK, SIDE), jnp.float32),
        ),
        in_specs=[pl.BlockSpec(memory_space=pl.ANY)] * 2,
        out_specs=(pl.BlockSpec(memory_space=pltpu.VMEM),) * 7,
        scratch_shapes=[
            pltpu.VMEM((DAYS, ASSET_BLOCK), jnp.bfloat16),
            pltpu.VMEM((2, DAYS, SIDE), jnp.bfloat16),
            pltpu.VMEM((FACTORS, FACTORS), jnp.float32),
            dma((2,)), dma((7,)), dma((8,)), dma((8,)), dma((10 * PARTS,)), dma((8, PARTS)),
            dma((8 * PARTS * 7,)), dma((8, PARTS)), dma((8, PARTS)), dma((8,)), dma((8, PARTS)),
        ],
        compiler_params=pltpu.CompilerParams(
            collective_id=0, has_side_effects=True, vmem_limit_bytes=36 * 2**20),
        name="gather",
    )(factors, returns)


def covariance_kernel(cols, fall, fall_t, inverse, loadings, mine_t, first_side, loadings_out, covariance, stage, sems):
    copies = [pltpu.make_async_copy(loadings, loadings_out, sems.at[0])]
    for core in range(2):
        lanes = pl.ds(core * ASSET_BLOCK, SIDE)
        copies.append(pltpu.make_async_copy(first_side.at[core], covariance.at[:, lanes], sems.at[1 + core]))
    for copy in copies:
        copy.start()
    for core in range(2):
        lanes = pl.ds(core * ASSET_BLOCK + SIDE, SIDE)
        _, residual = residual_of(cols[:, lanes], fall, fall_t, inverse)
        for block in range(2):
            rows = pl.ds(block * SIDE, SIDE)
            stage[core, rows, :] = jnp.dot(
                mine_t[rows, :], residual, preferred_element_type=jnp.float32) * (1.0 / DAYS)
            copy = pltpu.make_async_copy(
                stage.at[core, rows], covariance.at[rows, lanes], sems.at[3 + core * 2 + block])
            copy.start()
            copies.append(copy)
    for copy in copies:
        copy.wait()


def covariances(*args):
    return pl.pallas_call(
        covariance_kernel,
        out_shape=(
            jax.ShapeDtypeStruct((FACTORS, ASSET_BLOCK), jnp.float32),
            jax.ShapeDtypeStruct((ASSET_BLOCK, 2 * ASSET_BLOCK), jnp.float32),
        ),
        in_specs=[pl.BlockSpec(memory_space=pltpu.VMEM)] * len(args),
        out_specs=(pl.BlockSpec(memory_space=pltpu.HBM),) * 2,
        scratch_shapes=[pltpu.VMEM((2, ASSET_BLOCK, SIDE), jnp.float32), pltpu.SemaphoreType.DMA((7,))],
        compiler_params=pltpu.CompilerParams(vmem_limit_bytes=24 * 2**20),
        name="covariances",
    )(*args)


def per_device(factors, returns):
    factors = pltpu.with_memory_space_constraint(factors, pltpu.HBM)
    returns = pltpu.with_memory_space_constraint(returns, pltpu.HBM)
    return covariances(*gather(factors, returns))


def solution(mesh):
    in_specs = (P("days", None), P("days", "assets"))
    out_specs = (P(None, "assets"), P("assets", "days"))
    return jax.shard_map(
        per_device, mesh=mesh, in_specs=in_specs, out_specs=out_specs, check_vma=False
    )
```

time: 117 us -> 91.7 us (0.78); the launches traced: 115 us -> 91.6 us
  Pallas kernels: 114 us -> 90.8 us
    pallas_call x1, Pallas kernels: 28.3 us -> 7.48 us  [covariances(): pl.pallas_call(covariance_kernel, out_shape=(jax.ShapeDtypeStruct((FACTOR...]
    pallas_call x1, Pallas kernels: 85.9 us -> 83.3 us  [gather(): pl.pallas_call(gather_kernel, out_shape=(shape((DAYS, 2 * ASSET_BLOCK), j...]
where the time goes in v3:
time: 91.7 us; the launch traced here: 91.6 us
  Pallas kernels  90.8 us (99%)
    pallas_call x1, Pallas kernels, gather(): pl.pallas_call(gather_kernel, out_shape=(shape((DAYS, 2 * ASSET_BLOCK), j...  83.3 us
    pallas_call x1, Pallas kernels, covariances(): pl.pallas_call(covariance_kernel, out_shape=(jax.ShapeDtypeStruct((FACTOR...  7.48 us

profile of v3, /device:TPU:5, one launch (start us, length us, event | category | flops | bytes accessed | tf_op | source)
XLA Modules:
  0.0 91.6 jit_solution(10823893935624566337)
XLA Ops:
  0.6 83.3 %gather.1 = (bf16[1536,2048]{1,0:T(8,128)(2,1)S(1)}, bf16[1536,256]{1,0:T(8,128)(2,1)S(1)}, bf16[256,1536]{1,0:T(8,128)(2,1)S(1)}, f32[256,256]{1,0:T(8,128)S(1)...) custom-call(bf16[192,256]{1,0:T(8,128)(2,1)} %f_hbm.1, bf16[192,1024]{1,0:T(8,128)(2,1)} %x_hbm.1), custom_call_target="tpu_custom_call" | custom-call | tf_op jit(solution)/shard_map/gather/pallas_call | solution.py:335
  83.9 7.5 %covariances.1 = (f32[256,1024]{1,0:T(8,128)}, f32[1024,2048]{1,0:T(8,128)}) custom-call(bf16[1536,2048]{1,0:T(8,128)(2,1)S(1)} %get-tuple-element.9.cols, bf16[1536,256]{1,0:T(8,128)(2,1)S(1)} %get-tuple-element.10.fall, bf16[256,1536]{1,0:T(8,128)(2,1)S(1)} %get-tuple-element.11.fall_t, f32[256,256]{1,0:T(8,128)S(1)} %get-tuple-element.12.inverse, ...), custom_call_target="tpu_custom_call" | custom-call | tf_op jit(solution)/shard_map/covariances/pallas_call | solution.py:384

commit v4 on v3

--- a/solution.py
+++ b/solution.py
@@ -34,67 +34,76 @@
 
 LINKS = ("h", "x+", "x-", "root")
 ORDER = (
-    (3, 0), (0, 1, 0), (0, 2, 0), (0, 3, 0), (0, 0, 0), (0, 1, 1), (0, 2, 1), (0, 3, 1),
-    (0, 0, 1), (0, 1, 2), (0, 2, 2), (0, 3, 2), (0, 0, 2), (2, 0, 0, 1), (2, 0, 1, 1), (3, 1),
-    (0, 1, 3), (0, 2, 3), (0, 3, 3), (0, 0, 3), (0, 1, 4), (0, 2, 4), (0, 3, 4), (0, 0, 4),
-    (0, 1, 5), (0, 2, 5), (0, 3, 5), (0, 0, 5), (1, 2, 0), (1, 4, 0), (1, 2, 1), (1, 4, 1),
-    (2, 0, 2, 1), (1, 2, 2), (1, 4, 2), (3, 2), (1, 1, 0), (2, 0, 0, 2), (2, 0, 1, 2), (2, 0, 3, 1),
-    (2, 0, 4, 1), (1, 2, 3), (1, 4, 3), (1, 1, 1), (1, 1, 2), (2, 0, 2, 2), (2, 4, 0, 1), (2, 2, 0, 1),
-    (2, 4, 1, 1), (1, 2, 4), (2, 2, 1, 1), (1, 4, 4), (2, 0, 5, 1), (1, 1, 3), (2, 0, 0, 3), (2, 1, 0, 1),
-    (2, 0, 1, 3), (2, 0, 3, 2), (2, 1, 1, 1), (2, 0, 4, 2), (1, 2, 5), (1, 4, 5), (1, 1, 4), (2, 0, 2, 3),
-    (1, 1, 5), (1, 6, 2), (1, 6, 0), (2, 4, 0, 2), (2, 4, 1, 2), (2, 0, 5, 2), (2, 4, 3, 1), (2, 2, 3, 1),
-    (2, 4, 4, 1), (2, 2, 4, 1), (1, 3, 0), (1, 6, 1), (3, 3), (2, 0, 3, 3), (2, 0, 4, 3), (2, 0, 2, 4),
-    (2, 2, 0, 2), (2, 2, 1, 2), (2, 1, 4, 1), (2, 0, 0, 4), (1, 3, 1), (2, 4, 2, 1), (2, 1, 0, 2), (2, 1, 1, 2),
-    (1, 5, 0), (2, 6, 1, 1), (2, 0, 5, 3), (2, 0, 1, 4), (2, 4, 0, 3), (1, 3, 2), (2, 2, 2, 1), (2, 0, 3, 4),
-    (2, 1, 3, 1), (2, 6, 0, 1), (2, 4, 1, 3), (2, 4, 3, 2), (2, 4, 4, 2), (1, 6, 3), (2, 3, 0, 1), (1, 3, 3),
-    (2, 2, 0, 3), (2, 3, 1, 1), (2, 2, 1, 3), (2, 1, 2, 1), (2, 4, 2, 2), (2, 0, 4, 4), (2, 1, 0, 3), (1, 5, 1),
-    (2, 1, 1, 3), (2, 2, 3, 2), (2, 4, 5, 1), (1, 6, 5), (2, 0, 5, 4), (2, 4, 0, 4), (2, 2, 4, 2), (2, 1, 3, 2),
-    (2, 1, 4, 2), (1, 3, 4), (1, 5, 2), (2, 4, 3, 3), (2, 2, 5, 1), (2, 1, 5, 1), (2, 2, 2, 2), (2, 2, 0, 4),
-    (1, 6, 4), (2, 6, 0, 2), (2, 6, 1, 2), (2, 4, 1, 4), (2, 1, 2, 2), (1, 3, 5), (2, 6, 2, 1), (2, 1, 0, 4),
-    (2, 2, 3, 3), (1, 5, 3), (2, 3, 0, 2), (2, 3, 1, 2), (2, 2, 1, 4), (2, 1, 1, 4), (2, 4, 5, 2), (2, 4, 3, 4),
-    (2, 2, 5, 2), (2, 1, 3, 3), (1, 7, 1), (3, 4), (4, 0), (2, 2, 3, 4), (4, 1), (2, 4, 4, 3),
-    (2, 6, 0, 3), (4, 2), (2, 2, 4, 3), (2, 7, 1, 1), (2, 5, 1, 1), (2, 3, 4, 1), (4, 3), (2, 1, 4, 3),
-    (4, 4), (2, 4, 2, 3), (4, 5), (2, 2, 2, 3), (4, 6), (2, 1, 2, 3), (4, 7), (4, 8),
-    (4, 9), (2, 4, 2, 4), (4, 10), (4, 11), (4, 12), (4, 13), (4, 14), (4, 15),
-    (2, 1, 3, 4), (4, 16), (2, 6, 0, 4), (1, 7, 2), (1, 5, 4), (4, 17), (4, 18), (4, 19),
-    (2, 3, 0, 3), (1, 7, 0), (1, 5, 5), (4, 20), (2, 6, 4, 1), (2, 1, 5, 2), (2, 7, 2, 1), (2, 3, 2, 1),
-    (1, 7, 4), (4, 21), (2, 4, 5, 3), (2, 2, 5, 3), (2, 6, 2, 2), (1, 7, 3), (2, 6, 1, 3), (1, 7, 5),
-    (2, 7, 1, 2), (2, 3, 1, 3), (2, 5, 1, 2), (2, 7, 0, 1), (2, 3, 4, 2), (2, 5, 0, 1), (2, 6, 3, 1), (4, 22),
-    (2, 3, 3, 1), (4, 23), (2, 3, 0, 4), (2, 5, 2, 1), (2, 4, 4, 4), (4, 24), (2, 7, 3, 1), (2, 5, 3, 1),
-    (2, 7, 2, 2), (4, 25), (2, 7, 1, 3), (2, 7, 0, 2), (4, 26), (2, 3, 2, 2), (2, 6, 4, 2), (2, 1, 5, 3),
-    (4, 27), (2, 5, 0, 2), (2, 2, 2, 4), (2, 2, 4, 4), (2, 1, 2, 4), (4, 28), (2, 6, 2, 3), (2, 6, 3, 2),
-    (4, 29), (2, 7, 0, 3), (2, 6, 5, 1), (2, 5, 1, 3), (2, 7, 2, 3), (2, 1, 4, 4), (2, 4, 5, 4), (4, 30),
-    (2, 3, 4, 3), (2, 3, 3, 2), (2, 5, 0, 3), (2, 7, 5, 1), (4, 31), (2, 6, 1, 4), (2, 2, 5, 4), (2, 5, 2, 2),
-    (2, 5, 4, 1), (4, 32), (2, 6, 3, 3), (2, 3, 5, 1), (2, 7, 4, 1), (4, 33), (2, 7, 3, 2), (2, 7, 0, 4),
-    (2, 3, 2, 3), (4, 34), (2, 3, 1, 4), (2, 1, 5, 4), (2, 7, 1, 4), (4, 35), (2, 5, 0, 4), (2, 6, 4, 3),
-    (2, 3, 3, 3), (2, 5, 3, 2), (4, 36), (4, 37), (2, 6, 5, 2), (2, 5, 4, 2), (2, 5, 1, 4), (2, 7, 5, 2),
-    (2, 6, 3, 4), (4, 38), (2, 3, 4, 4), (2, 5, 2, 3), (2, 6, 2, 4), (2, 5, 5, 1), (2, 7, 4, 2), (2, 7, 3, 3),
-    (2, 3, 3, 4), (4, 39), (2, 6, 4, 4), (2, 7, 2, 4), (2, 5, 4, 3), (2, 3, 2, 4), (2, 6, 5, 3), (2, 5, 2, 4),
-    (4, 40), (2, 7, 5, 3), (2, 7, 4, 3), (2, 5, 3, 3), (2, 3, 5, 2), (2, 5, 5, 2), (2, 7, 3, 4), (2, 5, 4, 4),
-    (4, 41), (4, 42), (2, 6, 5, 4), (2, 3, 5, 3), (2, 5, 3, 4), (2, 7, 4, 4), (4, 43), (2, 7, 5, 4),
-    (4, 44), (4, 45), (2, 3, 5, 4), (2, 5, 5, 3), (2, 5, 5, 4),
+    (3, 0), (0, 2, 1), (0, 2, 2), (0, 1, 1), (0, 2, 0), (0, 0, 1), (0, 0, 0), (0, 1, 0),
+    (0, 3, 3), (0, 2, 3), (0, 1, 3), (0, 1, 4), (0, 3, 5), (0, 3, 1), (0, 1, 2), (2, 0, 1, 1),
+    (0, 3, 2), (0, 2, 4), (2, 0, 3, 1), (1, 4, 1), (0, 3, 0), (2, 0, 5, 1), (0, 0, 2), (3, 1),
+    (0, 0, 4), (2, 0, 3, 2), (2, 4, 0, 1), (1, 2, 2), (1, 4, 0), (1, 1, 0), (1, 2, 1), (3, 2),
+    (0, 1, 5), (2, 0, 1, 3), (2, 0, 1, 2), (0, 3, 4), (1, 4, 4), (2, 4, 1, 1), (1, 4, 3), (1, 4, 2),
+    (0, 0, 3), (2, 4, 0, 2), (1, 1, 1), (0, 2, 5), (2, 2, 1, 2), (2, 0, 2, 1), (2, 4, 1, 2), (2, 4, 3, 1),
+    (2, 2, 0, 1), (2, 2, 2, 1), (2, 0, 2, 2), (2, 2, 1, 1), (1, 2, 4), (2, 1, 0, 1), (2, 4, 2, 1), (1, 2, 0),
+    (2, 0, 4, 1), (1, 2, 3), (3, 3), (2, 0, 0, 1), (2, 1, 1, 1), (1, 1, 2), (2, 4, 2, 2), (0, 0, 5),
+    (1, 6, 1), (1, 5, 0), (1, 3, 1), (1, 1, 4), (2, 1, 2, 1), (2, 2, 1, 3), (1, 6, 0), (2, 6, 1, 1),
+    (1, 2, 5), (1, 6, 2), (1, 1, 3), (1, 3, 0), (2, 2, 4, 1), (2, 1, 1, 2), (2, 2, 0, 2), (3, 4),
+    (2, 2, 3, 1), (4, 0), (1, 3, 2), (2, 0, 0, 2), (2, 4, 3, 2), (2, 3, 1, 1), (2, 4, 4, 1), (2, 2, 2, 2),
+    (2, 2, 5, 1), (2, 5, 0, 1), (2, 0, 4, 2), (2, 1, 2, 2), (1, 6, 4), (4, 1), (2, 4, 0, 3), (2, 1, 4, 1),
+    (2, 4, 2, 3), (4, 2), (2, 6, 2, 1), (4, 3), (2, 4, 1, 3), (2, 0, 2, 3), (2, 6, 0, 1), (2, 4, 1, 4),
+    (2, 0, 3, 3), (1, 1, 5), (2, 2, 4, 2), (2, 2, 3, 2), (2, 0, 5, 2), (2, 2, 5, 2), (4, 4), (2, 3, 1, 2),
+    (1, 4, 5), (2, 5, 0, 2), (1, 6, 3), (4, 5), (4, 6), (2, 0, 4, 3), (2, 6, 4, 1), (2, 3, 2, 1),
+    (2, 2, 1, 4), (1, 3, 4), (2, 6, 0, 2), (4, 7), (4, 8), (2, 4, 4, 2), (4, 9), (2, 1, 0, 2),
+    (2, 3, 0, 1), (2, 6, 1, 2), (2, 3, 2, 2), (2, 3, 0, 2), (1, 7, 1), (1, 5, 2), (4, 10), (1, 3, 3),
+    (1, 7, 0), (2, 6, 3, 1), (2, 6, 4, 2), (2, 2, 2, 3), (1, 5, 1), (4, 11), (2, 1, 3, 1), (2, 2, 4, 3),
+    (2, 3, 4, 2), (2, 3, 4, 1), (2, 6, 2, 2), (4, 12), (2, 4, 5, 1), (2, 0, 0, 3), (2, 0, 0, 4), (2, 4, 3, 3),
+    (2, 1, 2, 3), (1, 6, 5), (4, 13), (1, 7, 2), (2, 5, 2, 1), (2, 1, 5, 1), (4, 14), (4, 15),
+    (2, 4, 2, 4), (4, 16), (2, 7, 1, 1), (2, 2, 0, 3), (1, 5, 3), (2, 5, 2, 2), (1, 5, 4), (4, 17),
+    (4, 18), (4, 19), (4, 20), (2, 4, 5, 2), (2, 7, 0, 1), (4, 21), (2, 7, 0, 2), (4, 22),
+    (2, 6, 0, 3), (2, 0, 3, 4), (2, 7, 2, 1), (2, 6, 5, 1), (2, 5, 1, 1), (2, 2, 2, 4), (2, 2, 5, 3), (2, 5, 1, 2),
+    (2, 5, 3, 1), (2, 2, 3, 3), (2, 5, 0, 3), (1, 3, 5), (2, 7, 1, 2), (4, 23), (2, 1, 5, 2), (2, 7, 2, 2),
+    (2, 1, 3, 2), (4, 24), (4, 25), (4, 26), (2, 0, 4, 4), (2, 3, 3, 2), (2, 5, 3, 2), (2, 3, 1, 3),
+    (2, 5, 4, 1), (2, 6, 5, 2), (2, 3, 3, 1), (2, 4, 0, 4), (2, 3, 2, 3), (2, 3, 1, 4), (2, 3, 5, 1), (4, 27),
+    (4, 28), (2, 1, 0, 3), (2, 0, 5, 3), (2, 6, 4, 3), (4, 29), (2, 1, 4, 2), (4, 30), (4, 31),
+    (4, 32), (1, 7, 4), (4, 33), (1, 5, 5), (2, 3, 5, 2), (2, 1, 1, 3), (2, 2, 0, 4), (2, 2, 4, 4),
+    (2, 5, 2, 3), (1, 7, 3), (4, 34), (2, 6, 1, 3), (2, 6, 3, 2), (2, 6, 2, 3), (2, 4, 4, 3), (4, 35),
+    (2, 0, 2, 4), (2, 1, 1, 4), (2, 5, 5, 1), (2, 5, 4, 2), (2, 7, 4, 1), (4, 36), (2, 4, 5, 3), (4, 37),
+    (2, 5, 5, 2), (2, 7, 0, 3), (2, 3, 0, 3), (1, 7, 5), (4, 38), (2, 1, 5, 3), (2, 3, 0, 4), (2, 4, 3, 4),
+    (2, 7, 1, 3), (2, 7, 4, 2), (2, 7, 3, 1), (2, 0, 5, 4), (2, 7, 3, 2), (2, 6, 0, 4), (2, 1, 0, 4), (2, 7, 5, 1),
+    (2, 5, 1, 3), (4, 39), (2, 5, 1, 4), (2, 6, 1, 4), (2, 1, 3, 3), (2, 5, 0, 4), (2, 5, 2, 4), (2, 2, 3, 4),
+    (2, 4, 4, 4), (2, 0, 1, 4), (2, 7, 1, 4), (2, 7, 0, 4), (2, 2, 5, 4), (2, 3, 4, 3), (2, 7, 2, 3), (2, 6, 2, 4),
+    (2, 3, 3, 3), (2, 1, 2, 4), (2, 7, 2, 4), (2, 7, 5, 2), (2, 5, 3, 3), (2, 3, 2, 4), (4, 40), (2, 6, 5, 3),
+    (2, 3, 3, 4), (4, 41), (2, 1, 4, 3), (4, 42), (2, 1, 4, 4), (2, 3, 4, 4), (2, 6, 4, 4), (2, 5, 5, 3),
+    (4, 43), (2, 3, 5, 3), (2, 1, 5, 4), (2, 5, 3, 4), (2, 4, 5, 4), (2, 5, 5, 4), (2, 5, 4, 3), (4, 44),
+    (2, 6, 5, 4), (2, 7, 3, 3), (2, 7, 3, 4), (4, 45), (2, 7, 4, 3), (2, 1, 3, 4), (2, 7, 4, 4), (2, 6, 3, 3),
+    (2, 7, 5, 4), (2, 6, 3, 4), (2, 5, 4, 4), (2, 3, 5, 4), (2, 7, 5, 3),
 )
 
 
 def forward_right(dh, p):
     return p % THIRDS < (THIRDS + 1 - dh) // 2
+
+
+def with_row(a, k, row):
+    n = a.shape[1]
+    g = k // 8 * 8
+    sub = lax.broadcasted_iota(jnp.int32, (8, n), 0)
+    middle = jnp.where(sub == k - g, jnp.broadcast_to(row, (8, n)), a[g:g + 8])
+    return jnp.concatenate([part for part in (a[:g], middle, a[g + 8:]) if part.shape[0]], axis=0)
 
 
 def invert(a):
     n = a.shape[0]
     lane = lax.broadcasted_iota(jnp.int32, (n, n), 1)
     lane_one = lax.broadcasted_iota(jnp.int32, (1, n), 1)
-    sub = lax.broadcasted_iota(jnp.int32, (8, n), 0)
-    for k in range(n):
-        row, col = a[k:k + 1, :], a[:, k:k + 1]
-        scale = 1.0 / a[k:k + 1, k:k + 1]
-        scaled = jnp.where(lane_one == k, scale, row * scale)
-        a = jnp.where(lane == k, 0.0, a) - col * scaled
-        g = k // 8 * 8
-        middle = jnp.where(sub == k - g, jnp.broadcast_to(scaled, (8, n)), a[g:g + 8])
-        a = jnp.concatenate([part for part in (a[:g], middle, a[g + 8:]) if part.shape[0]], axis=0)
-        if k % PIVOTS == PIVOTS - 1:
-            yield None
+    for start in range(0, n, PIVOTS):
+        spread = [jnp.broadcast_to(a[:, k:k + 1], (n, n)) for k in range(start, start + PIVOTS)]
+        for j in range(PIVOTS):
+            k = start + j
+            col = spread[j]
+            scale = 1.0 / col[k:k + 1, :]
+            row = jnp.where(lane_one == k, scale, a[k:k + 1, :] * scale)
+            a = with_row(jnp.where(lane == k, 0.0, a) - col * row, k, row)
+            for i in range(j + 1, PIVOTS):
+                row = spread[i][k:k + 1, :] * scale
+                spread[i] = with_row(spread[i] - col * row, k, row)
+        yield None
     yield a
 
 

time: 91.7 us -> 77.2 us (0.84); the launches traced: 91.6 us -> 75.8 us
  Pallas kernels: 90.8 us -> 75 us
    pallas_call x1, Pallas kernels: 83.3 us -> 67.5 us  [gather(): pl.pallas_call(gather_kernel, out_shape=(shape((DAYS, 2 * ASSET_BLOCK), j...]
where the time goes in v4:
time: 77.2 us; the launch traced here: 75.8 us
  Pallas kernels  75 us (97%)
  between operations  0.82 us (1%)
    pallas_call x1, Pallas kernels, gather(): pl.pallas_call(gather_kernel, out_shape=(shape((DAYS, 2 * ASSET_BLOCK), j...  67.5 us
    pallas_call x1, Pallas kernels, covariances(): pl.pallas_call(covariance_kernel, out_shape=(jax.ShapeDtypeStruct((FACTOR...  7.46 us

profile of v4, /device:TPU:5, one launch (start us, length us, event | category | flops | bytes accessed | tf_op | source)
XLA Modules:
  0.0 75.8 jit_solution(13272496270104662248)
XLA Ops:
  0.6 67.5 %gather.1 = (bf16[1536,2048]{1,0:T(8,128)(2,1)S(1)}, bf16[1536,256]{1,0:T(8,128)(2,1)S(1)}, bf16[256,1536]{1,0:T(8,128)(2,1)S(1)}, f32[256,256]{1,0:T(8,128)S(1)...) custom-call(bf16[192,256]{1,0:T(8,128)(2,1)} %f_hbm.1, bf16[192,1024]{1,0:T(8,128)(2,1)} %x_hbm.1), custom_call_target="tpu_custom_call" | custom-call | tf_op jit(solution)/shard_map/gather/pallas_call | solution.py:344
  68.1 7.5 %covariances.1 = (f32[256,1024]{1,0:T(8,128)}, f32[1024,2048]{1,0:T(8,128)}) custom-call(bf16[1536,2048]{1,0:T(8,128)(2,1)S(1)} %get-tuple-element.9.cols, bf16[1536,256]{1,0:T(8,128)(2,1)S(1)} %get-tuple-element.10.fall, bf16[256,1536]{1,0:T(8,128)(2,1)S(1)} %get-tuple-element.11.fall_t, f32[256,256]{1,0:T(8,128)S(1)} %get-tuple-element.12.inverse, ...), custom_call_target="tpu_custom_call" | custom-call | tf_op jit(solution)/shard_map/covariances/pallas_call | solution.py:393

commit v5 on v4

--- a/solution.py
+++ b/solution.py
@@ -17,7 +17,9 @@
 THIRDS, SIDES = 3, 2
 PARTS = THIRDS * SIDES
 PART = DAY_BLOCK // THIRDS
-SIDE = ASSET_BLOCK // SIDES
+SIDE_WIDTH = (512, 512)
+SIDE_AT = (0, SIDE_WIDTH[0])
+ROWS = 512
 PIVOTS = 8
 
 TREES = (
@@ -34,45 +36,46 @@
 
 LINKS = ("h", "x+", "x-", "root")
 ORDER = (
-    (3, 0), (0, 2, 1), (0, 2, 2), (0, 1, 1), (0, 2, 0), (0, 0, 1), (0, 0, 0), (0, 1, 0),
-    (0, 3, 3), (0, 2, 3), (0, 1, 3), (0, 1, 4), (0, 3, 5), (0, 3, 1), (0, 1, 2), (2, 0, 1, 1),
-    (0, 3, 2), (0, 2, 4), (2, 0, 3, 1), (1, 4, 1), (0, 3, 0), (2, 0, 5, 1), (0, 0, 2), (3, 1),
-    (0, 0, 4), (2, 0, 3, 2), (2, 4, 0, 1), (1, 2, 2), (1, 4, 0), (1, 1, 0), (1, 2, 1), (3, 2),
-    (0, 1, 5), (2, 0, 1, 3), (2, 0, 1, 2), (0, 3, 4), (1, 4, 4), (2, 4, 1, 1), (1, 4, 3), (1, 4, 2),
-    (0, 0, 3), (2, 4, 0, 2), (1, 1, 1), (0, 2, 5), (2, 2, 1, 2), (2, 0, 2, 1), (2, 4, 1, 2), (2, 4, 3, 1),
-    (2, 2, 0, 1), (2, 2, 2, 1), (2, 0, 2, 2), (2, 2, 1, 1), (1, 2, 4), (2, 1, 0, 1), (2, 4, 2, 1), (1, 2, 0),
-    (2, 0, 4, 1), (1, 2, 3), (3, 3), (2, 0, 0, 1), (2, 1, 1, 1), (1, 1, 2), (2, 4, 2, 2), (0, 0, 5),
-    (1, 6, 1), (1, 5, 0), (1, 3, 1), (1, 1, 4), (2, 1, 2, 1), (2, 2, 1, 3), (1, 6, 0), (2, 6, 1, 1),
-    (1, 2, 5), (1, 6, 2), (1, 1, 3), (1, 3, 0), (2, 2, 4, 1), (2, 1, 1, 2), (2, 2, 0, 2), (3, 4),
-    (2, 2, 3, 1), (4, 0), (1, 3, 2), (2, 0, 0, 2), (2, 4, 3, 2), (2, 3, 1, 1), (2, 4, 4, 1), (2, 2, 2, 2),
-    (2, 2, 5, 1), (2, 5, 0, 1), (2, 0, 4, 2), (2, 1, 2, 2), (1, 6, 4), (4, 1), (2, 4, 0, 3), (2, 1, 4, 1),
-    (2, 4, 2, 3), (4, 2), (2, 6, 2, 1), (4, 3), (2, 4, 1, 3), (2, 0, 2, 3), (2, 6, 0, 1), (2, 4, 1, 4),
-    (2, 0, 3, 3), (1, 1, 5), (2, 2, 4, 2), (2, 2, 3, 2), (2, 0, 5, 2), (2, 2, 5, 2), (4, 4), (2, 3, 1, 2),
-    (1, 4, 5), (2, 5, 0, 2), (1, 6, 3), (4, 5), (4, 6), (2, 0, 4, 3), (2, 6, 4, 1), (2, 3, 2, 1),
-    (2, 2, 1, 4), (1, 3, 4), (2, 6, 0, 2), (4, 7), (4, 8), (2, 4, 4, 2), (4, 9), (2, 1, 0, 2),
-    (2, 3, 0, 1), (2, 6, 1, 2), (2, 3, 2, 2), (2, 3, 0, 2), (1, 7, 1), (1, 5, 2), (4, 10), (1, 3, 3),
-    (1, 7, 0), (2, 6, 3, 1), (2, 6, 4, 2), (2, 2, 2, 3), (1, 5, 1), (4, 11), (2, 1, 3, 1), (2, 2, 4, 3),
-    (2, 3, 4, 2), (2, 3, 4, 1), (2, 6, 2, 2), (4, 12), (2, 4, 5, 1), (2, 0, 0, 3), (2, 0, 0, 4), (2, 4, 3, 3),
-    (2, 1, 2, 3), (1, 6, 5), (4, 13), (1, 7, 2), (2, 5, 2, 1), (2, 1, 5, 1), (4, 14), (4, 15),
-    (2, 4, 2, 4), (4, 16), (2, 7, 1, 1), (2, 2, 0, 3), (1, 5, 3), (2, 5, 2, 2), (1, 5, 4), (4, 17),
-    (4, 18), (4, 19), (4, 20), (2, 4, 5, 2), (2, 7, 0, 1), (4, 21), (2, 7, 0, 2), (4, 22),
-    (2, 6, 0, 3), (2, 0, 3, 4), (2, 7, 2, 1), (2, 6, 5, 1), (2, 5, 1, 1), (2, 2, 2, 4), (2, 2, 5, 3), (2, 5, 1, 2),
-    (2, 5, 3, 1), (2, 2, 3, 3), (2, 5, 0, 3), (1, 3, 5), (2, 7, 1, 2), (4, 23), (2, 1, 5, 2), (2, 7, 2, 2),
-    (2, 1, 3, 2), (4, 24), (4, 25), (4, 26), (2, 0, 4, 4), (2, 3, 3, 2), (2, 5, 3, 2), (2, 3, 1, 3),
-    (2, 5, 4, 1), (2, 6, 5, 2), (2, 3, 3, 1), (2, 4, 0, 4), (2, 3, 2, 3), (2, 3, 1, 4), (2, 3, 5, 1), (4, 27),
-    (4, 28), (2, 1, 0, 3), (2, 0, 5, 3), (2, 6, 4, 3), (4, 29), (2, 1, 4, 2), (4, 30), (4, 31),
-    (4, 32), (1, 7, 4), (4, 33), (1, 5, 5), (2, 3, 5, 2), (2, 1, 1, 3), (2, 2, 0, 4), (2, 2, 4, 4),
-    (2, 5, 2, 3), (1, 7, 3), (4, 34), (2, 6, 1, 3), (2, 6, 3, 2), (2, 6, 2, 3), (2, 4, 4, 3), (4, 35),
-    (2, 0, 2, 4), (2, 1, 1, 4), (2, 5, 5, 1), (2, 5, 4, 2), (2, 7, 4, 1), (4, 36), (2, 4, 5, 3), (4, 37),
-    (2, 5, 5, 2), (2, 7, 0, 3), (2, 3, 0, 3), (1, 7, 5), (4, 38), (2, 1, 5, 3), (2, 3, 0, 4), (2, 4, 3, 4),
-    (2, 7, 1, 3), (2, 7, 4, 2), (2, 7, 3, 1), (2, 0, 5, 4), (2, 7, 3, 2), (2, 6, 0, 4), (2, 1, 0, 4), (2, 7, 5, 1),
-    (2, 5, 1, 3), (4, 39), (2, 5, 1, 4), (2, 6, 1, 4), (2, 1, 3, 3), (2, 5, 0, 4), (2, 5, 2, 4), (2, 2, 3, 4),
-    (2, 4, 4, 4), (2, 0, 1, 4), (2, 7, 1, 4), (2, 7, 0, 4), (2, 2, 5, 4), (2, 3, 4, 3), (2, 7, 2, 3), (2, 6, 2, 4),
-    (2, 3, 3, 3), (2, 1, 2, 4), (2, 7, 2, 4), (2, 7, 5, 2), (2, 5, 3, 3), (2, 3, 2, 4), (4, 40), (2, 6, 5, 3),
-    (2, 3, 3, 4), (4, 41), (2, 1, 4, 3), (4, 42), (2, 1, 4, 4), (2, 3, 4, 4), (2, 6, 4, 4), (2, 5, 5, 3),
-    (4, 43), (2, 3, 5, 3), (2, 1, 5, 4), (2, 5, 3, 4), (2, 4, 5, 4), (2, 5, 5, 4), (2, 5, 4, 3), (4, 44),
-    (2, 6, 5, 4), (2, 7, 3, 3), (2, 7, 3, 4), (4, 45), (2, 7, 4, 3), (2, 1, 3, 4), (2, 7, 4, 4), (2, 6, 3, 3),
-    (2, 7, 5, 4), (2, 6, 3, 4), (2, 5, 4, 4), (2, 3, 5, 4), (2, 7, 5, 3),
+    (3, 0), (0, 3, 1), (0, 2, 0), (0, 2, 2), (0, 3, 4), (0, 1, 0), (0, 3, 2), (0, 0, 1),
+    (0, 1, 2), (0, 1, 1), (0, 0, 2), (0, 0, 0), (0, 1, 4), (0, 1, 3), (0, 3, 3), (0, 2, 3),
+    (1, 4, 0), (2, 0, 3, 1), (0, 2, 1), (0, 2, 4), (0, 0, 4), (1, 2, 2), (3, 1), (2, 0, 1, 1),
+    (1, 4, 2), (0, 0, 5), (2, 0, 2, 1), (2, 0, 4, 1), (1, 1, 0), (2, 0, 2, 2), (0, 3, 0), (2, 0, 1, 2),
+    (2, 2, 2, 1), (2, 4, 0, 1), (2, 4, 2, 1), (1, 4, 1), (2, 4, 1, 1), (3, 2), (0, 2, 5), (0, 0, 3),
+    (2, 1, 0, 1), (2, 0, 0, 1), (1, 4, 4), (1, 2, 4), (2, 0, 3, 2), (1, 2, 0), (2, 2, 0, 1), (1, 4, 3),
+    (1, 2, 1), (0, 1, 5), (1, 2, 3), (1, 6, 0), (3, 3), (1, 1, 1), (1, 1, 2), (2, 2, 4, 1),
+    (0, 3, 5), (2, 4, 2, 2), (2, 4, 1, 2), (2, 4, 3, 1), (1, 3, 0), (2, 1, 2, 1), (2, 4, 0, 2), (2, 2, 3, 1),
+    (1, 5, 0), (1, 2, 5), (1, 6, 2), (1, 6, 1), (2, 6, 0, 1), (2, 0, 4, 2), (1, 1, 4), (2, 2, 1, 1),
+    (2, 0, 5, 1), (2, 0, 0, 2), (3, 4), (2, 3, 0, 1), (2, 2, 5, 1), (2, 4, 4, 1), (1, 1, 3), (4, 0),
+    (1, 6, 4), (2, 1, 0, 2), (2, 2, 2, 2), (4, 1), (2, 5, 0, 1), (2, 2, 4, 2), (1, 3, 2), (4, 2),
+    (2, 4, 1, 3), (1, 1, 5), (2, 1, 2, 2), (2, 0, 5, 2), (2, 0, 0, 3), (2, 6, 2, 1), (2, 2, 0, 2), (2, 1, 1, 1),
+    (2, 6, 1, 1), (4, 3), (2, 2, 3, 2), (2, 6, 0, 2), (1, 3, 1), (2, 2, 5, 2), (2, 0, 4, 3), (4, 4),
+    (2, 3, 2, 1), (1, 4, 5), (1, 6, 3), (4, 5), (4, 6), (2, 2, 2, 3), (2, 2, 1, 2), (2, 3, 0, 2),
+    (1, 5, 1), (2, 4, 1, 4), (4, 7), (2, 4, 2, 3), (2, 0, 1, 3), (4, 8), (4, 9), (2, 6, 1, 2),
+    (2, 1, 5, 1), (2, 4, 3, 2), (2, 3, 1, 1), (2, 1, 4, 1), (2, 0, 2, 3), (4, 10), (2, 6, 2, 2), (2, 1, 3, 1),
+    (1, 3, 4), (2, 1, 1, 2), (2, 5, 2, 1), (2, 2, 4, 3), (1, 7, 0), (2, 4, 4, 2), (1, 5, 2), (2, 1, 2, 3),
+    (2, 5, 0, 2), (4, 11), (1, 6, 5), (2, 1, 5, 2), (1, 7, 2), (4, 12), (2, 4, 5, 1), (2, 6, 5, 1),
+    (4, 13), (2, 0, 3, 3), (1, 5, 4), (1, 3, 3), (4, 14), (2, 3, 2, 2), (2, 0, 5, 3), (4, 15),
+    (2, 5, 1, 1), (2, 4, 0, 3), (2, 1, 3, 2), (2, 7, 0, 1), (2, 1, 4, 2), (2, 3, 1, 2), (1, 3, 5), (1, 7, 1),
+    (4, 16), (4, 17), (4, 18), (2, 5, 2, 2), (2, 0, 0, 4), (1, 5, 3), (2, 7, 2, 1), (4, 19),
+    (2, 7, 1, 1), (2, 6, 3, 1), (4, 20), (2, 3, 5, 1), (1, 5, 5), (2, 4, 5, 2), (2, 1, 0, 3), (2, 5, 1, 2),
+    (4, 21), (2, 5, 3, 1), (4, 22), (2, 6, 3, 2), (2, 5, 4, 1), (2, 6, 5, 2), (2, 7, 0, 2), (4, 23),
+    (2, 3, 3, 1), (2, 5, 5, 1), (4, 24), (2, 1, 0, 4), (4, 25), (2, 6, 0, 3), (2, 6, 1, 3), (2, 7, 1, 2),
+    (2, 5, 3, 2), (2, 4, 3, 3), (2, 7, 2, 2), (4, 26), (4, 27), (1, 7, 4), (2, 2, 4, 4), (2, 5, 4, 2),
+    (4, 28), (4, 29), (4, 30), (2, 7, 4, 1), (2, 1, 5, 3), (2, 2, 1, 3), (2, 3, 0, 3), (2, 6, 4, 1),
+    (2, 1, 2, 4), (2, 3, 5, 2), (2, 6, 2, 3), (2, 7, 5, 1), (2, 3, 4, 1), (2, 0, 2, 4), (2, 4, 4, 3), (2, 2, 2, 4),
+    (4, 31), (4, 32), (4, 33), (2, 5, 5, 2), (2, 7, 4, 2), (2, 3, 0, 4), (1, 7, 5), (4, 34),
+    (2, 2, 0, 3), (2, 6, 1, 4), (4, 35), (4, 36), (4, 37), (2, 3, 1, 3), (2, 6, 4, 2), (2, 5, 2, 3),
+    (2, 3, 2, 3), (2, 2, 0, 4), (2, 2, 5, 3), (2, 5, 0, 3), (2, 0, 5, 4), (2, 7, 5, 2), (2, 7, 3, 1), (2, 1, 1, 3),
+    (1, 7, 3), (4, 38), (4, 39), (4, 40), (2, 5, 1, 3), (2, 4, 2, 4), (2, 3, 3, 2), (4, 41),
+    (2, 7, 0, 3), (4, 42), (2, 4, 0, 4), (2, 5, 1, 4), (4, 43), (2, 6, 2, 4), (2, 5, 2, 4), (2, 7, 0, 4),
+    (2, 0, 4, 4), (4, 44), (2, 0, 1, 4), (2, 3, 4, 2), (2, 7, 2, 3), (2, 2, 3, 3), (2, 7, 3, 2), (2, 6, 0, 4),
+    (2, 6, 3, 3), (4, 45), (2, 1, 1, 4), (2, 3, 1, 4), (2, 7, 1, 3), (2, 2, 3, 4), (2, 5, 3, 3), (2, 5, 0, 4),
+    (2, 7, 2, 4), (2, 4, 4, 4), (2, 4, 3, 4), (2, 2, 1, 4), (2, 1, 4, 3), (2, 6, 5, 3), (2, 7, 1, 4), (2, 2, 5, 4),
+    (2, 3, 2, 4), (4, 46), (2, 5, 4, 3), (4, 47), (2, 3, 5, 3), (4, 48), (4, 49), (4, 50),
+    (2, 4, 5, 3), (4, 51), (4, 52), (2, 6, 4, 3), (2, 7, 5, 3), (2, 1, 3, 3), (4, 53), (2, 5, 5, 3),
+    (2, 7, 4, 3), (2, 4, 5, 4), (2, 1, 4, 4), (2, 3, 3, 3), (4, 54), (2, 7, 4, 4), (2, 5, 3, 4), (4, 55),
+    (2, 5, 4, 4), (2, 6, 4, 4), (2, 1, 3, 4), (2, 3, 5, 4), (2, 6, 3, 4), (2, 3, 4, 4), (2, 7, 5, 4), (2, 1, 5, 4),
+    (2, 3, 3, 4), (2, 7, 3, 3), (2, 3, 4, 3), (2, 0, 3, 4), (2, 6, 5, 4), (2, 7, 3, 4), (2, 5, 5, 4),
 )
 
 
@@ -135,18 +138,30 @@
     yield
 
 
-def residual_of(block, fall, fall_t, inverse):
+def residual_steps(block, fall, fall_t, inverse):
     cross = jnp.dot(fall_t[...], block, preferred_element_type=jnp.float32)
+    yield
     exposure = exact_dot(inverse[...], cross)
+    yield
     fitted = jnp.dot(fall[...], exposure.astype(jnp.bfloat16), preferred_element_type=jnp.float32)
     return exposure, (block.astype(jnp.float32) - fitted).astype(jnp.bfloat16)
 
 
+def residual_of(*args):
+    steps = residual_steps(*args)
+    while True:
+        try:
+            next(steps)
+        except StopIteration as done:
+            return done.value
+
+
 def own_residuals(mine, fall, fall_t, inverse, loadings, mine_t):
     for side in range(SIDES):
-        part = pl.ds(side * SIDE, SIDE)
-        exposure, residual = residual_of(mine[:, part], fall, fall_t, inverse)
+        part = pl.ds(SIDE_AT[side], SIDE_WIDTH[side])
+        exposure, residual = yield from residual_steps(mine[:, part], fall, fall_t, inverse)
         loadings[:, part] = exposure
+        yield
         mine_t[part, :] = residual.T
         yield
 
@@ -155,12 +170,12 @@
     for core in range(2):
         if core == 0:
             prepare()
-        part = pl.ds(core * ASSET_BLOCK, SIDE)
-        residuals[core] = residual_of(cols[:, part], fall, fall_t, inverse)[1]
+        part = pl.ds(core * ASSET_BLOCK, SIDE_WIDTH[0])
+        _, residuals[core] = yield from residual_steps(cols[:, part], fall, fall_t, inverse)
         yield
     for core in range(2):
         for block in range(2):
-            rows = pl.ds(block * SIDE, SIDE)
+            rows = pl.ds(block * ROWS, ROWS)
             first_side[core, rows, :] = jnp.dot(
                 mine_t[rows, :], residuals[core], preferred_element_type=jnp.float32) * (1.0 / DAYS)
             yield
@@ -231,10 +246,11 @@
         return pl.ds(pl.multiple_of(day_of(dx, dh) * DAY_BLOCK + p % THIRDS * PART, PART), PART)
 
     def m_part(dx, dh, p):
-        return mine.at[part_rows(dx, dh, p), pl.ds(p // THIRDS * SIDE, SIDE)]
+        return mine.at[part_rows(dx, dh, p), pl.ds(SIDE_AT[p // THIRDS], SIDE_WIDTH[p // THIRDS])]
 
     def c_part(dx, dh, p, core):
-        lanes = pl.ds(pl.multiple_of(core * ASSET_BLOCK + p // THIRDS * SIDE, SIDE), SIDE)
+        side = p // THIRDS
+        lanes = pl.ds(pl.multiple_of(core * ASSET_BLOCK + SIDE_AT[side], 128), SIDE_WIDTH[side])
         return cols.at[part_rows(dx, dh, p), lanes]
 
     n_f, n_m, n_c = [0], [0], [0]
@@ -290,12 +306,13 @@
     def fill(side):
         @pl.when(is_root)
         def _():
-            lanes = pl.ds(pl.multiple_of(c * ASSET_BLOCK + side * SIDE, SIDE), SIDE)
+            at, width = SIDE_AT[side], SIDE_WIDTH[side]
+            lanes = pl.ds(pl.multiple_of(c * ASSET_BLOCK + at, 128), width)
 
             @pl.loop(0, DAYS // 64)
             def _(i):
                 rows = pl.ds(pl.multiple_of(i * 64, 64), 64)
-                cols[rows, lanes] = mine[rows, pl.ds(side * SIDE, SIDE)]
+                cols[rows, lanes] = mine[rows, pl.ds(at, width)]
 
         for dx, dh in CHUNKS:
             for p in range(side * THIRDS, (side + 1) * THIRDS):
@@ -350,13 +367,13 @@
             shape((FACTORS, FACTORS), jnp.float32),
             shape((FACTORS, ASSET_BLOCK), jnp.float32),
             shape((ASSET_BLOCK, DAYS), jnp.bfloat16),
-            shape((2, ASSET_BLOCK, SIDE), jnp.float32),
+            shape((2, ASSET_BLOCK, SIDE_WIDTH[0]), jnp.float32),
         ),
         in_specs=[pl.BlockSpec(memory_space=pl.ANY)] * 2,
         out_specs=(pl.BlockSpec(memory_space=pltpu.VMEM),) * 7,
         scratch_shapes=[
             pltpu.VMEM((DAYS, ASSET_BLOCK), jnp.bfloat16),
-            pltpu.VMEM((2, DAYS, SIDE), jnp.bfloat16),
+            pltpu.VMEM((2, DAYS, SIDE_WIDTH[0]), jnp.bfloat16),
             pltpu.VMEM((FACTORS, FACTORS), jnp.float32),
             dma((2,)), dma((7,)), dma((8,)), dma((8,)), dma((10 * PARTS,)), dma((8, PARTS)),
             dma((8 * PARTS * 7,)), dma((8, PARTS)), dma((8, PARTS)), dma((8,)), dma((8, PARTS)),
@@ -368,23 +385,28 @@
 
 
 def covariance_kernel(cols, fall, fall_t, inverse, loadings, mine_t, first_side, loadings_out, covariance, stage, sems):
+    width = SIDE_WIDTH[1]
     copies = [pltpu.make_async_copy(loadings, loadings_out, sems.at[0])]
     for core in range(2):
-        lanes = pl.ds(core * ASSET_BLOCK, SIDE)
+        lanes = pl.ds(core * ASSET_BLOCK, SIDE_WIDTH[0])
         copies.append(pltpu.make_async_copy(first_side.at[core], covariance.at[:, lanes], sems.at[1 + core]))
     for copy in copies:
         copy.start()
-    for core in range(2):
-        lanes = pl.ds(core * ASSET_BLOCK + SIDE, SIDE)
-        _, residual = residual_of(cols[:, lanes], fall, fall_t, inverse)
-        for block in range(2):
-            rows = pl.ds(block * SIDE, SIDE)
-            stage[core, rows, :] = jnp.dot(
-                mine_t[rows, :], residual, preferred_element_type=jnp.float32) * (1.0 / DAYS)
-            copy = pltpu.make_async_copy(
-                stage.at[core, rows], covariance.at[rows, lanes], sems.at[3 + core * 2 + block])
-            copy.start()
-            copies.append(copy)
+    lanes = [pl.ds(core * ASSET_BLOCK + SIDE_AT[1], width) for core in range(2)]
+    blocks = [cols[:, part] for part in lanes]
+    groups = [(0,), (1,)] if width >= 512 else [(0, 1)]
+    for group in groups:
+        block = jnp.concatenate([blocks[core] for core in group], axis=1)
+        _, residual = residual_of(block, fall, fall_t, inverse)
+        for half in range(2):
+            rows = pl.ds(half * ROWS, ROWS)
+            product = jnp.dot(mine_t[rows, :], residual, preferred_element_type=jnp.float32) * (1.0 / DAYS)
+            for i, core in enumerate(group):
+                stage[core, rows, :] = product[:, i * width:(i + 1) * width]
+                copy = pltpu.make_async_copy(
+                    stage.at[core, rows], covariance.at[rows, lanes[core]], sems.at[3 + core * 2 + half])
+                copy.start()
+                copies.append(copy)
     for copy in copies:
         copy.wait()
 
@@ -398,7 +420,7 @@
         ),
         in_specs=[pl.BlockSpec(memory_space=pltpu.VMEM)] * len(args),
         out_specs=(pl.BlockSpec(memory_space=pltpu.HBM),) * 2,
-        scratch_shapes=[pltpu.VMEM((2, ASSET_BLOCK, SIDE), jnp.float32), pltpu.SemaphoreType.DMA((7,))],
+        scratch_shapes=[pltpu.VMEM((2, ASSET_BLOCK, SIDE_WIDTH[1]), jnp.float32), pltpu.SemaphoreType.DMA((7,))],
         compiler_params=pltpu.CompilerParams(vmem_limit_bytes=24 * 2**20),
         name="covariances",
     )(*args)

time: 77.2 us -> 74.7 us (0.968)
  Pallas kernels: 75 us -> 72.9 us
    pallas_call x1, Pallas kernels: 67.5 us -> 65.4 us  [gather(): pl.pallas_call(gather_kernel, out_shape=(shape((DAYS, 2 * ASSET_BLOCK), j...]
where the time goes in v5:
time: 74.7 us; the launch traced here: 73.7 us
  Pallas kernels  72.9 us (98%)
  between operations  0.82 us (1%)
    pallas_call x1, Pallas kernels, gather(): pl.pallas_call(gather_kernel, out_shape=(shape((DAYS, 2 * ASSET_BLOCK), j...  65.4 us
    pallas_call x1, Pallas kernels, covariances(): pl.pallas_call(covariance_kernel, out_shape=(jax.ShapeDtypeStruct((FACTOR...  7.48 us

profile of v5, /device:TPU:5, one launch (start us, length us, event | category | flops | bytes accessed | tf_op | source)
XLA Modules:
  0.0 73.7 jit_solution(7783339244180502818)
XLA Ops:
  0.6 65.4 %gather.1 = (bf16[1536,2048]{1,0:T(8,128)(2,1)S(1)}, bf16[1536,256]{1,0:T(8,128)(2,1)S(1)}, bf16[256,1536]{1,0:T(8,128)(2,1)S(1)}, f32[256,256]{1,0:T(8,128)S(1)...) custom-call(bf16[192,256]{1,0:T(8,128)(2,1)} %f_hbm.1, bf16[192,1024]{1,0:T(8,128)(2,1)} %x_hbm.1), custom_call_target="tpu_custom_call" | custom-call | tf_op jit(solution)/shard_map/gather/pallas_call | solution.py:361
  66.1 7.5 %covariances.1 = (f32[256,1024]{1,0:T(8,128)}, f32[1024,2048]{1,0:T(8,128)}) custom-call(bf16[1536,2048]{1,0:T(8,128)(2,1)S(1)} %get-tuple-element.9.cols, bf16[1536,256]{1,0:T(8,128)(2,1)S(1)} %get-tuple-element.10.fall, bf16[256,1536]{1,0:T(8,128)(2,1)S(1)} %get-tuple-element.11.fall_t, f32[256,256]{1,0:T(8,128)S(1)} %get-tuple-element.12.inverse, ...), custom_call_target="tpu_custom_call" | custom-call | tf_op jit(solution)/shard_map/covariances/pallas_call | solution.py:415

commit v6 on v5

--- a/solution.py
+++ b/solution.py
@@ -27,55 +27,69 @@
     (("z-", ((0, 0), (0, 3), (0, 2), (1, 3), (1, 2))), ("y", ((0, 3),)), ("z+", ((1, 3),))),
     (("y", ((0, 0), (1, 1), (1, 2), (1, 3))), ("z+", ((1, 0), (1, 1))), ("z-", ((1, 0),))),
 )
-DEPTHS = (
-    (((0, 1),), ((0, 2), (1, 1)), ((0, 3), (1, 2), (1, 0)), ((1, 3),)),
-    (((0, 3),), ((0, 2), (1, 3)), ((0, 1), (1, 2), (1, 0)), ((1, 1),)),
-    (((1, 0),), ((1, 1), (1, 3)), ((0, 1), (1, 2), (0, 3)), ((0, 2),)),
-)
+ROLES = ((0, 1), (0, 2), (0, 3), (1, 0), (1, 1), (1, 2), (1, 3))
 CHUNKS = ((0, 0), (0, 1), (1, 0), (1, 1), (-1, 0), (-1, 1), (2, 0), (2, 1))
 
 LINKS = ("h", "x+", "x-", "root")
 ORDER = (
-    (3, 0), (0, 3, 1), (0, 2, 0), (0, 2, 2), (0, 3, 4), (0, 1, 0), (0, 3, 2), (0, 0, 1),
-    (0, 1, 2), (0, 1, 1), (0, 0, 2), (0, 0, 0), (0, 1, 4), (0, 1, 3), (0, 3, 3), (0, 2, 3),
-    (1, 4, 0), (2, 0, 3, 1), (0, 2, 1), (0, 2, 4), (0, 0, 4), (1, 2, 2), (3, 1), (2, 0, 1, 1),
-    (1, 4, 2), (0, 0, 5), (2, 0, 2, 1), (2, 0, 4, 1), (1, 1, 0), (2, 0, 2, 2), (0, 3, 0), (2, 0, 1, 2),
-    (2, 2, 2, 1), (2, 4, 0, 1), (2, 4, 2, 1), (1, 4, 1), (2, 4, 1, 1), (3, 2), (0, 2, 5), (0, 0, 3),
-    (2, 1, 0, 1), (2, 0, 0, 1), (1, 4, 4), (1, 2, 4), (2, 0, 3, 2), (1, 2, 0), (2, 2, 0, 1), (1, 4, 3),
-    (1, 2, 1), (0, 1, 5), (1, 2, 3), (1, 6, 0), (3, 3), (1, 1, 1), (1, 1, 2), (2, 2, 4, 1),
-    (0, 3, 5), (2, 4, 2, 2), (2, 4, 1, 2), (2, 4, 3, 1), (1, 3, 0), (2, 1, 2, 1), (2, 4, 0, 2), (2, 2, 3, 1),
-    (1, 5, 0), (1, 2, 5), (1, 6, 2), (1, 6, 1), (2, 6, 0, 1), (2, 0, 4, 2), (1, 1, 4), (2, 2, 1, 1),
-    (2, 0, 5, 1), (2, 0, 0, 2), (3, 4), (2, 3, 0, 1), (2, 2, 5, 1), (2, 4, 4, 1), (1, 1, 3), (4, 0),
-    (1, 6, 4), (2, 1, 0, 2), (2, 2, 2, 2), (4, 1), (2, 5, 0, 1), (2, 2, 4, 2), (1, 3, 2), (4, 2),
-    (2, 4, 1, 3), (1, 1, 5), (2, 1, 2, 2), (2, 0, 5, 2), (2, 0, 0, 3), (2, 6, 2, 1), (2, 2, 0, 2), (2, 1, 1, 1),
-    (2, 6, 1, 1), (4, 3), (2, 2, 3, 2), (2, 6, 0, 2), (1, 3, 1), (2, 2, 5, 2), (2, 0, 4, 3), (4, 4),
-    (2, 3, 2, 1), (1, 4, 5), (1, 6, 3), (4, 5), (4, 6), (2, 2, 2, 3), (2, 2, 1, 2), (2, 3, 0, 2),
-    (1, 5, 1), (2, 4, 1, 4), (4, 7), (2, 4, 2, 3), (2, 0, 1, 3), (4, 8), (4, 9), (2, 6, 1, 2),
-    (2, 1, 5, 1), (2, 4, 3, 2), (2, 3, 1, 1), (2, 1, 4, 1), (2, 0, 2, 3), (4, 10), (2, 6, 2, 2), (2, 1, 3, 1),
-    (1, 3, 4), (2, 1, 1, 2), (2, 5, 2, 1), (2, 2, 4, 3), (1, 7, 0), (2, 4, 4, 2), (1, 5, 2), (2, 1, 2, 3),
-    (2, 5, 0, 2), (4, 11), (1, 6, 5), (2, 1, 5, 2), (1, 7, 2), (4, 12), (2, 4, 5, 1), (2, 6, 5, 1),
-    (4, 13), (2, 0, 3, 3), (1, 5, 4), (1, 3, 3), (4, 14), (2, 3, 2, 2), (2, 0, 5, 3), (4, 15),
-    (2, 5, 1, 1), (2, 4, 0, 3), (2, 1, 3, 2), (2, 7, 0, 1), (2, 1, 4, 2), (2, 3, 1, 2), (1, 3, 5), (1, 7, 1),
-    (4, 16), (4, 17), (4, 18), (2, 5, 2, 2), (2, 0, 0, 4), (1, 5, 3), (2, 7, 2, 1), (4, 19),
-    (2, 7, 1, 1), (2, 6, 3, 1), (4, 20), (2, 3, 5, 1), (1, 5, 5), (2, 4, 5, 2), (2, 1, 0, 3), (2, 5, 1, 2),
-    (4, 21), (2, 5, 3, 1), (4, 22), (2, 6, 3, 2), (2, 5, 4, 1), (2, 6, 5, 2), (2, 7, 0, 2), (4, 23),
-    (2, 3, 3, 1), (2, 5, 5, 1), (4, 24), (2, 1, 0, 4), (4, 25), (2, 6, 0, 3), (2, 6, 1, 3), (2, 7, 1, 2),
-    (2, 5, 3, 2), (2, 4, 3, 3), (2, 7, 2, 2), (4, 26), (4, 27), (1, 7, 4), (2, 2, 4, 4), (2, 5, 4, 2),
-    (4, 28), (4, 29), (4, 30), (2, 7, 4, 1), (2, 1, 5, 3), (2, 2, 1, 3), (2, 3, 0, 3), (2, 6, 4, 1),
-    (2, 1, 2, 4), (2, 3, 5, 2), (2, 6, 2, 3), (2, 7, 5, 1), (2, 3, 4, 1), (2, 0, 2, 4), (2, 4, 4, 3), (2, 2, 2, 4),
-    (4, 31), (4, 32), (4, 33), (2, 5, 5, 2), (2, 7, 4, 2), (2, 3, 0, 4), (1, 7, 5), (4, 34),
-    (2, 2, 0, 3), (2, 6, 1, 4), (4, 35), (4, 36), (4, 37), (2, 3, 1, 3), (2, 6, 4, 2), (2, 5, 2, 3),
-    (2, 3, 2, 3), (2, 2, 0, 4), (2, 2, 5, 3), (2, 5, 0, 3), (2, 0, 5, 4), (2, 7, 5, 2), (2, 7, 3, 1), (2, 1, 1, 3),
-    (1, 7, 3), (4, 38), (4, 39), (4, 40), (2, 5, 1, 3), (2, 4, 2, 4), (2, 3, 3, 2), (4, 41),
-    (2, 7, 0, 3), (4, 42), (2, 4, 0, 4), (2, 5, 1, 4), (4, 43), (2, 6, 2, 4), (2, 5, 2, 4), (2, 7, 0, 4),
-    (2, 0, 4, 4), (4, 44), (2, 0, 1, 4), (2, 3, 4, 2), (2, 7, 2, 3), (2, 2, 3, 3), (2, 7, 3, 2), (2, 6, 0, 4),
-    (2, 6, 3, 3), (4, 45), (2, 1, 1, 4), (2, 3, 1, 4), (2, 7, 1, 3), (2, 2, 3, 4), (2, 5, 3, 3), (2, 5, 0, 4),
-    (2, 7, 2, 4), (2, 4, 4, 4), (2, 4, 3, 4), (2, 2, 1, 4), (2, 1, 4, 3), (2, 6, 5, 3), (2, 7, 1, 4), (2, 2, 5, 4),
-    (2, 3, 2, 4), (4, 46), (2, 5, 4, 3), (4, 47), (2, 3, 5, 3), (4, 48), (4, 49), (4, 50),
-    (2, 4, 5, 3), (4, 51), (4, 52), (2, 6, 4, 3), (2, 7, 5, 3), (2, 1, 3, 3), (4, 53), (2, 5, 5, 3),
-    (2, 7, 4, 3), (2, 4, 5, 4), (2, 1, 4, 4), (2, 3, 3, 3), (4, 54), (2, 7, 4, 4), (2, 5, 3, 4), (4, 55),
-    (2, 5, 4, 4), (2, 6, 4, 4), (2, 1, 3, 4), (2, 3, 5, 4), (2, 6, 3, 4), (2, 3, 4, 4), (2, 7, 5, 4), (2, 1, 5, 4),
-    (2, 3, 3, 4), (2, 7, 3, 3), (2, 3, 4, 3), (2, 0, 3, 4), (2, 6, 5, 4), (2, 7, 3, 4), (2, 5, 5, 4),
+    (3, 0), (0, 1, 2), (0, 3, 2), (0, 1, 0), (0, 1, 1), (0, 0, 1), (0, 2, 4), (0, 2, 1),
+    (0, 0, 0), (0, 2, 0), (0, 1, 3), (0, 3, 1), (0, 3, 3), (0, 0, 2), (0, 3, 0), (2, 0, 1, 2),
+    (2, 0, 2, 3), (0, 2, 2), (2, 0, 3, 0), (0, 3, 4), (0, 1, 4), (1, 4, 2), (1, 4, 0), (1, 2, 4),
+    (3, 1), (2, 0, 0, 0), (0, 2, 3), (1, 4, 1), (0, 0, 3), (2, 0, 4, 2), (1, 1, 0), (0, 0, 4),
+    (3, 2), (1, 2, 1), (2, 4, 0, 0), (2, 2, 4, 2), (1, 4, 3), (0, 2, 5), (1, 4, 4), (2, 4, 2, 3),
+    (2, 4, 1, 2), (1, 2, 0), (1, 2, 2), (1, 2, 3), (0, 1, 5), (2, 2, 2, 3), (2, 0, 4, 6), (2, 0, 1, 6),
+    (0, 0, 5), (2, 0, 2, 6), (2, 0, 2, 4), (2, 4, 2, 4), (2, 0, 4, 1), (3, 3), (1, 1, 1), (2, 1, 0, 0),
+    (2, 4, 1, 6), (1, 1, 2), (1, 3, 0), (2, 2, 1, 2), (1, 6, 0), (2, 1, 2, 3), (2, 4, 4, 2), (2, 0, 0, 1),
+    (2, 0, 3, 4), (1, 6, 1), (2, 0, 3, 1), (2, 2, 0, 0), (0, 3, 5), (2, 4, 3, 0), (2, 1, 0, 4), (1, 5, 0),
+    (2, 4, 0, 1), (1, 1, 4), (2, 2, 2, 4), (2, 2, 4, 6), (1, 2, 5), (3, 4), (2, 0, 5, 3), (2, 6, 1, 2),
+    (1, 6, 2), (2, 3, 0, 0), (4, 0), (2, 0, 4, 3), (2, 6, 0, 0), (2, 2, 4, 1), (4, 1), (2, 1, 2, 6),
+    (1, 1, 3), (2, 2, 5, 3), (2, 4, 2, 5), (2, 0, 0, 4), (1, 6, 3), (2, 4, 2, 6), (1, 1, 5), (1, 3, 1),
+    (2, 1, 2, 4), (2, 0, 0, 5), (4, 2), (2, 2, 0, 1), (2, 5, 0, 0), (2, 0, 1, 1), (2, 4, 0, 5), (2, 4, 1, 5),
+    (2, 6, 2, 3), (2, 2, 0, 4), (2, 4, 0, 4), (4, 3), (2, 3, 0, 1), (2, 6, 0, 1), (2, 0, 5, 4), (1, 3, 2),
+    (2, 0, 2, 0), (4, 4), (4, 5), (2, 0, 1, 3), (1, 4, 5), (2, 0, 4, 5), (1, 3, 4), (2, 1, 5, 3),
+    (2, 1, 0, 3), (4, 6), (2, 1, 0, 1), (2, 0, 0, 2), (2, 0, 3, 3), (1, 6, 4), (2, 2, 3, 0), (2, 2, 1, 6),
+    (2, 0, 3, 5), (2, 5, 0, 1), (2, 4, 1, 3), (4, 7), (2, 1, 4, 2), (2, 2, 2, 6), (2, 4, 1, 4), (2, 1, 3, 0),
+    (2, 2, 5, 4), (2, 4, 3, 4), (2, 4, 1, 1), (2, 6, 0, 4), (2, 3, 2, 3), (2, 3, 0, 4), (2, 0, 1, 0), (4, 8),
+    (4, 9), (2, 4, 4, 6), (2, 3, 1, 2), (4, 10), (2, 6, 2, 4), (2, 4, 4, 1), (2, 0, 5, 6), (2, 4, 0, 6),
+    (2, 4, 5, 3), (2, 6, 1, 6), (1, 7, 0), (2, 2, 4, 3), (2, 3, 2, 4), (1, 5, 2), (2, 1, 1, 2), (2, 2, 2, 0),
+    (1, 3, 3), (2, 5, 2, 3), (2, 1, 2, 2), (2, 0, 1, 5), (1, 6, 5), (1, 5, 1), (2, 1, 2, 5), (2, 5, 0, 4),
+    (2, 2, 5, 6), (2, 6, 3, 0), (4, 11), (4, 12), (2, 1, 5, 6), (2, 0, 2, 2), (4, 13), (2, 1, 5, 4),
+    (4, 14), (2, 3, 0, 2), (2, 2, 4, 0), (2, 0, 4, 0), (2, 6, 1, 1), (2, 1, 3, 4), (1, 3, 5), (2, 3, 1, 6),
+    (2, 7, 0, 0), (2, 2, 1, 3), (2, 2, 3, 4), (2, 2, 3, 1), (1, 5, 4), (2, 6, 4, 2), (2, 4, 2, 0), (4, 15),
+    (2, 6, 5, 3), (2, 3, 3, 0), (4, 16), (2, 4, 3, 1), (2, 1, 2, 0), (2, 2, 1, 1), (2, 2, 0, 5), (2, 5, 2, 4),
+    (4, 17), (2, 0, 2, 5), (4, 18), (1, 5, 3), (2, 0, 1, 4), (1, 7, 1), (2, 5, 1, 2), (2, 1, 1, 6),
+    (2, 3, 0, 5), (2, 4, 2, 2), (4, 19), (2, 0, 5, 0), (2, 2, 4, 5), (2, 7, 2, 3), (2, 0, 0, 3), (2, 1, 0, 2),
+    (2, 2, 5, 5), (2, 6, 2, 6), (2, 4, 1, 0), (2, 1, 1, 1), (2, 6, 0, 3), (2, 0, 0, 6), (2, 4, 5, 4), (2, 2, 4, 4),
+    (2, 3, 3, 4), (2, 2, 2, 2), (2, 3, 1, 1), (4, 20), (2, 5, 2, 6), (2, 1, 4, 6), (1, 7, 2), (4, 21),
+    (4, 22), (2, 5, 3, 0), (2, 4, 3, 3), (2, 2, 0, 3), (2, 3, 5, 3), (2, 7, 0, 4), (2, 7, 1, 2), (2, 4, 2, 1),
+    (2, 2, 2, 5), (2, 6, 2, 0), (2, 5, 4, 2), (2, 5, 1, 6), (2, 4, 5, 6), (2, 1, 0, 5), (4, 23), (2, 7, 0, 1),
+    (2, 1, 4, 1), (4, 24), (2, 0, 2, 1), (2, 6, 5, 6), (2, 4, 0, 3), (1, 7, 4), (2, 6, 3, 1), (4, 25),
+    (4, 26), (2, 5, 5, 3), (2, 2, 1, 5), (2, 0, 3, 2), (2, 4, 0, 2), (2, 1, 0, 6), (2, 2, 3, 5), (2, 6, 3, 4),
+    (2, 7, 1, 6), (2, 1, 3, 1), (2, 7, 2, 4), (2, 5, 0, 5), (1, 5, 5), (4, 27), (2, 7, 1, 1), (2, 7, 4, 2),
+    (2, 3, 2, 6), (2, 3, 1, 3), (2, 2, 3, 6), (2, 3, 3, 1), (2, 6, 1, 5), (2, 2, 2, 1), (2, 0, 5, 2), (2, 5, 4, 6),
+    (2, 6, 5, 4), (2, 5, 1, 1), (2, 5, 3, 1), (2, 3, 4, 2), (2, 5, 3, 4), (4, 28), (2, 6, 2, 5), (4, 29),
+    (2, 3, 2, 5), (2, 6, 0, 5), (2, 7, 2, 6), (4, 30), (4, 31), (2, 3, 5, 4), (1, 7, 3), (2, 7, 5, 3),
+    (2, 4, 4, 5), (4, 32), (2, 6, 4, 6), (2, 7, 4, 6), (1, 7, 5), (2, 3, 0, 3), (2, 1, 5, 5), (2, 5, 0, 2),
+    (2, 1, 1, 3), (2, 5, 0, 6), (4, 33), (2, 7, 3, 0), (2, 5, 4, 1), (4, 34), (2, 5, 2, 0), (2, 3, 1, 5),
+    (4, 35), (2, 1, 1, 5), (2, 7, 4, 1), (4, 36), (4, 37), (4, 38), (2, 0, 5, 5), (2, 3, 4, 6),
+    (2, 7, 0, 5), (2, 4, 3, 5), (2, 2, 3, 3), (2, 5, 5, 4), (2, 3, 1, 0), (4, 39), (2, 6, 1, 3), (2, 7, 3, 1),
+    (2, 6, 0, 2), (2, 1, 5, 0), (2, 5, 1, 5), (2, 7, 5, 6), (2, 2, 0, 6), (4, 40), (2, 5, 2, 5), (2, 2, 3, 2),
+    (4, 41), (4, 42), (2, 5, 5, 6), (2, 6, 4, 1), (2, 7, 1, 5), (4, 43), (2, 7, 0, 3), (2, 2, 5, 0),
+    (2, 6, 3, 2), (2, 7, 1, 3), (2, 3, 5, 6), (2, 1, 5, 2), (2, 2, 1, 4), (2, 7, 5, 4), (2, 1, 5, 1), (2, 5, 4, 5),
+    (2, 3, 4, 1), (2, 5, 1, 3), (2, 3, 2, 2), (2, 6, 2, 1), (2, 6, 2, 2), (2, 4, 4, 3), (2, 1, 4, 5), (2, 1, 2, 1),
+    (2, 7, 2, 5), (4, 44), (2, 1, 3, 5), (2, 1, 3, 3), (2, 4, 5, 5), (2, 3, 3, 5), (2, 5, 2, 1), (2, 7, 0, 2),
+    (4, 45), (2, 7, 1, 0), (2, 7, 0, 6), (2, 6, 1, 4), (2, 1, 4, 0), (2, 7, 2, 1), (2, 2, 5, 2), (2, 4, 5, 2),
+    (2, 6, 5, 5), (2, 6, 4, 3), (2, 0, 4, 4), (2, 6, 3, 3), (2, 5, 0, 3), (2, 2, 0, 2), (2, 7, 2, 0), (2, 1, 4, 3),
+    (2, 5, 1, 0), (2, 3, 0, 6), (2, 3, 2, 0), (2, 1, 1, 0), (2, 5, 3, 2), (2, 5, 3, 3), (2, 4, 4, 4), (2, 7, 4, 3),
+    (2, 5, 2, 2), (2, 1, 1, 4), (2, 3, 1, 4), (2, 6, 0, 6), (2, 7, 1, 4), (2, 3, 2, 1), (2, 5, 1, 4), (2, 4, 5, 0),
+    (2, 6, 3, 5), (2, 7, 2, 2), (2, 4, 3, 2), (2, 6, 1, 0), (2, 3, 3, 3), (2, 2, 1, 0), (4, 46), (4, 47),
+    (4, 48), (2, 6, 5, 2), (2, 1, 3, 2), (2, 7, 3, 4), (2, 6, 4, 5), (4, 49), (4, 50), (4, 51),
+    (2, 3, 5, 5), (2, 0, 3, 6), (2, 3, 3, 2), (2, 4, 5, 1), (2, 4, 4, 0), (4, 52), (2, 6, 3, 6), (2, 5, 5, 0),
+    (2, 7, 4, 5), (2, 7, 5, 2), (2, 5, 3, 5), (2, 5, 4, 0), (2, 5, 5, 5), (2, 3, 3, 6), (2, 3, 4, 5), (2, 4, 3, 6),
+    (4, 53), (2, 5, 4, 4), (2, 1, 4, 4), (2, 7, 3, 2), (4, 54), (2, 6, 4, 4), (2, 6, 4, 0), (2, 6, 5, 0),
+    (2, 7, 4, 4), (2, 7, 3, 5), (2, 3, 5, 1), (2, 5, 5, 2), (2, 7, 5, 5), (2, 1, 3, 6), (2, 0, 5, 1), (2, 5, 3, 6),
+    (2, 5, 5, 1), (2, 5, 4, 3), (4, 55), (2, 3, 4, 4), (2, 2, 5, 1), (2, 3, 5, 2), (2, 6, 5, 1), (2, 3, 4, 0),
+    (2, 3, 4, 3), (2, 7, 4, 0), (2, 7, 5, 1), (2, 3, 5, 0), (2, 7, 3, 3), (2, 7, 5, 0), (2, 7, 3, 6),
 )
 
 
@@ -253,7 +267,7 @@
         lanes = pl.ds(pl.multiple_of(core * ASSET_BLOCK + SIDE_AT[side], 128), SIDE_WIDTH[side])
         return cols.at[part_rows(dx, dh, p), lanes]
 
-    n_f, n_m, n_c = [0], [0], [0]
+    n_f, n_m = [0], [0]
 
     def send_f(dx, dh, to):
         ref = f_rows(dx, dh, c)
@@ -270,12 +284,25 @@
         arrived(ref, f_recv.at[day_of(dx, dh)])
         send(ref, ref, fp_send.at[day_of(dx, dh)], f_pair.at[day_of(dx, dh)], day, sibling)
 
+    def relayed(src, dst, ssem, rsem, a):
+        return pltpu.make_async_remote_copy(
+            src_ref=src, dst_ref=dst, send_sem=ssem, recv_sem=rsem,
+            device_id={"days": day, "assets": a}, device_id_type=MESH)
+
+    def to_chip(src, dx, dh, p, i):
+        k = day_of(dx, dh)
+        link = TREES[p % THIRDS][i][0]
+        return relayed(src, c_part(dx, dh, p, c), c_send.at[k, p, i], c_recv.at[k, p], asset_of(link))
+
+    def to_sibling(src, dx, dh, p):
+        k = day_of(dx, dh)
+        return relayed(src, c_part(dx, dh, p, c), cp_send.at[k, p], c_pair.at[k, p], sibling)
+
     def root_sends(dx, dh, p):
-        link = TREES[p % THIRDS][0][0]
-        src, dst = m_part(dx, dh, p), c_part(dx, dh, p, c)
-        send(src, dst, c_send.at[n_c[0]], c_recv.at[day_of(dx, dh), p], day, asset_of(link), is_root)
-        n_c[0] += 1
-        send(src, dst, cp_send.at[day_of(dx, dh), p], c_pair.at[day_of(dx, dh), p], day, sibling, is_root)
+        @pl.when(is_root)
+        def _():
+            to_chip(m_part(dx, dh, p), dx, dh, p, 0).start()
+            to_sibling(m_part(dx, dh, p), dx, dh, p).start()
 
     def relay_mine(dx, dh, p):
         arrived(m_part(dx, dh, p), m_recv.at[day_of(dx, dh), p])
@@ -291,17 +318,15 @@
             send_m(dx, dh, p, (0, 1), partner_is_root)
         root_sends(dx, dh, p)
 
-    def relay_cols(dx, dh, p, depth):
-        ref = c_part(dx, dh, p, c)
-        tree = p % THIRDS
-        here = DEPTHS[tree][depth - 1]
-        pl.when(among(here))(lambda: arrived(ref, c_recv.at[day_of(dx, dh), p]))
-        for link, roles in TREES[tree]:
-            roles = [role for role in roles if role in here]
-            if roles:
-                send(ref, ref, c_send.at[n_c[0]], c_recv.at[day_of(dx, dh), p], day, asset_of(link), among(roles))
-                n_c[0] += 1
-        send(ref, ref, cp_send.at[day_of(dx, dh), p], c_pair.at[day_of(dx, dh), p], day, sibling, among(here))
+    def relay_cols(dx, dh, p, role):
+        @pl.when(among((ROLES[role],)))
+        def _():
+            ref = c_part(dx, dh, p, c)
+            arrived(ref, c_recv.at[day_of(dx, dh), p])
+            for i, (_, roles) in enumerate(TREES[p % THIRDS]):
+                if ROLES[role] in roles:
+                    to_chip(ref, dx, dh, p, i).start()
+            to_sibling(ref, dx, dh, p).start()
 
     def fill(side):
         @pl.when(is_root)
@@ -353,6 +378,16 @@
             copy.wait_send()
         else:
             pl.when(when)(copy.wait_send)
+    for i in range(THIRDS):
+        for third in range(THIRDS):
+            @pl.when(among(TREES[third][i][1]))
+            def _():
+                for dx, dh in CHUNKS:
+                    for p in range(third, PARTS, THIRDS):
+                        to_chip(c_part(dx, dh, p, c), dx, dh, p, i).wait_send()
+    for dx, dh in CHUNKS:
+        for p in range(PARTS):
+            to_sibling(c_part(dx, dh, p, c), dx, dh, p).wait_send()
 
 
 def gather(factors, returns):
@@ -376,7 +411,7 @@
             pltpu.VMEM((2, DAYS, SIDE_WIDTH[0]), jnp.bfloat16),
             pltpu.VMEM((FACTORS, FACTORS), jnp.float32),
             dma((2,)), dma((7,)), dma((8,)), dma((8,)), dma((10 * PARTS,)), dma((8, PARTS)),
-            dma((8 * PARTS * 7,)), dma((8, PARTS)), dma((8, PARTS)), dma((8,)), dma((8, PARTS)),
+            dma((8, PARTS, 3)), dma((8, PARTS)), dma((8, PARTS)), dma((8,)), dma((8, PARTS)),
         ],
         compiler_params=pltpu.CompilerParams(
             collective_id=0, has_side_effects=True, vmem_limit_bytes=36 * 2**20),

time: 74.7 us -> 72.5 us (0.971)
  Pallas kernels: 72.9 us -> 70.4 us
    pallas_call x1, Pallas kernels: 65.4 us -> 63 us  [gather(): pl.pallas_call(gather_kernel, out_shape=(shape((DAYS, 2 * ASSET_BLOCK), j...]
where the time goes in v6:
time: 72.5 us; the launch traced here: 71.2 us
  Pallas kernels  70.4 us (97%)
  between operations  0.82 us (1%)
    pallas_call x1, Pallas kernels, gather(): pl.pallas_call(gather_kernel, out_shape=(shape((DAYS, 2 * ASSET_BLOCK), j...  63 us
    pallas_call x1, Pallas kernels, covariances(): pl.pallas_call(covariance_kernel, out_shape=(jax.ShapeDtypeStruct((FACTOR...  7.46 us

profile of v6, /device:TPU:5, one launch (start us, length us, event | category | flops | bytes accessed | tf_op | source)
XLA Modules:
  0.0 71.2 jit_solution(919991321571975632)
XLA Ops:
  0.6 63.0 %gather.1 = (bf16[1536,2048]{1,0:T(8,128)(2,1)S(1)}, bf16[1536,256]{1,0:T(8,128)(2,1)S(1)}, bf16[256,1536]{1,0:T(8,128)(2,1)S(1)}, f32[256,256]{1,0:T(8,128)S(1)...) custom-call(bf16[192,256]{1,0:T(8,128)(2,1)} %f_hbm.1, bf16[192,1024]{1,0:T(8,128)(2,1)} %x_hbm.1), custom_call_target="tpu_custom_call" | custom-call | tf_op jit(solution)/shard_map/gather/pallas_call | solution.py:396
  63.6 7.5 %covariances.1 = (f32[256,1024]{1,0:T(8,128)}, f32[1024,2048]{1,0:T(8,128)}) custom-call(bf16[1536,2048]{1,0:T(8,128)(2,1)S(1)} %get-tuple-element.9.cols, bf16[1536,256]{1,0:T(8,128)(2,1)S(1)} %get-tuple-element.10.fall, bf16[256,1536]{1,0:T(8,128)(2,1)S(1)} %get-tuple-element.11.fall_t, f32[256,256]{1,0:T(8,128)S(1)} %get-tuple-element.12.inverse, ...), custom_call_target="tpu_custom_call" | custom-call | tf_op jit(solution)/shard_map/covariances/pallas_call | solution.py:450

commit v7 on v6

--- a/solution.py
+++ b/solution.py
@@ -32,64 +32,64 @@
 
 LINKS = ("h", "x+", "x-", "root")
 ORDER = (
-    (3, 0), (0, 1, 2), (0, 3, 2), (0, 1, 0), (0, 1, 1), (0, 0, 1), (0, 2, 4), (0, 2, 1),
-    (0, 0, 0), (0, 2, 0), (0, 1, 3), (0, 3, 1), (0, 3, 3), (0, 0, 2), (0, 3, 0), (2, 0, 1, 2),
-    (2, 0, 2, 3), (0, 2, 2), (2, 0, 3, 0), (0, 3, 4), (0, 1, 4), (1, 4, 2), (1, 4, 0), (1, 2, 4),
-    (3, 1), (2, 0, 0, 0), (0, 2, 3), (1, 4, 1), (0, 0, 3), (2, 0, 4, 2), (1, 1, 0), (0, 0, 4),
-    (3, 2), (1, 2, 1), (2, 4, 0, 0), (2, 2, 4, 2), (1, 4, 3), (0, 2, 5), (1, 4, 4), (2, 4, 2, 3),
-    (2, 4, 1, 2), (1, 2, 0), (1, 2, 2), (1, 2, 3), (0, 1, 5), (2, 2, 2, 3), (2, 0, 4, 6), (2, 0, 1, 6),
-    (0, 0, 5), (2, 0, 2, 6), (2, 0, 2, 4), (2, 4, 2, 4), (2, 0, 4, 1), (3, 3), (1, 1, 1), (2, 1, 0, 0),
-    (2, 4, 1, 6), (1, 1, 2), (1, 3, 0), (2, 2, 1, 2), (1, 6, 0), (2, 1, 2, 3), (2, 4, 4, 2), (2, 0, 0, 1),
-    (2, 0, 3, 4), (1, 6, 1), (2, 0, 3, 1), (2, 2, 0, 0), (0, 3, 5), (2, 4, 3, 0), (2, 1, 0, 4), (1, 5, 0),
-    (2, 4, 0, 1), (1, 1, 4), (2, 2, 2, 4), (2, 2, 4, 6), (1, 2, 5), (3, 4), (2, 0, 5, 3), (2, 6, 1, 2),
-    (1, 6, 2), (2, 3, 0, 0), (4, 0), (2, 0, 4, 3), (2, 6, 0, 0), (2, 2, 4, 1), (4, 1), (2, 1, 2, 6),
-    (1, 1, 3), (2, 2, 5, 3), (2, 4, 2, 5), (2, 0, 0, 4), (1, 6, 3), (2, 4, 2, 6), (1, 1, 5), (1, 3, 1),
-    (2, 1, 2, 4), (2, 0, 0, 5), (4, 2), (2, 2, 0, 1), (2, 5, 0, 0), (2, 0, 1, 1), (2, 4, 0, 5), (2, 4, 1, 5),
-    (2, 6, 2, 3), (2, 2, 0, 4), (2, 4, 0, 4), (4, 3), (2, 3, 0, 1), (2, 6, 0, 1), (2, 0, 5, 4), (1, 3, 2),
-    (2, 0, 2, 0), (4, 4), (4, 5), (2, 0, 1, 3), (1, 4, 5), (2, 0, 4, 5), (1, 3, 4), (2, 1, 5, 3),
-    (2, 1, 0, 3), (4, 6), (2, 1, 0, 1), (2, 0, 0, 2), (2, 0, 3, 3), (1, 6, 4), (2, 2, 3, 0), (2, 2, 1, 6),
-    (2, 0, 3, 5), (2, 5, 0, 1), (2, 4, 1, 3), (4, 7), (2, 1, 4, 2), (2, 2, 2, 6), (2, 4, 1, 4), (2, 1, 3, 0),
-    (2, 2, 5, 4), (2, 4, 3, 4), (2, 4, 1, 1), (2, 6, 0, 4), (2, 3, 2, 3), (2, 3, 0, 4), (2, 0, 1, 0), (4, 8),
-    (4, 9), (2, 4, 4, 6), (2, 3, 1, 2), (4, 10), (2, 6, 2, 4), (2, 4, 4, 1), (2, 0, 5, 6), (2, 4, 0, 6),
-    (2, 4, 5, 3), (2, 6, 1, 6), (1, 7, 0), (2, 2, 4, 3), (2, 3, 2, 4), (1, 5, 2), (2, 1, 1, 2), (2, 2, 2, 0),
-    (1, 3, 3), (2, 5, 2, 3), (2, 1, 2, 2), (2, 0, 1, 5), (1, 6, 5), (1, 5, 1), (2, 1, 2, 5), (2, 5, 0, 4),
-    (2, 2, 5, 6), (2, 6, 3, 0), (4, 11), (4, 12), (2, 1, 5, 6), (2, 0, 2, 2), (4, 13), (2, 1, 5, 4),
-    (4, 14), (2, 3, 0, 2), (2, 2, 4, 0), (2, 0, 4, 0), (2, 6, 1, 1), (2, 1, 3, 4), (1, 3, 5), (2, 3, 1, 6),
-    (2, 7, 0, 0), (2, 2, 1, 3), (2, 2, 3, 4), (2, 2, 3, 1), (1, 5, 4), (2, 6, 4, 2), (2, 4, 2, 0), (4, 15),
-    (2, 6, 5, 3), (2, 3, 3, 0), (4, 16), (2, 4, 3, 1), (2, 1, 2, 0), (2, 2, 1, 1), (2, 2, 0, 5), (2, 5, 2, 4),
-    (4, 17), (2, 0, 2, 5), (4, 18), (1, 5, 3), (2, 0, 1, 4), (1, 7, 1), (2, 5, 1, 2), (2, 1, 1, 6),
-    (2, 3, 0, 5), (2, 4, 2, 2), (4, 19), (2, 0, 5, 0), (2, 2, 4, 5), (2, 7, 2, 3), (2, 0, 0, 3), (2, 1, 0, 2),
-    (2, 2, 5, 5), (2, 6, 2, 6), (2, 4, 1, 0), (2, 1, 1, 1), (2, 6, 0, 3), (2, 0, 0, 6), (2, 4, 5, 4), (2, 2, 4, 4),
-    (2, 3, 3, 4), (2, 2, 2, 2), (2, 3, 1, 1), (4, 20), (2, 5, 2, 6), (2, 1, 4, 6), (1, 7, 2), (4, 21),
-    (4, 22), (2, 5, 3, 0), (2, 4, 3, 3), (2, 2, 0, 3), (2, 3, 5, 3), (2, 7, 0, 4), (2, 7, 1, 2), (2, 4, 2, 1),
-    (2, 2, 2, 5), (2, 6, 2, 0), (2, 5, 4, 2), (2, 5, 1, 6), (2, 4, 5, 6), (2, 1, 0, 5), (4, 23), (2, 7, 0, 1),
-    (2, 1, 4, 1), (4, 24), (2, 0, 2, 1), (2, 6, 5, 6), (2, 4, 0, 3), (1, 7, 4), (2, 6, 3, 1), (4, 25),
-    (4, 26), (2, 5, 5, 3), (2, 2, 1, 5), (2, 0, 3, 2), (2, 4, 0, 2), (2, 1, 0, 6), (2, 2, 3, 5), (2, 6, 3, 4),
-    (2, 7, 1, 6), (2, 1, 3, 1), (2, 7, 2, 4), (2, 5, 0, 5), (1, 5, 5), (4, 27), (2, 7, 1, 1), (2, 7, 4, 2),
-    (2, 3, 2, 6), (2, 3, 1, 3), (2, 2, 3, 6), (2, 3, 3, 1), (2, 6, 1, 5), (2, 2, 2, 1), (2, 0, 5, 2), (2, 5, 4, 6),
-    (2, 6, 5, 4), (2, 5, 1, 1), (2, 5, 3, 1), (2, 3, 4, 2), (2, 5, 3, 4), (4, 28), (2, 6, 2, 5), (4, 29),
-    (2, 3, 2, 5), (2, 6, 0, 5), (2, 7, 2, 6), (4, 30), (4, 31), (2, 3, 5, 4), (1, 7, 3), (2, 7, 5, 3),
-    (2, 4, 4, 5), (4, 32), (2, 6, 4, 6), (2, 7, 4, 6), (1, 7, 5), (2, 3, 0, 3), (2, 1, 5, 5), (2, 5, 0, 2),
-    (2, 1, 1, 3), (2, 5, 0, 6), (4, 33), (2, 7, 3, 0), (2, 5, 4, 1), (4, 34), (2, 5, 2, 0), (2, 3, 1, 5),
-    (4, 35), (2, 1, 1, 5), (2, 7, 4, 1), (4, 36), (4, 37), (4, 38), (2, 0, 5, 5), (2, 3, 4, 6),
-    (2, 7, 0, 5), (2, 4, 3, 5), (2, 2, 3, 3), (2, 5, 5, 4), (2, 3, 1, 0), (4, 39), (2, 6, 1, 3), (2, 7, 3, 1),
-    (2, 6, 0, 2), (2, 1, 5, 0), (2, 5, 1, 5), (2, 7, 5, 6), (2, 2, 0, 6), (4, 40), (2, 5, 2, 5), (2, 2, 3, 2),
-    (4, 41), (4, 42), (2, 5, 5, 6), (2, 6, 4, 1), (2, 7, 1, 5), (4, 43), (2, 7, 0, 3), (2, 2, 5, 0),
-    (2, 6, 3, 2), (2, 7, 1, 3), (2, 3, 5, 6), (2, 1, 5, 2), (2, 2, 1, 4), (2, 7, 5, 4), (2, 1, 5, 1), (2, 5, 4, 5),
-    (2, 3, 4, 1), (2, 5, 1, 3), (2, 3, 2, 2), (2, 6, 2, 1), (2, 6, 2, 2), (2, 4, 4, 3), (2, 1, 4, 5), (2, 1, 2, 1),
-    (2, 7, 2, 5), (4, 44), (2, 1, 3, 5), (2, 1, 3, 3), (2, 4, 5, 5), (2, 3, 3, 5), (2, 5, 2, 1), (2, 7, 0, 2),
-    (4, 45), (2, 7, 1, 0), (2, 7, 0, 6), (2, 6, 1, 4), (2, 1, 4, 0), (2, 7, 2, 1), (2, 2, 5, 2), (2, 4, 5, 2),
-    (2, 6, 5, 5), (2, 6, 4, 3), (2, 0, 4, 4), (2, 6, 3, 3), (2, 5, 0, 3), (2, 2, 0, 2), (2, 7, 2, 0), (2, 1, 4, 3),
-    (2, 5, 1, 0), (2, 3, 0, 6), (2, 3, 2, 0), (2, 1, 1, 0), (2, 5, 3, 2), (2, 5, 3, 3), (2, 4, 4, 4), (2, 7, 4, 3),
-    (2, 5, 2, 2), (2, 1, 1, 4), (2, 3, 1, 4), (2, 6, 0, 6), (2, 7, 1, 4), (2, 3, 2, 1), (2, 5, 1, 4), (2, 4, 5, 0),
-    (2, 6, 3, 5), (2, 7, 2, 2), (2, 4, 3, 2), (2, 6, 1, 0), (2, 3, 3, 3), (2, 2, 1, 0), (4, 46), (4, 47),
-    (4, 48), (2, 6, 5, 2), (2, 1, 3, 2), (2, 7, 3, 4), (2, 6, 4, 5), (4, 49), (4, 50), (4, 51),
-    (2, 3, 5, 5), (2, 0, 3, 6), (2, 3, 3, 2), (2, 4, 5, 1), (2, 4, 4, 0), (4, 52), (2, 6, 3, 6), (2, 5, 5, 0),
-    (2, 7, 4, 5), (2, 7, 5, 2), (2, 5, 3, 5), (2, 5, 4, 0), (2, 5, 5, 5), (2, 3, 3, 6), (2, 3, 4, 5), (2, 4, 3, 6),
-    (4, 53), (2, 5, 4, 4), (2, 1, 4, 4), (2, 7, 3, 2), (4, 54), (2, 6, 4, 4), (2, 6, 4, 0), (2, 6, 5, 0),
-    (2, 7, 4, 4), (2, 7, 3, 5), (2, 3, 5, 1), (2, 5, 5, 2), (2, 7, 5, 5), (2, 1, 3, 6), (2, 0, 5, 1), (2, 5, 3, 6),
-    (2, 5, 5, 1), (2, 5, 4, 3), (4, 55), (2, 3, 4, 4), (2, 2, 5, 1), (2, 3, 5, 2), (2, 6, 5, 1), (2, 3, 4, 0),
-    (2, 3, 4, 3), (2, 7, 4, 0), (2, 7, 5, 1), (2, 3, 5, 0), (2, 7, 3, 3), (2, 7, 5, 0), (2, 7, 3, 6),
+    (0, 3, 2), (0, 2, 4), (0, 3, 3), (0, 1, 2), (0, 2, 2), (0, 2, 1), (0, 1, 0), (0, 1, 1),
+    (0, 3, 1), (0, 2, 0), (0, 0, 0), (3, 0), (0, 3, 0), (0, 0, 2), (0, 3, 4), (2, 0, 2, 3),
+    (1, 4, 2), (0, 1, 3), (2, 0, 1, 2), (2, 0, 4, 2), (0, 1, 4), (1, 1, 0), (2, 0, 1, 6), (0, 2, 5),
+    (2, 0, 0, 0), (0, 0, 4), (2, 0, 2, 4), (3, 1), (1, 2, 4), (1, 4, 1), (2, 2, 4, 2), (1, 2, 2),
+    (1, 4, 0), (0, 0, 1), (3, 2), (1, 2, 0), (2, 0, 0, 1), (2, 1, 0, 0), (0, 1, 5), (1, 1, 2),
+    (0, 0, 3), (0, 3, 5), (2, 4, 2, 3), (2, 0, 4, 6), (1, 2, 1), (2, 4, 1, 2), (1, 4, 4), (1, 3, 0),
+    (1, 4, 3), (2, 0, 3, 0), (1, 5, 0), (2, 0, 4, 1), (2, 2, 2, 3), (0, 0, 5), (3, 3), (0, 2, 3),
+    (2, 2, 0, 0), (2, 3, 0, 0), (2, 1, 2, 3), (1, 1, 1), (1, 2, 5), (1, 6, 1), (2, 1, 0, 1), (2, 4, 2, 4),
+    (1, 1, 4), (1, 6, 2), (2, 4, 0, 0), (2, 2, 2, 4), (2, 0, 2, 6), (1, 1, 3), (2, 0, 5, 3), (2, 2, 1, 2),
+    (2, 0, 0, 2), (2, 0, 4, 5), (2, 4, 3, 0), (2, 2, 0, 1), (1, 6, 0), (2, 1, 1, 2), (2, 0, 1, 1), (3, 4),
+    (4, 0), (2, 6, 0, 0), (2, 1, 2, 4), (2, 4, 4, 2), (2, 0, 4, 4), (2, 6, 1, 2), (2, 1, 0, 4), (1, 2, 3),
+    (2, 2, 5, 3), (2, 0, 3, 1), (2, 3, 0, 1), (2, 0, 2, 0), (1, 1, 5), (4, 1), (2, 2, 4, 6), (4, 2),
+    (2, 0, 3, 4), (2, 5, 0, 0), (2, 6, 2, 3), (1, 3, 1), (1, 3, 2), (2, 1, 3, 0), (2, 0, 2, 5), (1, 4, 5),
+    (4, 3), (4, 4), (2, 4, 0, 1), (2, 2, 2, 5), (2, 0, 1, 5), (2, 4, 0, 4), (2, 2, 1, 6), (1, 5, 2),
+    (2, 2, 4, 1), (2, 0, 5, 6), (2, 0, 0, 5), (4, 5), (2, 0, 0, 4), (2, 0, 5, 4), (2, 1, 5, 3), (4, 6),
+    (2, 2, 5, 4), (2, 1, 1, 1), (2, 4, 1, 6), (2, 1, 0, 5), (2, 2, 0, 5), (2, 4, 2, 6), (2, 2, 3, 0), (1, 6, 4),
+    (4, 7), (2, 0, 1, 0), (4, 8), (1, 3, 4), (2, 2, 2, 6), (2, 1, 0, 2), (2, 2, 4, 3), (1, 6, 3),
+    (2, 6, 0, 1), (2, 3, 2, 3), (2, 3, 0, 4), (4, 9), (2, 6, 2, 4), (4, 10), (2, 0, 1, 3), (2, 1, 0, 3),
+    (2, 4, 4, 6), (4, 11), (2, 3, 1, 2), (1, 6, 5), (2, 4, 5, 3), (1, 7, 0), (4, 12), (4, 13),
+    (2, 6, 2, 6), (2, 4, 3, 4), (2, 1, 5, 4), (2, 5, 0, 1), (1, 5, 1), (2, 1, 0, 6), (2, 4, 1, 3), (2, 0, 4, 3),
+    (1, 3, 3), (2, 5, 2, 3), (2, 2, 5, 6), (2, 0, 1, 4), (2, 4, 2, 5), (2, 4, 3, 1), (2, 6, 1, 6), (2, 0, 4, 0),
+    (2, 6, 1, 1), (4, 14), (2, 1, 4, 2), (4, 15), (4, 16), (2, 2, 4, 5), (2, 4, 0, 5), (4, 17),
+    (2, 6, 5, 3), (2, 3, 1, 6), (2, 3, 1, 1), (2, 7, 0, 0), (2, 0, 3, 5), (2, 1, 2, 6), (2, 2, 4, 0), (2, 3, 0, 5),
+    (2, 6, 0, 4), (2, 6, 4, 2), (1, 7, 1), (2, 2, 1, 1), (2, 3, 2, 4), (4, 18), (2, 2, 3, 1), (4, 19),
+    (1, 5, 3), (2, 1, 1, 6), (4, 20), (1, 5, 4), (2, 0, 5, 0), (2, 1, 3, 1), (2, 2, 0, 4), (2, 5, 1, 2),
+    (2, 4, 4, 1), (1, 7, 2), (2, 3, 3, 0), (2, 4, 5, 4), (4, 21), (2, 0, 5, 5), (1, 3, 5), (2, 5, 3, 0),
+    (2, 0, 3, 2), (2, 4, 4, 5), (2, 6, 3, 0), (2, 7, 0, 4), (4, 22), (2, 1, 4, 6), (2, 2, 1, 5), (4, 23),
+    (2, 6, 0, 5), (2, 5, 2, 6), (2, 7, 1, 2), (2, 5, 2, 4), (2, 7, 2, 3), (4, 24), (2, 4, 0, 3), (2, 3, 1, 0),
+    (2, 2, 5, 5), (4, 25), (2, 7, 0, 1), (2, 6, 5, 4), (2, 5, 4, 2), (2, 3, 3, 4), (4, 26), (2, 6, 1, 3),
+    (2, 5, 0, 5), (2, 1, 2, 5), (2, 3, 2, 6), (2, 5, 1, 6), (2, 2, 0, 2), (2, 5, 0, 4), (1, 5, 5), (2, 3, 5, 3),
+    (2, 3, 4, 2), (4, 27), (2, 1, 5, 6), (2, 4, 1, 5), (2, 2, 2, 1), (4, 28), (2, 3, 0, 6), (1, 7, 4),
+    (4, 29), (2, 5, 1, 1), (2, 7, 1, 6), (2, 7, 2, 4), (2, 2, 5, 2), (2, 2, 3, 5), (2, 3, 3, 1), (4, 30),
+    (2, 6, 4, 6), (2, 3, 1, 5), (2, 1, 2, 2), (2, 2, 3, 2), (2, 3, 2, 5), (2, 1, 1, 5), (2, 6, 2, 5), (1, 7, 3),
+    (2, 1, 2, 0), (2, 3, 0, 2), (2, 6, 1, 5), (2, 4, 3, 3), (2, 4, 5, 0), (2, 3, 1, 3), (4, 31), (4, 32),
+    (2, 4, 1, 4), (2, 1, 1, 0), (2, 4, 5, 6), (2, 5, 3, 1), (2, 5, 5, 3), (2, 0, 0, 6), (2, 7, 2, 6), (2, 6, 3, 4),
+    (2, 7, 3, 0), (2, 7, 4, 2), (2, 4, 3, 5), (2, 5, 4, 6), (2, 7, 1, 1), (2, 3, 5, 4), (4, 33), (4, 34),
+    (1, 7, 5), (4, 35), (2, 0, 0, 3), (2, 1, 3, 5), (4, 36), (2, 1, 2, 1), (2, 1, 5, 5), (2, 3, 2, 0),
+    (4, 37), (2, 5, 1, 5), (2, 0, 3, 3), (2, 4, 1, 1), (2, 4, 2, 0), (2, 6, 3, 1), (2, 1, 3, 4), (2, 7, 5, 3),
+    (2, 5, 2, 5), (2, 4, 3, 2), (4, 38), (2, 3, 4, 6), (2, 5, 4, 1), (2, 2, 3, 4), (2, 4, 4, 3), (2, 7, 0, 5),
+    (2, 2, 1, 4), (2, 2, 0, 6), (2, 2, 5, 0), (4, 39), (2, 0, 3, 6), (2, 5, 0, 2), (2, 5, 5, 4), (2, 7, 3, 1),
+    (2, 1, 4, 1), (4, 40), (2, 2, 2, 2), (2, 5, 0, 6), (2, 2, 1, 0), (2, 5, 5, 6), (2, 6, 1, 0), (2, 7, 0, 3),
+    (2, 2, 4, 4), (4, 41), (2, 4, 4, 0), (2, 6, 0, 3), (2, 1, 5, 1), (2, 1, 1, 3), (2, 7, 1, 3), (2, 1, 4, 3),
+    (2, 3, 3, 2), (4, 42), (2, 6, 0, 2), (2, 6, 2, 1), (2, 2, 0, 3), (2, 6, 5, 6), (2, 5, 2, 1), (2, 4, 2, 1),
+    (2, 5, 3, 5), (2, 3, 5, 6), (2, 3, 4, 1), (2, 7, 1, 5), (2, 3, 2, 1), (2, 3, 0, 3), (2, 0, 5, 1), (2, 0, 2, 1),
+    (2, 1, 1, 4), (2, 3, 1, 4), (2, 5, 2, 0), (2, 6, 2, 2), (2, 2, 2, 0), (2, 5, 1, 4), (2, 6, 0, 6), (2, 3, 3, 5),
+    (2, 7, 2, 5), (2, 5, 2, 2), (2, 1, 4, 5), (2, 1, 3, 2), (2, 5, 0, 3), (2, 6, 5, 5), (2, 4, 2, 2), (2, 2, 1, 3),
+    (2, 7, 5, 4), (4, 43), (2, 1, 5, 2), (4, 44), (2, 0, 2, 2), (2, 6, 1, 4), (2, 1, 3, 6), (2, 7, 5, 6),
+    (4, 45), (2, 3, 2, 2), (2, 7, 2, 0), (2, 4, 5, 2), (2, 7, 4, 6), (2, 6, 4, 5), (2, 1, 5, 0), (2, 4, 1, 0),
+    (2, 6, 2, 0), (2, 6, 4, 1), (2, 4, 0, 6), (2, 7, 2, 1), (2, 4, 5, 5), (2, 7, 1, 4), (2, 7, 0, 6), (2, 4, 0, 2),
+    (2, 3, 5, 0), (2, 5, 1, 3), (2, 7, 0, 2), (2, 6, 3, 5), (2, 7, 2, 2), (2, 5, 1, 0), (2, 5, 3, 4), (2, 7, 1, 0),
+    (2, 7, 3, 4), (4, 46), (2, 7, 4, 1), (2, 4, 3, 6), (2, 6, 3, 2), (4, 47), (4, 48), (2, 3, 4, 5),
+    (2, 3, 3, 3), (2, 3, 5, 5), (4, 49), (2, 5, 4, 5), (2, 3, 4, 3), (4, 50), (4, 51), (4, 52),
+    (2, 5, 5, 5), (2, 7, 3, 5), (4, 53), (2, 7, 5, 5), (2, 6, 3, 3), (2, 4, 5, 1), (2, 5, 5, 2), (2, 7, 4, 5),
+    (4, 54), (2, 1, 4, 4), (4, 55), (2, 7, 4, 0), (2, 3, 5, 1), (2, 2, 5, 1), (2, 7, 4, 3), (2, 3, 3, 6),
+    (2, 6, 5, 1), (2, 4, 4, 4), (2, 5, 4, 0), (2, 6, 4, 4), (2, 5, 4, 4), (2, 5, 3, 2), (2, 5, 5, 0), (2, 5, 5, 1),
+    (2, 3, 5, 2), (2, 1, 4, 0), (2, 7, 4, 4), (2, 7, 3, 6), (2, 7, 5, 2), (2, 7, 5, 1), (2, 7, 5, 0), (2, 6, 3, 6),
+    (2, 1, 3, 3), (2, 2, 3, 3), (2, 6, 4, 3), (2, 5, 3, 3), (2, 5, 4, 3), (2, 6, 4, 0), (2, 3, 4, 4), (2, 6, 5, 2),
+    (2, 3, 4, 0), (2, 5, 3, 6), (2, 7, 3, 3), (2, 7, 3, 2), (2, 0, 5, 2), (2, 6, 5, 0), (2, 2, 3, 6),
 )
 
 

time: 72.5 us -> 71.2 us (0.982)
    pallas_call x1, Pallas kernels: 63 us -> 62.2 us  [gather(): pl.pallas_call(gather_kernel, out_shape=(shape((DAYS, 2 * ASSET_BLOCK), j...]
where the time goes in v7:
time: 71.2 us; the launch traced here: 70.5 us
  Pallas kernels  69.7 us (98%)
  between operations  0.82 us (1%)
    pallas_call x1, Pallas kernels, gather(): pl.pallas_call(gather_kernel, out_shape=(shape((DAYS, 2 * ASSET_BLOCK), j...  62.2 us
    pallas_call x1, Pallas kernels, covariances(): pl.pallas_call(covariance_kernel, out_shape=(jax.ShapeDtypeStruct((FACTOR...  7.48 us

profile of v7, /device:TPU:5, one launch (start us, length us, event | category | flops | bytes accessed | tf_op | source)
XLA Modules:
  0.0 70.5 jit_solution(3161570975544467810)
XLA Ops:
  0.6 62.2 %gather.1 = (bf16[1536,2048]{1,0:T(8,128)(2,1)S(1)}, bf16[1536,256]{1,0:T(8,128)(2,1)S(1)}, bf16[256,1536]{1,0:T(8,128)(2,1)S(1)}, f32[256,256]{1,0:T(8,128)S(1)...) custom-call(bf16[192,256]{1,0:T(8,128)(2,1)} %f_hbm.1, bf16[192,1024]{1,0:T(8,128)(2,1)} %x_hbm.1), custom_call_target="tpu_custom_call" | custom-call | tf_op jit(solution)/shard_map/gather/pallas_call | solution.py:396
  62.9 7.5 %covariances.1 = (f32[256,1024]{1,0:T(8,128)}, f32[1024,2048]{1,0:T(8,128)}) custom-call(bf16[1536,2048]{1,0:T(8,128)(2,1)S(1)} %get-tuple-element.9.cols, bf16[1536,256]{1,0:T(8,128)(2,1)S(1)} %get-tuple-element.10.fall, bf16[256,1536]{1,0:T(8,128)(2,1)S(1)} %get-tuple-element.11.fall_t, f32[256,256]{1,0:T(8,128)S(1)} %get-tuple-element.12.inverse, ...), custom_call_target="tpu_custom_call" | custom-call | tf_op jit(solution)/shard_map/covariances/pallas_call | solution.py:450

commit v8 on v7

--- a/solution.py
+++ b/solution.py
@@ -32,64 +32,64 @@
 
 LINKS = ("h", "x+", "x-", "root")
 ORDER = (
-    (0, 3, 2), (0, 2, 4), (0, 3, 3), (0, 1, 2), (0, 2, 2), (0, 2, 1), (0, 1, 0), (0, 1, 1),
-    (0, 3, 1), (0, 2, 0), (0, 0, 0), (3, 0), (0, 3, 0), (0, 0, 2), (0, 3, 4), (2, 0, 2, 3),
-    (1, 4, 2), (0, 1, 3), (2, 0, 1, 2), (2, 0, 4, 2), (0, 1, 4), (1, 1, 0), (2, 0, 1, 6), (0, 2, 5),
-    (2, 0, 0, 0), (0, 0, 4), (2, 0, 2, 4), (3, 1), (1, 2, 4), (1, 4, 1), (2, 2, 4, 2), (1, 2, 2),
-    (1, 4, 0), (0, 0, 1), (3, 2), (1, 2, 0), (2, 0, 0, 1), (2, 1, 0, 0), (0, 1, 5), (1, 1, 2),
-    (0, 0, 3), (0, 3, 5), (2, 4, 2, 3), (2, 0, 4, 6), (1, 2, 1), (2, 4, 1, 2), (1, 4, 4), (1, 3, 0),
-    (1, 4, 3), (2, 0, 3, 0), (1, 5, 0), (2, 0, 4, 1), (2, 2, 2, 3), (0, 0, 5), (3, 3), (0, 2, 3),
-    (2, 2, 0, 0), (2, 3, 0, 0), (2, 1, 2, 3), (1, 1, 1), (1, 2, 5), (1, 6, 1), (2, 1, 0, 1), (2, 4, 2, 4),
-    (1, 1, 4), (1, 6, 2), (2, 4, 0, 0), (2, 2, 2, 4), (2, 0, 2, 6), (1, 1, 3), (2, 0, 5, 3), (2, 2, 1, 2),
-    (2, 0, 0, 2), (2, 0, 4, 5), (2, 4, 3, 0), (2, 2, 0, 1), (1, 6, 0), (2, 1, 1, 2), (2, 0, 1, 1), (3, 4),
-    (4, 0), (2, 6, 0, 0), (2, 1, 2, 4), (2, 4, 4, 2), (2, 0, 4, 4), (2, 6, 1, 2), (2, 1, 0, 4), (1, 2, 3),
-    (2, 2, 5, 3), (2, 0, 3, 1), (2, 3, 0, 1), (2, 0, 2, 0), (1, 1, 5), (4, 1), (2, 2, 4, 6), (4, 2),
-    (2, 0, 3, 4), (2, 5, 0, 0), (2, 6, 2, 3), (1, 3, 1), (1, 3, 2), (2, 1, 3, 0), (2, 0, 2, 5), (1, 4, 5),
-    (4, 3), (4, 4), (2, 4, 0, 1), (2, 2, 2, 5), (2, 0, 1, 5), (2, 4, 0, 4), (2, 2, 1, 6), (1, 5, 2),
-    (2, 2, 4, 1), (2, 0, 5, 6), (2, 0, 0, 5), (4, 5), (2, 0, 0, 4), (2, 0, 5, 4), (2, 1, 5, 3), (4, 6),
-    (2, 2, 5, 4), (2, 1, 1, 1), (2, 4, 1, 6), (2, 1, 0, 5), (2, 2, 0, 5), (2, 4, 2, 6), (2, 2, 3, 0), (1, 6, 4),
-    (4, 7), (2, 0, 1, 0), (4, 8), (1, 3, 4), (2, 2, 2, 6), (2, 1, 0, 2), (2, 2, 4, 3), (1, 6, 3),
-    (2, 6, 0, 1), (2, 3, 2, 3), (2, 3, 0, 4), (4, 9), (2, 6, 2, 4), (4, 10), (2, 0, 1, 3), (2, 1, 0, 3),
-    (2, 4, 4, 6), (4, 11), (2, 3, 1, 2), (1, 6, 5), (2, 4, 5, 3), (1, 7, 0), (4, 12), (4, 13),
-    (2, 6, 2, 6), (2, 4, 3, 4), (2, 1, 5, 4), (2, 5, 0, 1), (1, 5, 1), (2, 1, 0, 6), (2, 4, 1, 3), (2, 0, 4, 3),
-    (1, 3, 3), (2, 5, 2, 3), (2, 2, 5, 6), (2, 0, 1, 4), (2, 4, 2, 5), (2, 4, 3, 1), (2, 6, 1, 6), (2, 0, 4, 0),
-    (2, 6, 1, 1), (4, 14), (2, 1, 4, 2), (4, 15), (4, 16), (2, 2, 4, 5), (2, 4, 0, 5), (4, 17),
-    (2, 6, 5, 3), (2, 3, 1, 6), (2, 3, 1, 1), (2, 7, 0, 0), (2, 0, 3, 5), (2, 1, 2, 6), (2, 2, 4, 0), (2, 3, 0, 5),
-    (2, 6, 0, 4), (2, 6, 4, 2), (1, 7, 1), (2, 2, 1, 1), (2, 3, 2, 4), (4, 18), (2, 2, 3, 1), (4, 19),
-    (1, 5, 3), (2, 1, 1, 6), (4, 20), (1, 5, 4), (2, 0, 5, 0), (2, 1, 3, 1), (2, 2, 0, 4), (2, 5, 1, 2),
-    (2, 4, 4, 1), (1, 7, 2), (2, 3, 3, 0), (2, 4, 5, 4), (4, 21), (2, 0, 5, 5), (1, 3, 5), (2, 5, 3, 0),
-    (2, 0, 3, 2), (2, 4, 4, 5), (2, 6, 3, 0), (2, 7, 0, 4), (4, 22), (2, 1, 4, 6), (2, 2, 1, 5), (4, 23),
-    (2, 6, 0, 5), (2, 5, 2, 6), (2, 7, 1, 2), (2, 5, 2, 4), (2, 7, 2, 3), (4, 24), (2, 4, 0, 3), (2, 3, 1, 0),
-    (2, 2, 5, 5), (4, 25), (2, 7, 0, 1), (2, 6, 5, 4), (2, 5, 4, 2), (2, 3, 3, 4), (4, 26), (2, 6, 1, 3),
-    (2, 5, 0, 5), (2, 1, 2, 5), (2, 3, 2, 6), (2, 5, 1, 6), (2, 2, 0, 2), (2, 5, 0, 4), (1, 5, 5), (2, 3, 5, 3),
-    (2, 3, 4, 2), (4, 27), (2, 1, 5, 6), (2, 4, 1, 5), (2, 2, 2, 1), (4, 28), (2, 3, 0, 6), (1, 7, 4),
-    (4, 29), (2, 5, 1, 1), (2, 7, 1, 6), (2, 7, 2, 4), (2, 2, 5, 2), (2, 2, 3, 5), (2, 3, 3, 1), (4, 30),
-    (2, 6, 4, 6), (2, 3, 1, 5), (2, 1, 2, 2), (2, 2, 3, 2), (2, 3, 2, 5), (2, 1, 1, 5), (2, 6, 2, 5), (1, 7, 3),
-    (2, 1, 2, 0), (2, 3, 0, 2), (2, 6, 1, 5), (2, 4, 3, 3), (2, 4, 5, 0), (2, 3, 1, 3), (4, 31), (4, 32),
-    (2, 4, 1, 4), (2, 1, 1, 0), (2, 4, 5, 6), (2, 5, 3, 1), (2, 5, 5, 3), (2, 0, 0, 6), (2, 7, 2, 6), (2, 6, 3, 4),
-    (2, 7, 3, 0), (2, 7, 4, 2), (2, 4, 3, 5), (2, 5, 4, 6), (2, 7, 1, 1), (2, 3, 5, 4), (4, 33), (4, 34),
-    (1, 7, 5), (4, 35), (2, 0, 0, 3), (2, 1, 3, 5), (4, 36), (2, 1, 2, 1), (2, 1, 5, 5), (2, 3, 2, 0),
-    (4, 37), (2, 5, 1, 5), (2, 0, 3, 3), (2, 4, 1, 1), (2, 4, 2, 0), (2, 6, 3, 1), (2, 1, 3, 4), (2, 7, 5, 3),
-    (2, 5, 2, 5), (2, 4, 3, 2), (4, 38), (2, 3, 4, 6), (2, 5, 4, 1), (2, 2, 3, 4), (2, 4, 4, 3), (2, 7, 0, 5),
-    (2, 2, 1, 4), (2, 2, 0, 6), (2, 2, 5, 0), (4, 39), (2, 0, 3, 6), (2, 5, 0, 2), (2, 5, 5, 4), (2, 7, 3, 1),
-    (2, 1, 4, 1), (4, 40), (2, 2, 2, 2), (2, 5, 0, 6), (2, 2, 1, 0), (2, 5, 5, 6), (2, 6, 1, 0), (2, 7, 0, 3),
-    (2, 2, 4, 4), (4, 41), (2, 4, 4, 0), (2, 6, 0, 3), (2, 1, 5, 1), (2, 1, 1, 3), (2, 7, 1, 3), (2, 1, 4, 3),
-    (2, 3, 3, 2), (4, 42), (2, 6, 0, 2), (2, 6, 2, 1), (2, 2, 0, 3), (2, 6, 5, 6), (2, 5, 2, 1), (2, 4, 2, 1),
-    (2, 5, 3, 5), (2, 3, 5, 6), (2, 3, 4, 1), (2, 7, 1, 5), (2, 3, 2, 1), (2, 3, 0, 3), (2, 0, 5, 1), (2, 0, 2, 1),
-    (2, 1, 1, 4), (2, 3, 1, 4), (2, 5, 2, 0), (2, 6, 2, 2), (2, 2, 2, 0), (2, 5, 1, 4), (2, 6, 0, 6), (2, 3, 3, 5),
-    (2, 7, 2, 5), (2, 5, 2, 2), (2, 1, 4, 5), (2, 1, 3, 2), (2, 5, 0, 3), (2, 6, 5, 5), (2, 4, 2, 2), (2, 2, 1, 3),
-    (2, 7, 5, 4), (4, 43), (2, 1, 5, 2), (4, 44), (2, 0, 2, 2), (2, 6, 1, 4), (2, 1, 3, 6), (2, 7, 5, 6),
-    (4, 45), (2, 3, 2, 2), (2, 7, 2, 0), (2, 4, 5, 2), (2, 7, 4, 6), (2, 6, 4, 5), (2, 1, 5, 0), (2, 4, 1, 0),
-    (2, 6, 2, 0), (2, 6, 4, 1), (2, 4, 0, 6), (2, 7, 2, 1), (2, 4, 5, 5), (2, 7, 1, 4), (2, 7, 0, 6), (2, 4, 0, 2),
-    (2, 3, 5, 0), (2, 5, 1, 3), (2, 7, 0, 2), (2, 6, 3, 5), (2, 7, 2, 2), (2, 5, 1, 0), (2, 5, 3, 4), (2, 7, 1, 0),
-    (2, 7, 3, 4), (4, 46), (2, 7, 4, 1), (2, 4, 3, 6), (2, 6, 3, 2), (4, 47), (4, 48), (2, 3, 4, 5),
-    (2, 3, 3, 3), (2, 3, 5, 5), (4, 49), (2, 5, 4, 5), (2, 3, 4, 3), (4, 50), (4, 51), (4, 52),
-    (2, 5, 5, 5), (2, 7, 3, 5), (4, 53), (2, 7, 5, 5), (2, 6, 3, 3), (2, 4, 5, 1), (2, 5, 5, 2), (2, 7, 4, 5),
-    (4, 54), (2, 1, 4, 4), (4, 55), (2, 7, 4, 0), (2, 3, 5, 1), (2, 2, 5, 1), (2, 7, 4, 3), (2, 3, 3, 6),
-    (2, 6, 5, 1), (2, 4, 4, 4), (2, 5, 4, 0), (2, 6, 4, 4), (2, 5, 4, 4), (2, 5, 3, 2), (2, 5, 5, 0), (2, 5, 5, 1),
-    (2, 3, 5, 2), (2, 1, 4, 0), (2, 7, 4, 4), (2, 7, 3, 6), (2, 7, 5, 2), (2, 7, 5, 1), (2, 7, 5, 0), (2, 6, 3, 6),
-    (2, 1, 3, 3), (2, 2, 3, 3), (2, 6, 4, 3), (2, 5, 3, 3), (2, 5, 4, 3), (2, 6, 4, 0), (2, 3, 4, 4), (2, 6, 5, 2),
-    (2, 3, 4, 0), (2, 5, 3, 6), (2, 7, 3, 3), (2, 7, 3, 2), (2, 0, 5, 2), (2, 6, 5, 0), (2, 2, 3, 6),
+    (3, 0), (0, 0, 2), (0, 3, 4), (0, 3, 3), (0, 1, 2), (0, 3, 2), (0, 1, 3), (0, 2, 2),
+    (0, 3, 1), (0, 2, 0), (0, 0, 0), (0, 1, 0), (2, 0, 3, 0), (0, 2, 4), (0, 1, 1), (2, 0, 2, 3),
+    (0, 3, 0), (1, 4, 2), (0, 0, 3), (3, 1), (0, 2, 1), (0, 0, 4), (2, 0, 0, 0), (1, 1, 0),
+    (0, 1, 4), (2, 0, 1, 2), (0, 0, 1), (2, 4, 2, 3), (0, 2, 5), (2, 0, 0, 1), (1, 2, 4), (3, 2),
+    (0, 2, 3), (1, 4, 0), (1, 4, 1), (2, 0, 3, 1), (1, 2, 0), (3, 3), (2, 1, 0, 0), (2, 0, 2, 4),
+    (1, 2, 1), (2, 0, 2, 6), (2, 0, 4, 2), (1, 2, 2), (2, 2, 4, 2), (0, 3, 5), (2, 1, 0, 1), (1, 4, 3),
+    (2, 4, 0, 0), (0, 1, 5), (1, 3, 0), (1, 4, 4), (0, 0, 5), (1, 1, 2), (2, 2, 0, 0), (2, 4, 3, 0),
+    (2, 2, 2, 3), (2, 2, 4, 1), (1, 5, 0), (2, 3, 0, 0), (2, 4, 2, 4), (2, 4, 0, 1), (2, 0, 0, 5), (2, 2, 1, 2),
+    (1, 1, 1), (2, 4, 1, 2), (2, 0, 4, 6), (1, 1, 3), (1, 6, 0), (2, 0, 5, 3), (1, 2, 5), (3, 4),
+    (1, 6, 1), (2, 0, 1, 6), (1, 6, 2), (2, 5, 0, 0), (2, 4, 0, 4), (4, 0), (2, 2, 1, 6), (2, 1, 1, 2),
+    (2, 4, 2, 5), (2, 0, 5, 4), (2, 1, 2, 3), (2, 2, 1, 1), (2, 4, 4, 2), (1, 1, 4), (2, 0, 0, 4), (4, 1),
+    (2, 6, 0, 0), (4, 2), (2, 4, 3, 1), (2, 0, 4, 5), (2, 2, 0, 4), (2, 2, 2, 4), (4, 3), (1, 1, 5),
+    (4, 4), (1, 6, 3), (1, 3, 1), (2, 4, 3, 4), (2, 6, 1, 2), (2, 4, 0, 5), (2, 1, 3, 0), (2, 1, 2, 4),
+    (2, 2, 5, 3), (2, 1, 0, 4), (2, 0, 4, 1), (2, 2, 0, 1), (1, 2, 3), (4, 5), (2, 0, 3, 5), (2, 6, 2, 3),
+    (2, 1, 0, 5), (2, 1, 5, 3), (2, 2, 4, 6), (4, 6), (2, 1, 2, 6), (1, 3, 2), (1, 4, 5), (4, 7),
+    (2, 0, 1, 1), (2, 1, 1, 6), (2, 3, 1, 2), (4, 8), (2, 0, 1, 5), (1, 6, 4), (2, 3, 0, 1), (2, 3, 2, 3),
+    (2, 4, 2, 6), (2, 2, 4, 0), (4, 9), (2, 2, 5, 4), (2, 2, 1, 3), (2, 4, 3, 5), (4, 10), (2, 0, 1, 3),
+    (2, 5, 0, 4), (2, 2, 1, 5), (2, 0, 2, 5), (2, 6, 0, 4), (2, 4, 1, 6), (4, 11), (2, 4, 5, 3), (2, 1, 4, 2),
+    (1, 7, 0), (4, 12), (2, 2, 0, 5), (1, 5, 2), (2, 2, 3, 0), (2, 0, 4, 0), (2, 1, 2, 2), (2, 6, 0, 1),
+    (2, 1, 1, 1), (2, 6, 2, 4), (4, 13), (1, 6, 5), (2, 0, 5, 5), (2, 6, 1, 6), (2, 4, 4, 6), (2, 2, 0, 2),
+    (2, 4, 2, 0), (2, 6, 4, 2), (2, 2, 2, 5), (2, 1, 3, 1), (4, 14), (1, 5, 1), (2, 5, 2, 3), (4, 15),
+    (2, 1, 5, 4), (1, 3, 3), (2, 7, 0, 0), (2, 2, 2, 6), (4, 16), (2, 3, 1, 6), (2, 2, 4, 5), (2, 5, 1, 2),
+    (4, 17), (2, 3, 0, 4), (2, 3, 2, 4), (2, 5, 0, 1), (2, 6, 3, 0), (2, 0, 0, 6), (1, 7, 1), (1, 3, 4),
+    (1, 5, 3), (2, 6, 5, 3), (2, 0, 5, 6), (4, 18), (4, 19), (2, 1, 4, 6), (2, 0, 2, 1), (2, 3, 1, 1),
+    (4, 20), (2, 4, 2, 2), (1, 7, 2), (2, 4, 1, 3), (2, 4, 5, 4), (2, 3, 2, 6), (4, 21), (2, 3, 3, 0),
+    (2, 6, 2, 6), (2, 7, 1, 2), (2, 7, 2, 3), (2, 7, 0, 4), (2, 6, 0, 5), (2, 2, 3, 1), (2, 0, 0, 3), (1, 5, 4),
+    (2, 4, 4, 3), (2, 1, 1, 5), (2, 6, 0, 3), (1, 3, 5), (2, 5, 2, 4), (2, 2, 4, 4), (2, 2, 5, 5), (4, 22),
+    (2, 2, 5, 6), (4, 23), (4, 24), (2, 1, 2, 5), (2, 2, 4, 3), (2, 5, 4, 2), (2, 0, 5, 0), (2, 3, 4, 2),
+    (2, 7, 0, 1), (2, 4, 2, 1), (2, 4, 0, 3), (2, 6, 1, 1), (2, 3, 0, 5), (2, 1, 0, 3), (2, 5, 3, 0), (2, 5, 1, 1),
+    (2, 0, 1, 0), (2, 4, 1, 5), (2, 6, 2, 5), (2, 3, 5, 3), (2, 6, 4, 6), (2, 2, 0, 6), (2, 6, 5, 4), (2, 5, 1, 6),
+    (2, 1, 3, 2), (2, 2, 1, 4), (4, 25), (2, 4, 3, 3), (4, 26), (4, 27), (2, 0, 4, 3), (2, 1, 1, 0),
+    (2, 4, 4, 1), (2, 6, 0, 6), (2, 3, 2, 0), (4, 28), (1, 5, 5), (2, 3, 0, 3), (2, 1, 5, 5), (2, 3, 1, 5),
+    (2, 3, 3, 1), (2, 7, 2, 4), (2, 2, 3, 2), (2, 6, 1, 5), (4, 29), (2, 6, 3, 4), (2, 3, 0, 2), (2, 5, 3, 1),
+    (2, 3, 3, 4), (2, 1, 3, 5), (2, 1, 1, 4), (2, 7, 1, 1), (2, 5, 5, 3), (2, 5, 0, 5), (2, 4, 1, 1), (2, 1, 4, 3),
+    (1, 7, 4), (2, 0, 4, 4), (2, 7, 4, 2), (2, 7, 1, 6), (1, 7, 3), (4, 30), (2, 6, 3, 1), (2, 2, 3, 5),
+    (2, 7, 3, 0), (2, 1, 5, 6), (2, 5, 0, 3), (2, 1, 4, 1), (4, 31), (2, 5, 0, 2), (2, 1, 1, 3), (2, 6, 1, 0),
+    (2, 4, 4, 5), (2, 0, 5, 1), (4, 32), (4, 33), (4, 34), (2, 6, 2, 1), (2, 6, 1, 3), (2, 2, 2, 1),
+    (2, 5, 1, 3), (2, 3, 5, 4), (2, 7, 2, 6), (4, 35), (2, 5, 4, 1), (2, 7, 5, 3), (2, 0, 3, 4), (2, 5, 2, 6),
+    (4, 36), (2, 1, 5, 1), (2, 3, 2, 5), (2, 5, 2, 5), (2, 0, 2, 0), (2, 4, 1, 4), (2, 5, 4, 6), (4, 37),
+    (1, 7, 5), (4, 38), (2, 5, 5, 4), (2, 5, 1, 5), (2, 7, 0, 5), (2, 4, 5, 0), (2, 5, 3, 4), (2, 0, 3, 6),
+    (2, 7, 3, 1), (2, 6, 4, 3), (2, 3, 4, 6), (2, 4, 0, 2), (4, 39), (4, 40), (2, 1, 5, 2), (2, 7, 2, 0),
+    (2, 0, 1, 4), (2, 5, 5, 6), (2, 1, 3, 4), (2, 2, 2, 0), (2, 7, 0, 2), (2, 7, 3, 4), (2, 3, 4, 1), (2, 4, 4, 0),
+    (4, 41), (2, 7, 2, 5), (2, 1, 5, 0), (2, 7, 1, 0), (2, 2, 2, 2), (2, 4, 5, 6), (2, 5, 0, 6), (2, 7, 1, 5),
+    (4, 42), (2, 3, 1, 0), (2, 3, 3, 3), (2, 6, 5, 5), (2, 0, 2, 2), (4, 43), (2, 6, 4, 5), (2, 7, 5, 4),
+    (4, 44), (4, 45), (2, 5, 1, 0), (2, 3, 2, 2), (2, 0, 3, 3), (2, 3, 5, 6), (2, 5, 2, 0), (2, 7, 4, 1),
+    (2, 6, 4, 1), (2, 0, 0, 2), (2, 7, 4, 6), (2, 1, 2, 1), (2, 7, 2, 2), (2, 6, 2, 2), (2, 7, 1, 4), (2, 4, 3, 6),
+    (2, 2, 0, 3), (2, 5, 1, 4), (2, 3, 1, 4), (2, 6, 3, 2), (2, 5, 4, 3), (2, 5, 3, 5), (2, 7, 5, 6), (2, 0, 3, 2),
+    (2, 6, 3, 3), (2, 6, 5, 6), (2, 5, 2, 1), (2, 1, 2, 0), (2, 2, 3, 4), (2, 7, 2, 1), (2, 2, 1, 0), (2, 4, 1, 0),
+    (2, 7, 0, 3), (2, 1, 4, 5), (2, 7, 0, 6), (2, 6, 1, 4), (2, 3, 1, 3), (2, 3, 2, 1), (2, 3, 3, 5), (2, 6, 0, 2),
+    (2, 1, 0, 2), (2, 5, 2, 2), (2, 1, 0, 6), (2, 6, 2, 0), (2, 3, 3, 2), (2, 3, 0, 6), (2, 4, 4, 4), (2, 7, 1, 3),
+    (2, 6, 3, 5), (2, 2, 5, 0), (2, 3, 4, 3), (2, 4, 0, 6), (4, 46), (2, 4, 5, 5), (4, 47), (4, 48),
+    (4, 49), (4, 50), (2, 2, 5, 2), (2, 6, 4, 4), (2, 3, 5, 5), (2, 3, 4, 5), (2, 6, 5, 1), (4, 51),
+    (2, 5, 5, 5), (2, 5, 4, 5), (2, 5, 3, 3), (4, 52), (2, 7, 3, 5), (4, 53), (2, 7, 5, 5), (2, 7, 4, 5),
+    (2, 2, 5, 1), (2, 7, 3, 2), (2, 6, 5, 0), (4, 54), (4, 55), (2, 7, 3, 3), (2, 3, 4, 0), (2, 5, 3, 6),
+    (2, 4, 3, 2), (2, 5, 5, 2), (2, 6, 3, 6), (2, 3, 4, 4), (2, 4, 5, 2), (2, 0, 5, 2), (2, 1, 4, 4), (2, 5, 4, 4),
+    (2, 2, 3, 3), (2, 7, 5, 2), (2, 5, 5, 1), (2, 3, 5, 0), (2, 2, 3, 6), (2, 6, 4, 0), (2, 7, 4, 4), (2, 3, 3, 6),
+    (2, 1, 3, 3), (2, 1, 3, 6), (2, 7, 4, 0), (2, 7, 4, 3), (2, 5, 3, 2), (2, 7, 3, 6), (2, 4, 5, 1), (2, 3, 5, 1),
+    (2, 5, 4, 0), (2, 3, 5, 2), (2, 6, 5, 2), (2, 7, 5, 1), (2, 5, 5, 0), (2, 7, 5, 0), (2, 1, 4, 0),
 )
 
 

time: 71.2 us -> 71.4 us (level)
  the two profiles are of different devices: /device:TPU:5 before, /device:TPU:16 now
where the time goes in v8:
time: 71.4 us; the launch traced here: 71.3 us
  Pallas kernels  70.5 us (99%)
  between operations  0.82 us (1%)
    pallas_call x1, Pallas kernels, gather(): pl.pallas_call(gather_kernel, out_shape=(shape((DAYS, 2 * ASSET_BLOCK), j...  63 us
    pallas_call x1, Pallas kernels, covariances(): pl.pallas_call(covariance_kernel, out_shape=(jax.ShapeDtypeStruct((FACTOR...  7.48 us

profile of v8, /device:TPU:16, one launch (start us, length us, event | category | flops | bytes accessed | tf_op | source)
XLA Modules:
  0.0 71.3 jit_solution(7979856825052060707)
XLA Ops:
  0.6 63.0 %gather.1 = (bf16[1536,2048]{1,0:T(8,128)(2,1)S(1)}, bf16[1536,256]{1,0:T(8,128)(2,1)S(1)}, bf16[256,1536]{1,0:T(8,128)(2,1)S(1)}, f32[256,256]{1,0:T(8,128)S(1)...) custom-call(bf16[192,256]{1,0:T(8,128)(2,1)} %f_hbm.1, bf16[192,1024]{1,0:T(8,128)(2,1)} %x_hbm.1), custom_call_target="tpu_custom_call" | custom-call | tf_op jit(solution)/shard_map/gather/pallas_call | solution.py:396
  63.7 7.5 %covariances.1 = (f32[256,1024]{1,0:T(8,128)}, f32[1024,2048]{1,0:T(8,128)}) custom-call(bf16[1536,2048]{1,0:T(8,128)(2,1)S(1)} %get-tuple-element.9.cols, bf16[1536,256]{1,0:T(8,128)(2,1)S(1)} %get-tuple-element.10.fall, bf16[256,1536]{1,0:T(8,128)(2,1)S(1)} %get-tuple-element.11.fall_t, f32[256,256]{1,0:T(8,128)S(1)} %get-tuple-element.12.inverse, ...), custom_call_target="tpu_custom_call" | custom-call | tf_op jit(solution)/shard_map/covariances/pallas_call | solution.py:450
